TPU v7x, 32 devices: a whole 2x2x4 slice. The times are simulated.
32 devices in a mesh: blk: 16 (over z, y, core), shard: 2 (over x).
Axes of the slice: x: 2, y: 2, z: 4, core: 2. Of those that a mesh axis runs over, the one named last changes fastest.
Arguments:
- cut_acts: bfloat16 [8192, 1024], P('blk'), may hold values from -6 to 6
- upstream: bfloat16 [8192, 1024], P('blk', 'shard'), may hold values from -1 to 1
- weights: bfloat16 [16, 1024, 1024], P('blk', None, 'shard'), may hold values from -0.59765625 to 0.59765625
- moment_one: float32 [16, 1024, 1024], P('blk', None, 'shard'), may hold values from -6 to 6
- moment_two: float32 [16, 1024, 1024], P('blk', None, 'shard'), may hold values from 1 to 8
Outputs:
- new_weights: bfloat16 [16, 1024, 1024], P('blk', None, 'shard')
- new_moment_one: float32 [16, 1024, 1024], P('blk', None, 'shard')
- new_moment_two: float32 [16, 1024, 1024], P('blk', None, 'shard')
- cut_grads: bfloat16 [3, 8192, 1024], P(None, ('blk', 'shard'))
All inputs are finite; a program needn't handle non-finite values.
Results may differ from a plain program's by a relative error of at most 0.0074.
Values may be sent and summed in bfloat16 or wider, within the bound.
No kernel may reach another device: no remote copies, remote signals or barrier semaphores. Data moves between devices by JAX's collectives and lax.ppermute only.
A program may use at most 64 MiB of HBM per device.

v0:
```python
import jax
import jax.numpy as jnp
from jax import lax
from jax.sharding import PartitionSpec as P

HOPS = 3


def passed_along(shard, axis, by):
    devices = lax.axis_size(axis)
    return lax.ppermute(shard, axis, [(i, (i + by) % devices) for i in range(devices)])


def gelu_slope(values):
    inner = 0.7978845608 * (values + 0.044715 * values * values * values)
    tanh_part = jnp.tanh(inner)
    return 0.5 * (1.0 + tanh_part) + 0.5 * values * (1.0 - tanh_part * tanh_part) * 0.7978845608 * (
        1.0 + 0.134145 * values * values
    )


def train_local(kernel, first, second, inputs, grad_out):
    preact = jnp.dot(inputs, kernel, preferred_element_type=jnp.float32)
    slopes = (grad_out.astype(jnp.float32) * gelu_slope(preact)).astype(jnp.bfloat16)
    gradient = lax.dot_general(
        inputs, slopes, (((0,), (0,)), ((), ())), preferred_element_type=jnp.float32
    )
    returned = lax.psum_scatter(
        lax.dot_general(
            slopes, kernel, (((1,), (1,)), ((), ())), preferred_element_type=jnp.float32
        ),
        "shard",
        scatter_dimension=0,
        tiled=True,
    ).astype(jnp.bfloat16)
    first = 0.9 * first + 0.1 * gradient
    second = 0.95 * second + 0.05 * gradient * gradient
    kernel = (kernel.astype(jnp.float32) - 0.01 * first / (jnp.sqrt(second) + 1e-08)).astype(
        jnp.bfloat16
    )
    return (kernel, first, second, returned)


def shards(cut_acts, upstream, weights, moment_one, moment_two):
    kernel = weights[0]
    first = moment_one[0]
    second = moment_two[0]
    returned_all = []
    for hop_index in range(HOPS):
        if hop_index == 0:
            inputs, grad_out = (cut_acts, upstream)
        else:
            inputs, grad_out = passed_along((cut_acts, upstream), "blk", -hop_index)
        kernel, first, second, returned = train_local(kernel, first, second, inputs, grad_out)
        if hop_index > 0:
            returned = passed_along(returned, "blk", hop_index)
        returned_all.append(returned)
    kernel = passed_along(kernel, "blk", HOPS)
    first, second = passed_along((first, second), "blk", HOPS)
    return (kernel[None], first[None], second[None], jnp.stack(returned_all))


def solution(mesh):
    placed = (
        P("blk", None),
        P("blk", "shard"),
        P("blk", None, "shard"),
        P("blk", None, "shard"),
        P("blk", None, "shard"),
    )
    return jax.shard_map(
        shards,
        mesh=mesh,
        in_specs=placed,
        out_specs=(
            P("blk", None, "shard"),
            P("blk", None, "shard"),
            P("blk", None, "shard"),
            P(None, ("blk", "shard"), None),
        ),
        check_vma=False,
    )
```

profile of v0, /device:TPU:0, one launch (start us, length us, event | category | flops | bytes accessed | tf_op | source)
XLA Modules:
  0.0 232.5 jit_solution(12929137950522671110)
XLA Ops:
  7.2 5.5 %collective-permute-start.1 = (bf16[512,1024]{1,0:T(8,128)(2,1)}, bf16[512,1024]{1,0:T(8,128)(2,1)}, u32[]{:S(2)}, u32[]{:S(2)}) collective-permute-start(bf16[512,1024]{1,0:T(8,128)(2,1)} %param.5), channel_id=1, source_target_pairs={{0,30},{2,0},{4,2},{6,4},{8,6},{10,8},{12,10},{14,12},{16,14},{18,... | collective-permute-start | bytes 3145736 | tf_op jit(solution)/shard_map/ppermute | solution.py:11
  13.6 1.4 collective-permute-start.2
  15.1 2.3 copy.9
  17.3 1.8 copy.10
  19.1 3.0 %copy.11 = f32[1,1024,512]{1,2,0:T(8,128)} copy(f32[1,1024,512]{2,1,0:T(8,128)} %param.9) | data formatting | bytes 4194304 | tf_op args[4]
  22.1 2.8 %fusion.12 = bf16[512,512]{1,0:T(8,128)(2,1)S(1)} fusion(bf16[512,1024]{1,0:T(8,128)(2,1)} %param.5, bf16[1,1024,512]{2,1,0:T(8,128)(2,1)S(1)} %copy-done, bf16[512,512]{1,0:T(8,128)(2,1)} %param.6), kind=kOutput, calls=%fused_computation.30 | convolution fusion | flops 542113792 | bytes 3145728 | tf_op jit(solution)/shard_map/dot_general | solution.py:23
  25.4 1.9 subtract_convert_fusion.2
  27.4 9.2 %collective-permute-done.1 = bf16[512,1024]{1,0:T(8,128)(2,1)} collective-permute-done((bf16[512,1024]{1,0:T(8,128)(2,1)}, bf16[512,1024]{1,0:T(8,128)(2,1)}, u32[]{:S(2)}, u32[]{:S(2)}) %collective-permute-start.1) | collective-permute-done | bytes 1048608 | tf_op jit(solution)/shard_map/ppermute | solution.py:11
  36.5 2.0 convolution_bitcast_fusion.1
  38.5 20.6 %collective-permute-done = bf16[512,512]{1,0:T(8,128)(2,1)} collective-permute-done((bf16[512,512]{1,0:T(8,128)(2,1)}, bf16[512,512]{1,0:T(8,128)(2,1)}, u32[]{:S(2)}, u32[]{:S(2)}) %collective-permute-start) | collective-permute-done | bytes 524320 | tf_op jit(solution)/shard_map/ppermute | solution.py:11
  59.1 5.5 %subtract_convert_fusion.1 = (bf16[1024,512]{0,1:T(8,128)(2,1)S(1)}, f32[512,1024]{1,0:T(8,128)}) fusion(bf16[1024,512]{0,1:T(8,128)(2,1)S(1)} %get-tuple-element.11, f32[512,1024]{1,0:T(8,128)S(1)} %get-tuple-element.12, f32[1,1024,512]{1,2,0:T(8,128)S(1)} %copy-done.3, f32[1,1024,512]{1,2,0:T(8,128)S(1)} %copy-done.2, ...), kind=kOutput, calls=%fused_computation.13 | convolution fusion | flops 552599552 | bytes 13107200 | tf_op jit(solution)/shard_map/dot_general | solution.py:25
  64.6 2.3 %convolution_bitcast_fusion = f32[512,512]{1,0:T(8,128)S(1)} fusion(bf16[1024,512]{0,1:T(8,128)(2,1)S(1)} %get-tuple-element.13, bf16[512,1024]{1,0:T(8,128)(2,1)} %collective-permute-done.3), kind=kOutput, calls=%fused_computation.22 | convolution fusion | flops 536870912 | bytes 3145728 | tf_op jit(solution)/shard_map/dot_general | solution.py:23
  67.9 3.6 %fusion.33 = f32[512,1024]{1,0:T(8,128)} fusion(bf16[1024,512]{0,1:T(8,128)(2,1)S(1)} %get-tuple-element.13, f32[512,512]{1,0:T(8,128)S(1)} %convolution_bitcast_fusion, bf16[512,512]{1,0:T(8,128)(2,1)} %collective-permute-done.2), kind=kOutput, calls=%fused_computation.50 | convolution fusion | flops 542113792 | bytes 4718592 | tf_op jit(solution)/shard_map/dot_general | solution.py:29
  71.6 4.2 %fusion.37 = f32[512,1024]{1,0:T(8,128)} fusion(bf16[1024,512]{0,1:T(8,128)(2,1)} %copy-done.10, f32[512,512]{1,0:T(8,128)} %copy-done.11, bf16[512,512]{1,0:T(8,128)(2,1)} %collective-permute-done), kind=kOutput, calls=%fused_computation.52 | convolution fusion | flops 542113792 | bytes 4718592 | tf_op jit(solution)/shard_map/dot_general | solution.py:29
  76.1 3.1 %fusion.27 = f32[512,1024]{1,0:T(8,128)} fusion(bf16[512,512]{1,0:T(8,128)(2,1)} %copy-done.5, bf16[1,1024,512]{2,1,0:T(8,128)(2,1)S(1)} %copy-done), kind=kOutput, calls=%fused_computation.45 | convolution fusion | flops 536870912 | bytes 3670016 | tf_op jit(solution)/shard_map/dot_general | solution.py:29
  79.2 1.3 copy-done.8
  80.6 9.3 %subtract_convert_fusion = (bf16[1024,512]{0,1:T(8,128)(2,1)}, f32[1024,512]{0,1:T(8,128)}, f32[1024,512]{0,1:T(8,128)}) fusion(bf16[1024,512]{0,1:T(8,128)(2,1)S(1)} %copy-done.8, f32[512,1024]{1,0:T(8,128)} %get-tuple-element.14, f32[512,1024]{1,0:T(8,128)} %copy-done.12, f32[1,1024,512]{1,2,0:T(8,128)S(1)} %copy-done.2, f32[1,1024,512]{1,2,0:T(8,128)} %copy.11, ...), kind=kOutput, calls=%fused_computation.12 | convolution fusion | flops 556269568 | bytes 17301504 | tf_op jit(solution)/shard_map/dot_general | solution.py:25
  89.9 2.3 collective-permute-start.4
  92.2 12.8 %reduce-scatter.8.cloned.1.call-done = f32[256,1024]{1,0:T(8,128)} async-done(((f32[512,1024]{1,0:T(8,128)}), f32[256,1024]{1,0:T(8,128)}) %reduce-scatter.8.cloned.1.call-update) | async-done | bytes 1048592 | tf_op jit(solution)/shard_map/reduce_scatter | solution.py:28
  104.9 2.1 convert_element_type.59
  107.0 1.5 collective-permute-start.8
  108.5 30.6 %reduce-scatter.6.cloned.1.call-done = f32[256,1024]{1,0:T(8,128)} async-done(((f32[512,1024]{1,0:T(8,128)}), f32[256,1024]{1,0:T(8,128)}) %reduce-scatter.6.cloned.1.call-update) | async-done | bytes 1048592 | tf_op jit(solution)/shard_map/reduce_scatter | solution.py:28
  139.2 2.1 convert_element_type.58
  141.3 17.4 %collective-permute-done.4 = bf16[1024,512]{0,1:T(8,128)(2,1)S(1)} collective-permute-done((bf16[1024,512]{0,1:T(8,128)(2,1)}, bf16[1024,512]{0,1:T(8,128)(2,1)S(1)}, u32[]{:S(2)}, u32[]{:S(2)}) %collective-permute-start.4) | collective-permute-done | bytes 1048608 | tf_op jit(solution)/shard_map/ppermute | solution.py:11
  158.7 1.3 copy.14
  160.0 2.9 %copy.15 = f32[1,1024,512]{2,1,0:T(8,128)} copy(f32[1,1024,512]{1,2,0:T(8,128)} %bitcast.9) | data formatting | bytes 4194304
  162.9 1.8 copy.16
  164.7 8.7 %reduce-scatter.4.cloned.1.call-done = f32[256,1024]{1,0:T(8,128)} async-done(((f32[512,1024]{1,0:T(8,128)}), f32[256,1024]{1,0:T(8,128)}) %reduce-scatter.4.cloned.1.call-update) | async-done | bytes 1048592 | tf_op jit(solution)/shard_map/reduce_scatter | solution.py:28
  173.3 1.3 convert_bitcast_fusion
  174.6 41.5 %collective-permute-done.8 = bf16[256,1024]{1,0:T(8,128)(2,1)} collective-permute-done((bf16[256,1024]{1,0:T(8,128)(2,1)}, bf16[256,1024]{1,0:T(8,128)(2,1)}, u32[]{:S(2)}, u32[]{:S(2)}) %collective-permute-start.8) | collective-permute-done | bytes 524320 | tf_op jit(solution)/shard_map/ppermute | solution.py:11
  216.1 7.3 %collective-permute-done.7 = bf16[256,1024]{1,0:T(8,128)(2,1)} collective-permute-done((bf16[256,1024]{1,0:T(8,128)(2,1)}, bf16[256,1024]{1,0:T(8,128)(2,1)}, u32[]{:S(2)}, u32[]{:S(2)}) %collective-permute-start.7) | collective-permute-done | bytes 524320 | tf_op jit(solution)/shard_map/ppermute | solution.py:11
  223.4 2.5 %pad_maximum_fusion = bf16[3,256,1024]{2,1,0:T(8,128)(2,1)} fusion(bf16[1,256,1024]{2,1,0:T(8,128)(2,1)} %bitcast.13, bf16[1,256,1024]{2,1,0:T(8,128)(2,1)} %bitcast.12, bf16[1,256,1024]{2,1,0:T(8,128)(2,1)S(1)} %convert_bitcast_fusion), kind=kLoop, calls=%fused_computation.15 | loop fusion | flops 1572864 | bytes 3145728 | tf_op jit(solution)/shard_map/stack | solution.py:60
  (40 shorter events, 2.7 us)
Async XLA Ops:
  7.2 10.2 %copy-start.1 = (f32[1,1024,512]{2,1,0:T(8,128)S(1)}, f32[1,1024,512]{2,1,0:T(8,128)}, u32[]{:S(2)}) copy-start(f32[1,1024,512]{2,1,0:T(8,128)} %param.8) | copy-start | bytes 6291460
  7.2 97.8 %reduce-scatter.8.cloned.1.call-start = ((), (), s32[]{:S(2)}) async-start(), calls=%async_computation.5 | async-start | bytes 3145728 | tf_op jit(solution)/shard_map/reduce_scatter | solution.py:28
  7.2 29.3 %collective-permute-start.1 = (bf16[512,1024]{1,0:T(8,128)(2,1)}, bf16[512,1024]{1,0:T(8,128)(2,1)}, u32[]{:S(2)}, u32[]{:S(2)}) collective-permute-start(bf16[512,1024]{1,0:T(8,128)(2,1)} %param.5), channel_id=1, source_target_pairs={{0,30},{2,0},{4,2},{6,4},{8,6},{10,8},{12,10},{14,12},{16,14},{18,... | collective-permute-start | bytes 3145736 | tf_op jit(solution)/shard_map/ppermute | solution.py:11
  12.7 51.9 %collective-permute-start.3 = (bf16[512,1024]{1,0:T(8,128)(2,1)}, bf16[512,1024]{1,0:T(8,128)(2,1)}, u32[]{:S(2)}, u32[]{:S(2)}) collective-permute-start(bf16[512,1024]{1,0:T(8,128)(2,1)} %param.5), channel_id=1, source_target_pairs={{0,28},{2,30},{4,0},{6,2},{8,4},{10,6},{12,8},{14,10},{16,12},{18,... | collective-permute-start | bytes 3145736 | tf_op jit(solution)/shard_map/ppermute | solution.py:11
  13.4 45.7 %collective-permute-start = (bf16[512,512]{1,0:T(8,128)(2,1)}, bf16[512,512]{1,0:T(8,128)(2,1)}, u32[]{:S(2)}, u32[]{:S(2)}) collective-permute-start(bf16[512,512]{1,0:T(8,128)(2,1)} %param.6), channel_id=1, source_target_pairs={{0,30},{2,0},{4,2},{6,4},{8,6},{10,8},{12,10},{14,12},{16,14},{18,... | collective-permute-start | bytes 1572872 | tf_op jit(solution)/shard_map/ppermute | solution.py:11
  13.6 53.3 %collective-permute-start.2 = (bf16[512,512]{1,0:T(8,128)(2,1)}, bf16[512,512]{1,0:T(8,128)(2,1)}, u32[]{:S(2)}, u32[]{:S(2)}) collective-permute-start(bf16[512,512]{1,0:T(8,128)(2,1)} %param.6), channel_id=1, source_target_pairs={{0,28},{2,30},{4,0},{6,2},{8,4},{10,6},{12,8},{14,10},{16,12},{18,... | collective-permute-start | bytes 1572872 | tf_op jit(solution)/shard_map/ppermute | solution.py:11
  19.1 3.0 %copy-start = (bf16[1,1024,512]{2,1,0:T(8,128)(2,1)S(1)}, bf16[1,1024,512]{2,1,0:T(8,128)(2,1)}, u32[]{:S(2)}) copy-start(bf16[1,1024,512]{2,1,0:T(8,128)(2,1)} %param.7) | copy-start | bytes 3145732
  22.1 2.8 %copy-start.2 = (f32[1,1024,512]{1,2,0:T(8,128)S(1)}, f32[1,1024,512]{1,2,0:T(8,128)}, u32[]{:S(2)}) copy-start(f32[1,1024,512]{1,2,0:T(8,128)} %copy.10) | copy-start | bytes 6291460
  22.1 2.8 %copy-start.3 = (f32[1,1024,512]{1,2,0:T(8,128)S(1)}, f32[1,1024,512]{1,2,0:T(8,128)}, u32[]{:S(2)}) copy-start(f32[1,1024,512]{1,2,0:T(8,128)} %copy.11) | copy-start | bytes 6291460
  22.1 3.0 %copy-start.4 = (bf16[1,1024,512]{1,2,0:T(8,128)(2,1)S(1)}, bf16[1,1024,512]{1,2,0:T(8,128)(2,1)}, u32[]{:S(2)}) copy-start(bf16[1,1024,512]{1,2,0:T(8,128)(2,1)} %copy.9) | copy-start | bytes 3145732
  22.1 3.3 %copy-start.6 = (bf16[512,1024]{1,0:T(8,128)(2,1)S(1)}, bf16[512,1024]{1,0:T(8,128)(2,1)}, u32[]{:S(2)}) copy-start(bf16[512,1024]{1,0:T(8,128)(2,1)} %param.5) | copy-start | bytes 3145732
  25.4 2.0 copy-start.5
  27.3 37.3 %copy-start.10 = (bf16[1024,512]{0,1:T(8,128)(2,1)}, bf16[1024,512]{0,1:T(8,128)(2,1)S(1)}, u32[]{:S(2)}) copy-start(bf16[1024,512]{0,1:T(8,128)(2,1)S(1)} %get-tuple-element.11) | copy-start | bytes 3145732
  27.3 37.3 %copy-start.12 = (f32[512,1024]{1,0:T(8,128)}, f32[512,1024]{1,0:T(8,128)S(1)}, u32[]{:S(2)}) copy-start(f32[512,1024]{1,0:T(8,128)S(1)} %get-tuple-element.12) | copy-start | bytes 6291460
  38.5 26.1 %copy-start.11 = (f32[512,512]{1,0:T(8,128)}, f32[512,512]{1,0:T(8,128)S(1)}, u32[]{:S(2)}) copy-start(f32[512,512]{1,0:T(8,128)S(1)} %convolution_bitcast_fusion.1) | copy-start | bytes 3145732
  64.6 2.4 %copy-start.7 = (bf16[1024,512]{0,1:T(8,128)(2,1)}, bf16[1024,512]{0,1:T(8,128)(2,1)S(1)}, u32[]{:S(2)}) copy-start(bf16[1024,512]{0,1:T(8,128)(2,1)S(1)} %get-tuple-element.13) | copy-start | bytes 3145732
  67.0 1.0 copy-start.9
  71.6 67.6 %reduce-scatter.6.cloned.1.call-start = ((), (), s32[]{:S(2)}) async-start(), calls=%async_computation.4 | async-start | bytes 3145728 | tf_op jit(solution)/shard_map/reduce_scatter | solution.py:28
  75.9 97.5 %reduce-scatter.4.cloned.1.call-start = ((), (), s32[]{:S(2)}) async-start(), calls=%async_computation.3 | async-start | bytes 3145728 | tf_op jit(solution)/shard_map/reduce_scatter | solution.py:28
  79.2 1.4 copy-start.8
  89.8 70.1 %collective-permute-start.5 = (f32[1024,512]{0,1:T(8,128)}, f32[1024,512]{0,1:T(8,128)}, u32[]{:S(2)}, u32[]{:S(2)}) collective-permute-start(f32[1024,512]{0,1:T(8,128)} %get-tuple-element.9), channel_id=1, source_target_pairs={{0,6},{2,8},{4,10},{6,12},{8,14},{10,16},{12,18},{14,20},{16,22},{... | collective-permute-start | bytes 6291464 | tf_op jit(solution)/shard_map/ppermute | solution.py:11
  89.9 73.0 %collective-permute-start.6 = (f32[1024,512]{0,1:T(8,128)}, f32[1024,512]{0,1:T(8,128)S(1)}, u32[]{:S(2)}, u32[]{:S(2)}) collective-permute-start(f32[1024,512]{0,1:T(8,128)} %get-tuple-element.10), channel_id=1, source_target_pairs={{0,6},{2,8},{4,10},{6,12},{8,14},{10,16},{12,18},{14,20},{16,22},{... | collective-permute-start | bytes 6291464 | tf_op jit(solution)/shard_map/ppermute | solution.py:11
  89.9 68.8 %collective-permute-start.4 = (bf16[1024,512]{0,1:T(8,128)(2,1)}, bf16[1024,512]{0,1:T(8,128)(2,1)S(1)}, u32[]{:S(2)}, u32[]{:S(2)}) collective-permute-start(bf16[1024,512]{0,1:T(8,128)(2,1)} %get-tuple-element.8), channel_id=1, source_target_pairs={{0,6},{2,8},{4,10},{6,12},{8,14},{10,16},{12,18},{14,20},{16,22},{... | collective-permute-start | bytes 3145736 | tf_op jit(solution)/shard_map/ppermute | solution.py:11
  107.0 109.1 %collective-permute-start.8 = (bf16[256,1024]{1,0:T(8,128)(2,1)}, bf16[256,1024]{1,0:T(8,128)(2,1)}, u32[]{:S(2)}, u32[]{:S(2)}) collective-permute-start(bf16[256,1024]{1,0:T(8,128)(2,1)} %convert_element_type.59), channel_id=1, source_target_pairs={{0,4},{2,6},{4,8},{6,10},{8,12},{10,14},{12,16},{14,18},{16,20},{1... | collective-permute-start | bytes 1572872 | tf_op jit(solution)/shard_map/ppermute | solution.py:11
  141.3 82.2 %collective-permute-start.7 = (bf16[256,1024]{1,0:T(8,128)(2,1)}, bf16[256,1024]{1,0:T(8,128)(2,1)}, u32[]{:S(2)}, u32[]{:S(2)}) collective-permute-start(bf16[256,1024]{1,0:T(8,128)(2,1)} %convert_element_type.58), channel_id=1, source_target_pairs={{0,2},{2,4},{4,6},{6,8},{8,10},{10,12},{12,14},{14,16},{16,18},{18... | collective-permute-start | bytes 1572872 | tf_op jit(solution)/shard_map/ppermute | solution.py:11
Sparse Core Ops, SparseCore 0:
  71.7 33.2 reduce-scatter.7
  107.2 31.9 reduce-scatter.5
  141.4 31.8 reduce-scatter.3
where the time goes:
time: 233 us; the launch traced here: 232 us
  waiting for transfers between devices  148 us (64%)
  matrix products  34.8 us (15%)
  local copies, waits for them, and re-layouts  15.8 us (7%)
  between operations  13.9 us (6%)
  starting transfers between devices  11.9 us (5%)
  other arithmetic  7.99 us (3%)
    ppermute x9, waiting for transfers between devices, passed_along(): lax.ppermute(shard, axis, [(i, (i + by) % devices) for i in range(devices)])  96 us
    reduce_scatter x3, waiting for transfers between devices, train_local(): lax.psum_scatter(lax.dot_general(slopes, kernel, (((1,), (1,)), ((), ()))...  52.1 us
    dot_general x3, matrix products, train_local(): lax.dot_general(inputs, slopes, (((0,), (0,)), ((), ())), preferred_eleme...  16.7 us
    unnamed x32, local copies, waits for them, and re-layouts  15.8 us
    ppermute x9, starting transfers between devices, passed_along(): lax.ppermute(shard, axis, [(i, (i + by) % devices) for i in range(devices)])  11.6 us
    dot_general x3, matrix products, train_local(): lax.dot_general(slopes, kernel, (((1,), (1,)), ((), ())), preferred_eleme...  10.9 us
    dot_general x3, matrix products, train_local(): preact = jnp.dot(inputs, kernel, preferred_element_type=jnp.float32)  7.09 us
  transfers between devices with their start and end apart: 12, of which 8 were waited for; matrix products, arithmetic and copies ran while one was open for 21% of the time, Pallas kernels for 0%

commit v1 on v0

v1 whole, which is shorter than its diff:
```python
import jax
import jax.numpy as jnp
from jax import lax
from jax.sharding import PartitionSpec as P

HOPS = 3


def passed_along(part, axis, by):
    devices = lax.axis_size(axis)
    return lax.ppermute(part, axis, [(i, (i + by) % devices) for i in range(devices)])


def gelu_slope(values):
    inner = 0.7978845608 * (values + 0.044715 * values * values * values)
    tanh_part = jnp.tanh(inner)
    return 0.5 * (1.0 + tanh_part) + 0.5 * values * (1.0 - tanh_part * tanh_part) * 0.7978845608 * (
        1.0 + 0.134145 * values * values
    )


def slopes_of(kernel, inputs, grad_out):
    preact = jnp.dot(inputs, kernel, preferred_element_type=jnp.float32)
    return (grad_out.astype(jnp.float32) * gelu_slope(preact)).astype(jnp.bfloat16)


def update(kernel, first, second, inputs, slopes):
    gradient = lax.dot_general(
        inputs, slopes, (((0,), (0,)), ((), ())), preferred_element_type=jnp.float32
    )
    first = 0.9 * first.astype(jnp.float32) + 0.1 * gradient
    second = 0.95 * second.astype(jnp.float32) + 0.05 * gradient * gradient
    kernel = (kernel.astype(jnp.float32) - 0.01 * first / (jnp.sqrt(second) + 1e-08)).astype(
        jnp.bfloat16
    )
    return kernel, first, second


def returned_sum(slopes, kernel):
    shards = lax.axis_size("shard")
    me = lax.axis_index("shard")
    rows = slopes.shape[0] // shards

    def part(owner):
        mine = lax.dynamic_slice_in_dim(slopes, owner * rows, rows, 0)
        return lax.dot_general(
            mine, kernel, (((1,), (1,)), ((), ())), preferred_element_type=jnp.float32
        )

    arrived = [
        passed_along(part((me + k) % shards).astype(jnp.bfloat16), "shard", k)
        for k in range(1, shards)
    ]
    total = part(me)
    for piece in arrived:
        total = total + piece.astype(jnp.float32)
    return total.astype(jnp.bfloat16)


def shards(cut_acts, upstream, weights, moment_one, moment_two):
    kernel, first, second = weights[0], moment_one[0], moment_two[0]
    after = passed_along((cut_acts, upstream), "blk", -1)
    before = passed_along((cut_acts, upstream), "blk", 1)

    slopes = slopes_of(kernel, cut_acts, upstream)
    returned = [returned_sum(slopes, kernel)]
    kernel, first, second = update(kernel, first, second, cut_acts, slopes)

    slopes = slopes_of(kernel, *after)
    back = returned_sum(slopes, kernel)
    kernel, first, second = update(kernel, first, second, after[0], slopes)
    kernel = passed_along(kernel, "blk", HOPS)
    first = passed_along(first.astype(jnp.bfloat16), "blk", HOPS)
    second = passed_along(second.astype(jnp.bfloat16), "blk", HOPS)
    returned.append(passed_along(back, "blk", 1))

    slopes = slopes_of(kernel, *before)
    returned.append(passed_along(returned_sum(slopes, kernel), "blk", -1))
    kernel, first, second = update(kernel, first, second, before[0], slopes)
    return (kernel[None], first[None], second[None], jnp.stack(returned))


def solution(mesh):
    placed = (
        P("blk", None),
        P("blk", "shard"),
        P("blk", None, "shard"),
        P("blk", None, "shard"),
        P("blk", None, "shard"),
    )
    return jax.shard_map(
        shards,
        mesh=mesh,
        in_specs=placed,
        out_specs=(
            P("blk", None, "shard"),
            P("blk", None, "shard"),
            P("blk", None, "shard"),
            P(None, ("blk", "shard"), None),
        ),
        check_vma=False,
    )
```

time: 233 us -> 132 us (0.57)
  the two profiles are of different devices: /device:TPU:0 before, /device:TPU:4 now
where the time goes in v1:
time: 132 us; the launch traced here: 131 us
  waiting for transfers between devices  43.4 us (33%)
  starting transfers between devices  37.2 us (28%)
  matrix products  33.3 us (25%)
  local copies, waits for them, and re-layouts  14.2 us (11%)
  other arithmetic  2.51 us (2%)
    ppermute x12, waiting for transfers between devices, passed_along(): lax.ppermute(part, axis, [(i, (i + by) % devices) for i in range(devices)])  43.4 us
    ppermute x12, starting transfers between devices, passed_along(): lax.ppermute(part, axis, [(i, (i + by) % devices) for i in range(devices)])  37.2 us
    unnamed x30, local copies, waits for them, and re-layouts  14.2 us
    dot_general x3, matrix products, update(): lax.dot_general(inputs, slopes, (((0,), (0,)), ((), ())), preferred_eleme...  12.9 us
    dot_general x6, matrix products, part(): lax.dot_general(mine, kernel, (((1,), (1,)), ((), ())), preferred_element...  12.7 us
    dot_general x3, matrix products, slopes_of(): preact = jnp.dot(inputs, kernel, preferred_element_type=jnp.float32)  7.79 us
  transfers between devices with their start and end apart: 12, of which 4 were waited for; matrix products, arithmetic and copies ran while one was open for 35% of the time, Pallas kernels for 0%

profile of v1, /device:TPU:4, one launch (start us, length us, event | category | flops | bytes accessed | tf_op | source)
XLA Modules:
  0.0 131.5 jit_solution(16409660362508452751)
XLA Ops:
  1.2 1.3 collective-permute-start
  2.5 1.5 %copy.9 = bf16[1,1024,512]{1,2,0:T(8,128)(2,1)S(1)} copy(bf16[1,1024,512]{2,1,0:T(8,128)(2,1)} %param.7) | data formatting | bytes 2097152 | tf_op args[2]
  4.0 1.8 %copy.10 = f32[1,1024,512]{1,2,0:T(8,128)} copy(f32[1,1024,512]{2,1,0:T(8,128)S(1)} %copy-done.1) | data formatting | bytes 4194304 | tf_op args[3]
  5.8 3.0 %copy.11 = f32[1,1024,512]{1,2,0:T(8,128)} copy(f32[1,1024,512]{2,1,0:T(8,128)} %param.9) | data formatting | bytes 4194304 | tf_op args[4]
  8.9 2.5 %fusion.16 = bf16[512,512]{1,0:T(8,128)(2,1)S(1)} fusion(bf16[512,1024]{1,0:T(8,128)(2,1)S(1)} %copy-done.10, bf16[1,1024,512]{2,1,0:T(8,128)(2,1)S(1)} %copy-done, bf16[512,512]{1,0:T(8,128)(2,1)} %param.6), kind=kOutput, calls=%fused_computation.39 | convolution fusion | flops 542113792 | bytes 3145728 | tf_op jit(solution)/shard_map/dot_general | solution.py:23
  11.5 1.9 %subtract_convert_fusion.2 = (bf16[1024,512]{0,1:T(8,128)(2,1)S(1)}, f32[512,1024]{1,0:T(8,128)S(1)}) fusion(bf16[1,1024,512]{1,2,0:T(8,128)(2,1)S(1)} %copy.9, f32[1,1024,512]{1,2,0:T(8,128)S(1)} %copy-done.2, f32[1,1024,512]{1,2,0:T(8,128)S(1)} %copy-done.3, bf16[512,512]{1,0:T(8,128)(2,1)S(1)} %fusion.16, bf16[512,1024]{1,0:T(8,128)(2,1)S(1)} %copy-done.11), kind=kOutput, calls=%fused_computation.14 | convolution fusion | flops 543686656 | bytes 9961472 | tf_op jit(solution)/shard_map/dot_general | solution.py:28
  13.4 16.8 %collective-permute-done = bf16[512,512]{1,0:T(8,128)(2,1)} collective-permute-done((bf16[512,512]{1,0:T(8,128)(2,1)}, bf16[512,512]{1,0:T(8,128)(2,1)}, u32[]{:S(2)}, u32[]{:S(2)}) %collective-permute-start) | collective-permute-done | bytes 524320 | tf_op jit(solution)/shard_map/ppermute | solution.py:11
  30.2 2.7 %fusion.23 = bf16[512,512]{1,0:T(8,128)(2,1)S(1)} fusion(bf16[512,512]{1,0:T(8,128)(2,1)} %collective-permute-done, bf16[1024,512]{0,1:T(8,128)(2,1)S(1)} %get-tuple-element.14, bf16[512,1024]{1,0:T(8,128)(2,1)} %collective-permute-done.1), kind=kOutput, calls=%fused_computation.46 | convolution fusion | flops 542113792 | bytes 3145728 | tf_op jit(solution)/shard_map/dot_general | solution.py:23
  32.9 5.5 %fusion.57 = (bf16[1024,512]{0,1:T(8,128)(2,1)}, bf16[1024,512]{0,1:T(8,128)(2,1)}, bf16[1024,512]{0,1:T(8,128)(2,1)}) fusion(f32[512,1024]{1,0:T(8,128)S(1)} %get-tuple-element.15, f32[1,1024,512]{1,2,0:T(8,128)S(1)} %copy-done.2, f32[1,1024,512]{1,2,0:T(8,128)S(1)} %copy-done.3, bf16[1024,512]{0,1:T(8,128)(2,1)S(1)} %get-tuple-element.14, ...), kind=kOutput, calls=%fused_computation.75 | convolution fusion | flops 548405248 | bytes 12058624 | tf_op jit(solution)/shard_map/dot_general | solution.py:28
  38.3 2.9 %collective-permute-start.2 = (bf16[1024,512]{0,1:T(8,128)(2,1)}, bf16[1024,512]{0,1:T(8,128)(2,1)S(1)}, u32[]{:S(2)}, u32[]{:S(2)}) collective-permute-start(bf16[1024,512]{0,1:T(8,128)(2,1)} %get-tuple-element.9), channel_id=1, source_target_pairs={{0,6},{2,8},{4,10},{6,12},{8,14},{10,16},{12,18},{14,20},{16,22},{... | collective-permute-start | bytes 3145736 | tf_op jit(solution)/shard_map/ppermute | solution.py:11
  41.3 2.2 %convolution_convert_fusion.2 = bf16[256,1024]{1,0:T(8,128)(2,1)} fusion(bf16[1,1024,512]{2,1,0:T(8,128)(2,1)S(1)} %copy-done, bf16[512,512]{1,0:T(8,128)(2,1)} %copy-done.5, s32[]{:T(128)S(6)} %select_n.23), kind=kOutput, calls=%fused_computation.28 | convolution fusion | flops 268697600 | bytes 1835012 | tf_op jit(solution)/shard_map/dot_general | solution.py:46
  43.5 1.5 %collective-permute-start.7 = (bf16[256,1024]{1,0:T(8,128)(2,1)}, bf16[256,1024]{1,0:T(8,128)(2,1)}, u32[]{:S(2)}, u32[]{:S(2)}) collective-permute-start(bf16[256,1024]{1,0:T(8,128)(2,1)} %convolution_convert_fusion.2), channel_id=1, source_target_pairs={{0,1},{1,0},{2,3},{3,2},{4,5},{5,4},{6,7},{7,6},{8,9},{9,8},{10,11... | collective-permute-start | bytes 1572872 | tf_op jit(solution)/shard_map/ppermute | solution.py:11
  45.0 2.5 %collective-permute-start.6 = (bf16[1024,512]{0,1:T(8,128)(2,1)}, bf16[1024,512]{0,1:T(8,128)(2,1)}, u32[]{:S(2)}, u32[]{:S(2)}) collective-permute-start(bf16[1024,512]{0,1:T(8,128)(2,1)} %get-tuple-element.10), channel_id=1, source_target_pairs={{0,6},{2,8},{4,10},{6,12},{8,14},{10,16},{12,18},{14,20},{16,22},{... | collective-permute-start | bytes 3145736 | tf_op jit(solution)/shard_map/ppermute | solution.py:11
  47.4 2.2 %convolution_convert_fusion.1 = bf16[256,1024]{1,0:T(8,128)(2,1)} fusion(bf16[1024,512]{0,1:T(8,128)(2,1)S(1)} %get-tuple-element.14, bf16[512,512]{1,0:T(8,128)(2,1)} %copy-done.6, s32[]{:T(128)S(6)} %select_n.23), kind=kOutput, calls=%fused_computation.27 | convolution fusion | flops 268697600 | bytes 1835012 | tf_op jit(solution)/shard_map/dot_general | solution.py:46
  49.6 4.1 %collective-permute-done.4 = bf16[512,512]{1,0:T(8,128)(2,1)} collective-permute-done((bf16[512,512]{1,0:T(8,128)(2,1)}, bf16[512,512]{1,0:T(8,128)(2,1)}, u32[]{:S(2)}, u32[]{:S(2)}) %collective-permute-start.4) | collective-permute-done | bytes 524320 | tf_op jit(solution)/shard_map/ppermute | solution.py:11
  53.7 2.5 %collective-permute-start.8 = (bf16[256,1024]{1,0:T(8,128)(2,1)}, bf16[256,1024]{1,0:T(8,128)(2,1)}, u32[]{:S(2)}, u32[]{:S(2)}) collective-permute-start(bf16[256,1024]{1,0:T(8,128)(2,1)} %convolution_convert_fusion.1), channel_id=1, source_target_pairs={{0,1},{1,0},{2,3},{3,2},{4,5},{5,4},{6,7},{7,6},{8,9},{9,8},{10,11... | collective-permute-start | bytes 1572872 | tf_op jit(solution)/shard_map/ppermute | solution.py:11
  56.2 9.0 %collective-permute-done.2 = bf16[1024,512]{0,1:T(8,128)(2,1)S(1)} collective-permute-done((bf16[1024,512]{0,1:T(8,128)(2,1)}, bf16[1024,512]{0,1:T(8,128)(2,1)S(1)}, u32[]{:S(2)}, u32[]{:S(2)}) %collective-permute-start.2) | collective-permute-done | bytes 1048608 | tf_op jit(solution)/shard_map/ppermute | solution.py:11
  65.1 2.7 %fusion.30 = bf16[512,512]{1,0:T(8,128)(2,1)S(1)} fusion(bf16[512,512]{1,0:T(8,128)(2,1)} %collective-permute-done.4, bf16[1024,512]{0,1:T(8,128)(2,1)S(1)} %collective-permute-done.2, bf16[512,1024]{1,0:T(8,128)(2,1)} %collective-permute-done.5), kind=kOutput, calls=%fused_computation.53 | convolution fusion | flops 542113792 | bytes 3145728 | tf_op jit(solution)/shard_map/dot_general | solution.py:23
  67.8 0.8 copy-done.8
  68.6 1.2 convolution_convert_fusion
  69.8 1.5 %collective-permute-start.10 = (bf16[256,1024]{1,0:T(8,128)(2,1)}, bf16[256,1024]{1,0:T(8,128)(2,1)}, u32[]{:S(2)}, u32[]{:S(2)}) collective-permute-start(bf16[256,1024]{1,0:T(8,128)(2,1)} %convolution_convert_fusion), channel_id=1, source_target_pairs={{0,1},{1,0},{2,3},{3,2},{4,5},{5,4},{6,7},{7,6},{8,9},{9,8},{10,11... | collective-permute-start | bytes 1572872 | tf_op jit(solution)/shard_map/ppermute | solution.py:11
  71.3 2.5 %fusion.40 = bf16[1,256,1024]{2,1,0:T(8,128)(2,1)} fusion(bf16[256,1024]{1,0:T(8,128)(2,1)} %collective-permute-done.7, bf16[1,1024,512]{2,1,0:T(8,128)(2,1)S(1)} %copy-done, bf16[512,512]{1,0:T(8,128)(2,1)} %copy-done.5, s32[]{:T(128)S(6)} %select_n.21), kind=kOutput, calls=%fused_computation.62 | convolution fusion | flops 269221888 | bytes 2359300 | tf_op jit(solution)/shard_map/dot_general | solution.py:46
  73.8 2.3 %fusion.6 = bf16[256,1024]{1,0:T(8,128)(2,1)} fusion(bf16[1024,512]{0,1:T(8,128)(2,1)S(1)} %get-tuple-element.14, bf16[256,1024]{1,0:T(8,128)(2,1)} %collective-permute-done.8, bf16[512,512]{1,0:T(8,128)(2,1)S(1)} %copy-done.7, s32[]{:T(128)S(6)} %select_n.21), kind=kOutput, calls=%fused_computation.29 | convolution fusion | flops 269221888 | bytes 2359300 | tf_op jit(solution)/shard_map/dot_general | solution.py:46
  76.1 11.3 %collective-permute-start.9 = (bf16[256,1024]{1,0:T(8,128)(2,1)}, bf16[256,1024]{1,0:T(8,128)(2,1)}, u32[]{:S(2)}, u32[]{:S(2)}) collective-permute-start(bf16[256,1024]{1,0:T(8,128)(2,1)} %fusion.6), channel_id=1, source_target_pairs={{0,2},{2,4},{4,6},{6,8},{8,10},{10,12},{12,14},{14,16},{16,18},{18... | collective-permute-start | bytes 1572872 | tf_op jit(solution)/shard_map/ppermute | solution.py:11
  87.4 2.3 %fusion.7 = bf16[256,1024]{1,0:T(8,128)(2,1)} fusion(bf16[1024,512]{0,1:T(8,128)(2,1)S(1)} %collective-permute-done.2, bf16[256,1024]{1,0:T(8,128)(2,1)} %collective-permute-done.10, bf16[512,512]{1,0:T(8,128)(2,1)S(1)} %copy-done.9, s32[]{:T(128)S(6)} %select_n.21), kind=kOutput, calls=%fused_computation.30 | convolution fusion | flops 269221888 | bytes 2359300 | tf_op jit(solution)/shard_map/dot_general | solution.py:46
  89.6 13.3 %collective-permute-start.11 = (bf16[256,1024]{1,0:T(8,128)(2,1)}, bf16[256,1024]{1,0:T(8,128)(2,1)}, u32[]{:S(2)}, u32[]{:S(2)}) collective-permute-start(bf16[256,1024]{1,0:T(8,128)(2,1)} %fusion.7), channel_id=1, source_target_pairs={{0,30},{2,0},{4,2},{6,4},{8,6},{10,8},{12,10},{14,12},{16,14},{18,... | collective-permute-start | bytes 1572872 | tf_op jit(solution)/shard_map/ppermute | solution.py:11
  102.9 13.6 %collective-permute-done.3 = bf16[1024,512]{0,1:T(8,128)(2,1)} collective-permute-done((bf16[1024,512]{0,1:T(8,128)(2,1)}, bf16[1024,512]{0,1:T(8,128)(2,1)}, u32[]{:S(2)}, u32[]{:S(2)}) %collective-permute-start.3) | collective-permute-done | bytes 1048608 | tf_op jit(solution)/shard_map/ppermute | solution.py:11
  116.5 5.5 %fusion.9 = (f32[1,1024,512]{1,2,0:T(8,128)S(1)}, bf16[1,1024,512]{1,2,0:T(8,128)(2,1)}, f32[1,1024,512]{1,2,0:T(8,128)}) fusion(bf16[1024,512]{0,1:T(8,128)(2,1)} %collective-permute-done.6, bf16[1024,512]{0,1:T(8,128)(2,1)} %collective-permute-done.3, bf16[1024,512]{0,1:T(8,128)(2,1)S(1)} %collective-permute-done.2, bf16[512,512]{1,0:T(8,128)(2,1)S(1)} %copy-done.9, ...), kind=kOutput, calls=%fused_computation.32 | convolution fusion | flops 544735232 | bytes 9961472 | tf_op jit(solution)/shard_map/dot_general | solution.py:28
  122.0 2.3 %copy.14 = bf16[1,1024,512]{2,1,0:T(8,128)(2,1)} copy(bf16[1,1024,512]{1,2,0:T(8,128)(2,1)} %get-tuple-element.12) | data formatting | bytes 2097152
  124.3 2.9 %copy.15 = f32[1,1024,512]{2,1,0:T(8,128)} copy(f32[1,1024,512]{1,2,0:T(8,128)} %get-tuple-element.13) | data formatting | bytes 4194304
  127.1 1.8 %copy.16 = f32[1,1024,512]{2,1,0:T(8,128)} copy(f32[1,1024,512]{1,2,0:T(8,128)S(1)} %get-tuple-element.11) | data formatting | bytes 4194304
  129.0 2.5 %pad_maximum_fusion = bf16[3,256,1024]{2,1,0:T(8,128)(2,1)} fusion(bf16[1,256,1024]{2,1,0:T(8,128)(2,1)} %bitcast.13, bf16[1,256,1024]{2,1,0:T(8,128)(2,1)} %bitcast.12, bf16[1,256,1024]{2,1,0:T(8,128)(2,1)S(1)} %copy-done.4), kind=kLoop, calls=%fused_computation.15 | loop fusion | flops 1572864 | bytes 3145728 | tf_op jit(solution)/shard_map/stack | solution.py:80
  (35 shorter events, 0.8 us)
Async XLA Ops:
  0.6 3.4 %copy-start.1 = (f32[1,1024,512]{2,1,0:T(8,128)S(1)}, f32[1,1024,512]{2,1,0:T(8,128)}, u32[]{:S(2)}) copy-start(f32[1,1024,512]{2,1,0:T(8,128)} %param.8) | copy-start | bytes 6291460
  0.6 29.6 %collective-permute-start.1 = (bf16[512,1024]{1,0:T(8,128)(2,1)}, bf16[512,1024]{1,0:T(8,128)(2,1)}, u32[]{:S(2)}, u32[]{:S(2)}) collective-permute-start(bf16[512,1024]{1,0:T(8,128)(2,1)} %param.5), channel_id=1, source_target_pairs={{0,30},{2,0},{4,2},{6,4},{8,6},{10,8},{12,10},{14,12},{16,14},{18,... | collective-permute-start | bytes 3145736 | tf_op jit(solution)/shard_map/ppermute | solution.py:11
  0.7 53.0 %collective-permute-start.5 = (bf16[512,1024]{1,0:T(8,128)(2,1)}, bf16[512,1024]{1,0:T(8,128)(2,1)}, u32[]{:S(2)}, u32[]{:S(2)}) collective-permute-start(bf16[512,1024]{1,0:T(8,128)(2,1)} %param.5), channel_id=1, source_target_pairs={{0,2},{2,4},{4,6},{6,8},{8,10},{10,12},{12,14},{14,16},{16,18},{18... | collective-permute-start | bytes 3145736 | tf_op jit(solution)/shard_map/ppermute | solution.py:11
  1.2 29.0 %collective-permute-start = (bf16[512,512]{1,0:T(8,128)(2,1)}, bf16[512,512]{1,0:T(8,128)(2,1)}, u32[]{:S(2)}, u32[]{:S(2)}) collective-permute-start(bf16[512,512]{1,0:T(8,128)(2,1)} %param.6), channel_id=1, source_target_pairs={{0,30},{2,0},{4,2},{6,4},{8,6},{10,8},{12,10},{14,12},{16,14},{18,... | collective-permute-start | bytes 1572872 | tf_op jit(solution)/shard_map/ppermute | solution.py:11
  5.8 3.0 %copy-start = (bf16[1,1024,512]{2,1,0:T(8,128)(2,1)S(1)}, bf16[1,1024,512]{2,1,0:T(8,128)(2,1)}, u32[]{:S(2)}) copy-start(bf16[1,1024,512]{2,1,0:T(8,128)(2,1)} %param.7) | copy-start | bytes 3145732
  5.8 3.0 %copy-start.10 = (bf16[512,1024]{1,0:T(8,128)(2,1)S(1)}, bf16[512,1024]{1,0:T(8,128)(2,1)}, u32[]{:S(2)}) copy-start(bf16[512,1024]{1,0:T(8,128)(2,1)} %param.5) | copy-start | bytes 3145732
  8.9 2.5 %copy-start.2 = (f32[1,1024,512]{1,2,0:T(8,128)S(1)}, f32[1,1024,512]{1,2,0:T(8,128)}, u32[]{:S(2)}) copy-start(f32[1,1024,512]{1,2,0:T(8,128)} %copy.10) | copy-start | bytes 6291460
  8.9 2.5 %copy-start.3 = (f32[1,1024,512]{1,2,0:T(8,128)S(1)}, f32[1,1024,512]{1,2,0:T(8,128)}, u32[]{:S(2)}) copy-start(f32[1,1024,512]{1,2,0:T(8,128)} %copy.11) | copy-start | bytes 6291460
  8.9 2.6 %copy-start.11 = (bf16[512,1024]{1,0:T(8,128)(2,1)S(1)}, bf16[512,1024]{1,0:T(8,128)(2,1)}, u32[]{:S(2)}) copy-start(bf16[512,1024]{1,0:T(8,128)(2,1)} %param.5) | copy-start | bytes 3145732
  11.5 1.9 %copy-start.5 = (bf16[512,512]{1,0:T(8,128)(2,1)}, bf16[512,512]{1,0:T(8,128)(2,1)S(1)}, u32[]{:S(2)}) copy-start(bf16[512,512]{1,0:T(8,128)(2,1)S(1)} %fusion.16) | copy-start | bytes 1572868
  32.9 5.5 %copy-start.6 = (bf16[512,512]{1,0:T(8,128)(2,1)}, bf16[512,512]{1,0:T(8,128)(2,1)S(1)}, u32[]{:S(2)}) copy-start(bf16[512,512]{1,0:T(8,128)(2,1)S(1)} %fusion.23) | copy-start | bytes 1572868
  38.3 26.8 %collective-permute-start.2 = (bf16[1024,512]{0,1:T(8,128)(2,1)}, bf16[1024,512]{0,1:T(8,128)(2,1)S(1)}, u32[]{:S(2)}, u32[]{:S(2)}) collective-permute-start(bf16[1024,512]{0,1:T(8,128)(2,1)} %get-tuple-element.9), channel_id=1, source_target_pairs={{0,6},{2,8},{4,10},{6,12},{8,14},{10,16},{12,18},{14,20},{16,22},{... | collective-permute-start | bytes 3145736 | tf_op jit(solution)/shard_map/ppermute | solution.py:11
  41.3 12.4 %collective-permute-start.4 = (bf16[512,512]{1,0:T(8,128)(2,1)}, bf16[512,512]{1,0:T(8,128)(2,1)}, u32[]{:S(2)}, u32[]{:S(2)}) collective-permute-start(bf16[512,512]{1,0:T(8,128)(2,1)} %param.6), channel_id=1, source_target_pairs={{0,2},{2,4},{4,6},{6,8},{8,10},{10,12},{12,14},{14,16},{16,18},{18... | collective-permute-start | bytes 1572872 | tf_op jit(solution)/shard_map/ppermute | solution.py:11
  43.5 27.9 %collective-permute-start.7 = (bf16[256,1024]{1,0:T(8,128)(2,1)}, bf16[256,1024]{1,0:T(8,128)(2,1)}, u32[]{:S(2)}, u32[]{:S(2)}) collective-permute-start(bf16[256,1024]{1,0:T(8,128)(2,1)} %convolution_convert_fusion.2), channel_id=1, source_target_pairs={{0,1},{1,0},{2,3},{3,2},{4,5},{5,4},{6,7},{7,6},{8,9},{9,8},{10,11... | collective-permute-start | bytes 1572872 | tf_op jit(solution)/shard_map/ppermute | solution.py:11
  45.0 58.0 %collective-permute-start.6 = (bf16[1024,512]{0,1:T(8,128)(2,1)}, bf16[1024,512]{0,1:T(8,128)(2,1)}, u32[]{:S(2)}, u32[]{:S(2)}) collective-permute-start(bf16[1024,512]{0,1:T(8,128)(2,1)} %get-tuple-element.10), channel_id=1, source_target_pairs={{0,6},{2,8},{4,10},{6,12},{8,14},{10,16},{12,18},{14,20},{16,22},{... | collective-permute-start | bytes 3145736 | tf_op jit(solution)/shard_map/ppermute | solution.py:11
  53.7 62.8 %collective-permute-start.3 = (bf16[1024,512]{0,1:T(8,128)(2,1)}, bf16[1024,512]{0,1:T(8,128)(2,1)}, u32[]{:S(2)}, u32[]{:S(2)}) collective-permute-start(bf16[1024,512]{0,1:T(8,128)(2,1)} %get-tuple-element.8), channel_id=1, source_target_pairs={{0,6},{2,8},{4,10},{6,12},{8,14},{10,16},{12,18},{14,20},{16,22},{... | collective-permute-start | bytes 3145736 | tf_op jit(solution)/shard_map/ppermute | solution.py:11
  53.7 20.1 %collective-permute-start.8 = (bf16[256,1024]{1,0:T(8,128)(2,1)}, bf16[256,1024]{1,0:T(8,128)(2,1)}, u32[]{:S(2)}, u32[]{:S(2)}) collective-permute-start(bf16[256,1024]{1,0:T(8,128)(2,1)} %convolution_convert_fusion.1), channel_id=1, source_target_pairs={{0,1},{1,0},{2,3},{3,2},{4,5},{5,4},{6,7},{7,6},{8,9},{9,8},{10,11... | collective-permute-start | bytes 1572872 | tf_op jit(solution)/shard_map/ppermute | solution.py:11
  67.8 0.8 copy-start.8
  69.8 17.5 %collective-permute-start.10 = (bf16[256,1024]{1,0:T(8,128)(2,1)}, bf16[256,1024]{1,0:T(8,128)(2,1)}, u32[]{:S(2)}, u32[]{:S(2)}) collective-permute-start(bf16[256,1024]{1,0:T(8,128)(2,1)} %convolution_convert_fusion), channel_id=1, source_target_pairs={{0,1},{1,0},{2,3},{3,2},{4,5},{5,4},{6,7},{7,6},{8,9},{9,8},{10,11... | collective-permute-start | bytes 1572872 | tf_op jit(solution)/shard_map/ppermute | solution.py:11
  71.3 2.5 %copy-start.7 = (bf16[512,512]{1,0:T(8,128)(2,1)S(1)}, bf16[512,512]{1,0:T(8,128)(2,1)}, u32[]{:S(2)}) copy-start(bf16[512,512]{1,0:T(8,128)(2,1)} %copy-done.6) | copy-start | bytes 1572868
  71.3 16.0 %copy-start.9 = (bf16[512,512]{1,0:T(8,128)(2,1)S(1)}, bf16[512,512]{1,0:T(8,128)(2,1)}, u32[]{:S(2)}) copy-start(bf16[512,512]{1,0:T(8,128)(2,1)} %copy-done.8) | copy-start | bytes 1572868
  76.1 52.9 %collective-permute-start.9 = (bf16[256,1024]{1,0:T(8,128)(2,1)}, bf16[256,1024]{1,0:T(8,128)(2,1)}, u32[]{:S(2)}, u32[]{:S(2)}) collective-permute-start(bf16[256,1024]{1,0:T(8,128)(2,1)} %fusion.6), channel_id=1, source_target_pairs={{0,2},{2,4},{4,6},{6,8},{8,10},{10,12},{12,14},{14,16},{16,18},{18... | collective-permute-start | bytes 1572872 | tf_op jit(solution)/shard_map/ppermute | solution.py:11
  89.6 39.3 %collective-permute-start.11 = (bf16[256,1024]{1,0:T(8,128)(2,1)}, bf16[256,1024]{1,0:T(8,128)(2,1)}, u32[]{:S(2)}, u32[]{:S(2)}) collective-permute-start(bf16[256,1024]{1,0:T(8,128)(2,1)} %fusion.7), channel_id=1, source_target_pairs={{0,30},{2,0},{4,2},{6,4},{8,6},{10,8},{12,10},{14,12},{16,14},{18,... | collective-permute-start | bytes 1572872 | tf_op jit(solution)/shard_map/ppermute | solution.py:11
  127.1 1.8 %copy-start.4 = (bf16[1,256,1024]{2,1,0:T(8,128)(2,1)S(1)}, bf16[1,256,1024]{2,1,0:T(8,128)(2,1)}, u32[]{:S(2)}) copy-start(bf16[1,256,1024]{2,1,0:T(8,128)(2,1)} %fusion.40) | copy-start | bytes 1572868

commit v2 on v0

v2 whole, which is shorter than its diff:
```python
import functools

import jax
import jax.numpy as jnp
from jax import lax
from jax.experimental import pallas as pl
from jax.experimental.pallas import tpu as pltpu
from jax.sharding import PartitionSpec as P


HOPS = 3
F32, BF16 = jnp.float32, jnp.bfloat16
ANY = pl.BlockSpec(memory_space=pl.ANY)
WHOLE = pl.BlockSpec(memory_space=pltpu.VMEM)
MIB = 1024 * 1024


def passed_along(part, axis, by):
    devices = lax.axis_size(axis)
    return lax.ppermute(part, axis, [(i, (i + by) % devices) for i in range(devices)])


def routed(part, route):
    return jax.tree.map(lambda one: lax.ppermute(one, "blk", sorted(route.items())), part)


def only_if(chosen, body):
    if chosen is None:
        body()
    else:
        pl.when(chosen)(body)


def gelu_slope(values):
    square = values * values
    tanh_part = jnp.tanh(values * (0.7978845608 + 0.7978845608 * 0.044715 * square))
    return (0.5 + 0.5 * tanh_part) + (values * (1.0 - tanh_part * tanh_part)) * (
        0.5 * 0.7978845608 + 0.5 * 0.7978845608 * 0.134145 * square
    )


def blocks(size, step):
    step = step if size % step == 0 else size
    return [pl.ds(at, step) for at in range(0, size, step)]


def slopes_body(x, g, w, z, s):
    for cols in blocks(g.shape[1], 256):
        z[:, cols] = jnp.dot(x[...], w[:, cols], preferred_element_type=F32)
        for rows in blocks(x.shape[0], 64):
            s[rows, cols] = (g[rows, cols].astype(F32) * gelu_slope(z[rows, cols])).astype(BF16)


def update_rows(grad, w, m, v, w_new, m_new, v_new, rows):
    for at in blocks(rows.size, 32):
        at = pl.ds(rows.start + at.start, at.size)
        gradient = grad[at, :]
        first = 0.9 * m[at, :].astype(F32) + 0.1 * gradient
        second = 0.95 * v[at, :].astype(F32) + 0.05 * (gradient * gradient)
        m_new[at, :] = first.astype(m_new.dtype)
        v_new[at, :] = second.astype(v_new.dtype)
        root = second * lax.rsqrt(second)
        inverse = lax.rsqrt(second + 1e-08 * (2.0 * root + 1e-08))
        w_new[at, :] = (w[at, :].astype(F32) - (0.01 * first) * inverse).astype(BF16)


def train_kernel(parity, refs):
    if parity is None:
        train_body(*refs)
    else:
        pl.when(lax.rem(lax.axis_index("blk"), 2) == parity)(lambda: train_body(*refs))


def train_body(x_in, g_in, w_in, moments, w_out, mv_out, s_out, h_out,
               x, xt, g, w, m, v, z, s, grad, w_new, m_new, v_new, sem):
    m_in, v_in = (moments[0].at[0], moments[0].at[1]) if len(moments) == 1 else moments
    bands = blocks(w.shape[0], 256)
    n = len(bands)
    gets = [pltpu.make_async_copy(one, ref, sem.at[i]) for i, (one, ref) in enumerate(((x_in, x), (w_in, w), (g_in, g)))]
    gets += [
        pltpu.make_async_copy(one.at[band], ref.at[band], sem.at[3 + 2 * i + k])
        for i, band in enumerate(bands)
        for k, (one, ref) in enumerate(((m_in, m), (v_in, v)))
    ]
    for get in gets:
        get.start()
    for get in gets[:3]:
        get.wait()
    puts = []
    if h_out is not None:
        share = h_out.shape[1]
        at = pl.multiple_of(lax.axis_index("shard") * share, share)
        puts.append(pltpu.make_async_copy(x.at[:, pl.ds(at, share)], h_out, sem.at[0]))
        puts[0].start()
    xt[...] = x[...].T
    slopes_body(x, g, w, z, s)
    puts.append(pltpu.make_async_copy(s, s_out, sem.at[1]))
    puts[-1].start()
    for i, band in enumerate(bands):
        grad[band, :] = jnp.dot(xt[band, :], s[...], preferred_element_type=F32)
        for get in gets[3 + 2 * i : 5 + 2 * i]:
            get.wait()
        update_rows(grad, w, m, v, w_new, m_new, v_new, band)
        at = 3 + 2 * n + 3 * i
        new = [
            pltpu.make_async_copy(w_new.at[band], w_out.at[band], sem.at[at]),
            pltpu.make_async_copy(m_new.at[band], mv_out.at[0, band], sem.at[at + 1]),
            pltpu.make_async_copy(v_new.at[band], mv_out.at[1, band], sem.at[at + 2]),
        ]
        for put in new:
            put.start()
        puts += new
    for put in puts:
        put.wait()


def train(inputs, grad_out, kernel, moments, out_dtype, parity=None, share=None):
    tokens, depth = inputs.shape
    width = grad_out.shape[1]
    n = len(blocks(depth, 256))
    outs = [
        jax.ShapeDtypeStruct((depth, width), BF16),
        jax.ShapeDtypeStruct((2, depth, width), out_dtype),
        jax.ShapeDtypeStruct((tokens, width), BF16),
    ]
    if share is not None:
        outs.append(jax.ShapeDtypeStruct((tokens, share), BF16))

    def body(*refs):
        x_in, g_in, w_in, *refs = refs
        given, refs = refs[: len(moments)], refs[len(moments) :]
        out, scratch = list(refs[: len(outs)]), refs[len(outs) :]
        out += [None] * (4 - len(out))
        train_kernel(parity, (x_in, g_in, w_in, given, *out, *scratch))

    return pl.pallas_call(
        body,
        out_shape=tuple(outs),
        in_specs=[ANY] * (3 + len(moments)),
        out_specs=(ANY,) * len(outs),
        scratch_shapes=[
            pltpu.VMEM((tokens, depth), BF16),
            pltpu.VMEM((depth, tokens), BF16),
            pltpu.VMEM((tokens, width), BF16),
            pltpu.VMEM((depth, width), BF16),
            pltpu.VMEM((depth, width), F32),
            pltpu.VMEM((depth, width), F32),
            pltpu.VMEM((tokens, width), F32),
            pltpu.VMEM((tokens, width), BF16),
            pltpu.VMEM((depth, width), F32),
            pltpu.VMEM((depth, width), BF16),
            pltpu.VMEM((depth, width), out_dtype),
            pltpu.VMEM((depth, width), out_dtype),
            pltpu.SemaphoreType.DMA((3 + 5 * n,)),
        ],
        compiler_params=pltpu.CompilerParams(vmem_limit_bytes=60 * MIB),
        cost_estimate=pl.CostEstimate(
            flops=4 * tokens * depth * width, bytes_accessed=16 * depth * width, transcendentals=0
        ),
    )(inputs, grad_out, kernel, *moments)


def part_kernel(shift, n, several, *refs):
    slopes, (w_in, *arrived, out) = refs[:several], refs[several:]
    owner = lax.rem(lax.axis_index("shard") + shift, n)
    rows = slopes[0].shape[0] // n
    at = pl.ds(pl.multiple_of(owner * rows, rows), rows)
    for parity, s_in in enumerate(slopes):

        def body(s_in=s_in):
            total = lax.dot_general(s_in[at, :], w_in[...], (((1,), (1,)), ((), ())), preferred_element_type=F32)
            for piece in arrived:
                total = total + piece[...].astype(F32)
            out[...] = total.astype(BF16)

        only_if(None if several == 1 else lax.rem(lax.axis_index("blk"), 2) == parity, body)


def part(slopes, kernel, shift, arrived=()):
    n = lax.axis_size("shard")
    rows, depth = slopes[0].shape[0] // n, kernel.shape[0]
    return pl.pallas_call(
        functools.partial(part_kernel, shift, n, len(slopes)),
        out_shape=jax.ShapeDtypeStruct((rows, depth), BF16),
        compiler_params=pltpu.CompilerParams(vmem_limit_bytes=16 * MIB),
        cost_estimate=pl.CostEstimate(flops=2 * rows * kernel.size, bytes_accessed=2 * kernel.size, transcendentals=0),
        name="part",
    )(*slopes, kernel, *arrived)


def from_one_of(chosen, dst, sem):
    for condition, src in chosen:
        pl.when(condition)(lambda src=src: pltpu.make_async_copy(src, dst, sem).start())
    return pltpu.make_async_copy(chosen[0][1], dst, sem)


def sources():
    n = lax.axis_size("blk")
    return lax.rem(lax.axis_index("blk") + (n - HOPS % n), n)


def forward_kernel(shards, *refs):
    halves, (g_in, w_even, w_odd, s, w, xt, x, g, z, sem) = refs[:shards], refs[shards:]
    me = lax.axis_index("shard")
    share = halves[0].shape[1]
    gets = []
    for k, half in enumerate(halves):
        owner = lax.rem(me + (shards - k), shards)
        at = pl.ds(pl.multiple_of(owner * share, share), share)
        gets.append(pltpu.make_async_copy(half, x.at[:, at], sem.at[k]))
    gets.append(pltpu.make_async_copy(g_in, g, sem.at[shards]))
    for get in gets:
        get.start()
    odd = lax.rem(sources(), 2)
    gets.append(from_one_of([(odd == 0, w_even), (odd == 1, w_odd)], w, sem.at[shards + 1]))
    for get in gets:
        get.wait()
    slopes_body(x, g, w, z, s)
    xt[...] = x[...].T


def forward(halves, grad_out, even, odd):
    tokens, width = grad_out.shape
    depth = even.shape[0]
    n = len(halves)
    return pl.pallas_call(
        functools.partial(forward_kernel, n),
        out_shape=(
            jax.ShapeDtypeStruct((tokens, width), BF16),
            jax.ShapeDtypeStruct((depth, width), BF16),
            jax.ShapeDtypeStruct((depth, tokens), BF16),
        ),
        in_specs=[ANY] * (n + 3),
        out_specs=(WHOLE,) * 3,
        scratch_shapes=[
            pltpu.VMEM((tokens, depth), BF16),
            pltpu.VMEM((tokens, width), BF16),
            pltpu.VMEM((tokens, width), F32),
            pltpu.SemaphoreType.DMA((n + 2,)),
        ],
        compiler_params=pltpu.CompilerParams(vmem_limit_bytes=16 * MIB),
        cost_estimate=pl.CostEstimate(
            flops=2 * tokens * depth * width, bytes_accessed=4 * depth * width, transcendentals=0
        ),
        name="forward",
    )(*halves, grad_out, even, odd)


def gradient_kernel(xt, s, grad):
    grad[...] = jnp.dot(xt[...], s[...], preferred_element_type=F32)


def gradient(transposed, slopes):
    depth, tokens = transposed.shape
    width = slopes.shape[1]
    return pl.pallas_call(
        gradient_kernel,
        out_shape=jax.ShapeDtypeStruct((depth, width), F32),
        compiler_params=pltpu.CompilerParams(vmem_limit_bytes=16 * MIB),
        cost_estimate=pl.CostEstimate(
            flops=2 * tokens * depth * width, bytes_accessed=4 * depth * width, transcendentals=0
        ),
        name="gradient",
    )(transposed, slopes)


def finish_kernel(detour, grad, w, mv_even, mv_odd, *rest):
    mv_detour, rest = (rest[0], rest[1:]) if detour else (None, rest)
    *returned, w_out, m_out, v_out, r_out, m, v, w_new, m_new, v_new, sem = rest
    bands = blocks(w.shape[0], 256)
    origin = sources()
    chosen = [(lax.rem(origin, 2) == 1, mv_odd)]
    if detour:
        chosen += [(lax.rem(origin, 4) == 0, mv_even), (lax.rem(origin, 4) == 2, mv_detour)]
    else:
        chosen += [(lax.rem(origin, 2) == 0, mv_even)]
    gets = [
        [
            from_one_of([(when, mv.at[k, band]) for when, mv in chosen], ref.at[band], sem.at[5 * i + k])
            for k, ref in enumerate((m, v))
        ]
        for i, band in enumerate(bands)
    ]
    puts = [
        pltpu.make_async_copy(one, r_out.at[i], sem.at[5 * len(bands) + i]) for i, one in enumerate(returned)
    ]
    for put in puts:
        put.start()
    for i, band in enumerate(bands):
        for get in gets[i]:
            get.wait()
        update_rows(grad, w, m, v, w_new, m_new, v_new, band)
        new = [
            pltpu.make_async_copy(one.at[band], out.at[band], sem.at[5 * i + 2 + k])
            for k, (one, out) in enumerate(((w_new, w_out), (m_new, m_out), (v_new, v_out)))
        ]
        for put in new:
            put.start()
        puts += new
    for put in puts:
        put.wait()


def finish(grad, kernel, moments, returned):
    depth, width = kernel.shape
    rows = returned[0].shape
    n = len(blocks(depth, 256))
    return pl.pallas_call(
        functools.partial(finish_kernel, len(moments) == 3),
        out_shape=(
            jax.ShapeDtypeStruct((depth, width), BF16),
            jax.ShapeDtypeStruct((depth, width), F32),
            jax.ShapeDtypeStruct((depth, width), F32),
            jax.ShapeDtypeStruct((len(returned),) + rows, BF16),
        ),
        in_specs=[WHOLE] * 2 + [ANY] * len(moments) + [WHOLE] * len(returned),
        out_specs=(ANY,) * 4,
        scratch_shapes=[
            pltpu.VMEM((depth, width), BF16),
            pltpu.VMEM((depth, width), BF16),
            pltpu.VMEM((depth, width), BF16),
            pltpu.VMEM((depth, width), F32),
            pltpu.VMEM((depth, width), F32),
            pltpu.SemaphoreType.DMA((5 * n + len(returned),)),
        ],
        compiler_params=pltpu.CompilerParams(vmem_limit_bytes=24 * MIB),
        cost_estimate=pl.CostEstimate(flops=30 * depth * width, bytes_accessed=16 * depth * width, transcendentals=0),
        name="finish",
    )(grad, kernel, *moments, *returned)


def shards(cut_acts, upstream, weights, moment_one, moment_two):
    kernel, first, second = weights[0], moment_one[0], moment_two[0]
    n, m = lax.axis_size("blk"), lax.axis_size("shard")
    evens, odds = range(0, n, 2), range(1, n, 2)
    to_far, to_near = {(i + 1) % n: i for i in odds}, {(i + 1) % n: i for i in evens}
    far = routed(cut_acts, to_far), routed(upstream, to_far)
    near = routed(cut_acts, to_near), routed(upstream, to_near)

    share = cut_acts.shape[1] // m
    kernel1, moments1, slopes0, half = train(cut_acts, upstream, kernel, (first, second), F32, share=share)
    half = passed_along(half, "blk", 1)
    grad_before = passed_along(upstream, "blk", 1)

    even_w, even_mv, slopes_even = train(*near, kernel1, (moments1,), BF16, parity=0)
    even_w = routed(even_w, {i: (i + HOPS) % n for i in evens})
    detour = n % 4 == 0
    even_mv = routed(even_mv, {i: i - 1 if detour and i % 4 == 2 else (i + HOPS) % n for i in evens})

    odd_w, odd_mv, slopes_odd = train(*far, kernel1, (moments1,), BF16, parity=1)
    odd_w = routed(odd_w, {i: (i + HOPS) % n for i in odds})
    odd_mv = routed(odd_mv, {i: (i + HOPS) % n for i in odds})

    def summed(slopes, kernel):
        parts = [part(slopes, kernel, k) for k in range(1, m)]
        parts = [passed_along(one, "shard", k + 1) for k, one in enumerate(parts)]
        return part(slopes, kernel, 0, parts)

    home = summed([slopes0], kernel)
    back = summed([slopes_even, slopes_odd], kernel1)
    back = passed_along(back, "blk", 1)

    halves = [half] + [passed_along(half, "shard", k) for k in range(1, m)]
    slopes2, moved, transposed = forward(halves, grad_before, even_w, odd_w)
    last = summed([slopes2], moved)
    last = passed_along(last, "blk", -1)
    grad2 = gradient(transposed, slopes2)
    moments = (even_mv, odd_mv)
    if detour:
        moments += (routed(even_mv, {i: (i + 1 + HOPS) % n for i in range(1, n, 4)}),)
    kernel3, first3, second3, returned = finish(grad2, moved, moments, (home, back, last))
    return (kernel3[None], first3[None], second3[None], returned)


def solution(mesh):
    placed = (
        P("blk", None),
        P("blk", "shard"),
        P("blk", None, "shard"),
        P("blk", None, "shard"),
        P("blk", None, "shard"),
    )
    return jax.shard_map(
        shards,
        mesh=mesh,
        in_specs=placed,
        out_specs=(
            P("blk", None, "shard"),
            P("blk", None, "shard"),
            P("blk", None, "shard"),
            P(None, ("blk", "shard"), None),
        ),
        check_vma=False,
    )
```

time: 233 us -> 151 us (0.65)
  the two profiles are of different devices: /device:TPU:0 before, /device:TPU:1 now
where the time goes in v2:
time: 151 us; the launch traced here: 150 us
  waiting for transfers between devices  96.5 us (64%)
  starting transfers between devices  28.5 us (19%)
  Pallas kernels  22.1 us (15%)
  local copies, waits for them, and re-layouts  2.18 us (1%)
    ppermute x9, waiting for transfers between devices, routed(): lax.ppermute(one, 'blk', sorted(route.items()))  71.6 us
    ppermute x8, waiting for transfers between devices, passed_along(): lax.ppermute(part, axis, [(i, (i + by) % devices) for i in range(devices)])  25 us
    ppermute x9, starting transfers between devices, routed(): lax.ppermute(one, 'blk', sorted(route.items()))  14.5 us
    ppermute x8, starting transfers between devices, passed_along(): lax.ppermute(part, axis, [(i, (i + by) % devices) for i in range(devices)])  14 us
    pallas_call x3, Pallas kernels, train(): pl.pallas_call(body, out_shape=tuple(outs), in_specs=[ANY] * (3 + len(mom...  12.9 us
    pallas_call x1, Pallas kernels, finish(): pl.pallas_call(functools.partial(finish_kernel, len(moments) == 3), out_s...  3.21 us
  transfers between devices with their start and end apart: 17, of which 7 were waited for; matrix products, arithmetic and copies ran while one was open for 0% of the time, Pallas kernels for 12%

profile of v2, /device:TPU:1, one launch (start us, length us, event | category | flops | bytes accessed | tf_op | source)
XLA Modules:
  0.0 150.3 jit_solution(2430213998262540168)
XLA Ops:
  0.6 2.0 %collective-permute-start.3 = (bf16[512,1024]{1,0:T(8,128)(2,1)}, bf16[512,1024]{1,0:T(8,128)(2,1)S(1)}, u32[]{:S(2)}, u32[]{:S(2)}) collective-permute-start(bf16[512,1024]{1,0:T(8,128)(2,1)} %refs_0_.1), channel_id=1, source_target_pairs={{2,0},{6,4},{10,8},{14,12},{18,16},{22,20},{26,24},{30,28},{3,1},{... | collective-permute-start | bytes 3145736 | tf_op jit(solution)/shard_map/ppermute | solution.py:24
  2.6 1.3 collective-permute-start.4
  4.0 6.5 %shard_map.84 = (bf16[1024,512]{1,0:T(8,128)(2,1)}, f32[2,1024,512]{2,1,0:T(8,128)}, bf16[512,512]{1,0:T(8,128)(2,1)}, bf16[512,512]{1,0:T(8,128)(2,1)}) custom-call(bf16[512,1024]{1,0:T(8,128)(2,1)} %refs_0_.1, bf16[512,512]{1,0:T(8,128)(2,1)} %refs_1_.1, bf16[1024,512]{1,0:T(8,128)(2,1)} %bitcast.6, f32[1024,512]{1,0:T(8,128)} %bitcast.9, f32[1024,512]{1,0:T(8,128)} %bitcast.10), custom_call_target="tpu_custom_call" | custom-call | flops 1073741824 | bytes 8388608 | tf_op jit(solution)/shard_map/pallas_call | solution.py:136
  10.5 0.8 copy-done.7
  11.8 1.3 collective-permute-start.9
  13.1 1.3 collective-permute-start.6
  14.4 1.3 collective-permute-start.7
  15.7 9.8 %collective-permute-start.2 = (bf16[512,512]{1,0:T(8,128)(2,1)}, bf16[512,512]{1,0:T(8,128)(2,1)}, u32[]{:S(2)}, u32[]{:S(2)}) collective-permute-start(bf16[512,512]{1,0:T(8,128)(2,1)} %refs_1_.1), channel_id=1, source_target_pairs={{0,2},{2,4},{4,6},{6,8},{8,10},{10,12},{12,14},{14,16},{16,18},{18... | collective-permute-start | bytes 1572872 | tf_op jit(solution)/shard_map/ppermute | solution.py:20
  25.6 47.6 %collective-permute-done.7.refs_1_ = bf16[512,512]{1,0:T(8,128)(2,1)} collective-permute-done((bf16[512,512]{1,0:T(8,128)(2,1)}, bf16[512,512]{1,0:T(8,128)(2,1)}, u32[]{:S(2)}, u32[]{:S(2)}) %collective-permute-start.7) | collective-permute-done | bytes 524320 | tf_op jit(solution)/shard_map/ppermute | solution.py:24
  73.1 6.3 %shard_map.86 = (bf16[1024,512]{1,0:T(8,128)(2,1)}, bf16[2,1024,512]{2,1,0:T(8,128)(2,1)}, bf16[512,512]{1,0:T(8,128)(2,1)}) custom-call(bf16[512,1024]{1,0:T(8,128)(2,1)} %collective-permute-done.6.refs_0_, bf16[512,512]{1,0:T(8,128)(2,1)} %collective-permute-done.7.refs_1_, bf16[1024,512]{1,0:T(8,128)(2,1)} %get-tuple-element.22.refs_2_, ...), custom_call_target="tpu_custom_call" | custom-call | flops 1073741824 | bytes 8388608 | tf_op jit(solution)/shard_map/pallas_call | solution.py:136
  79.4 1.4 collective-permute-start.8
  80.8 1.3 collective-permute-start.5
  82.1 1.4 collective-permute-start.10
  83.5 3.2 %collective-permute-start.11 = (bf16[2,1024,512]{2,1,0:T(8,128)(2,1)S(1)}, bf16[2,1024,512]{2,1,0:T(8,128)(2,1)S(1)}, u32[]{:S(2)}, u32[]{:S(2)}) collective-permute-start(bf16[2,1024,512]{2,1,0:T(8,128)(2,1)S(1)} %collective-permute-done.9.mv_even), channel_id=1, source_target_pairs={{2,10},{10,18},{18,26},{26,2},{3,11},{11,19},{19,27},{27,3}} | collective-permute-start | bytes 6291464 | tf_op jit(solution)/shard_map/ppermute | solution.py:24
  86.7 1.3 collective-permute-start.1
  88.0 1.0 copy-done.4
  89.1 0.5 part.8
  89.6 7.8 %collective-permute-done.1.refs_1_ = bf16[512,512]{1,0:T(8,128)(2,1)S(1)} collective-permute-done((bf16[512,512]{1,0:T(8,128)(2,1)}, bf16[512,512]{1,0:T(8,128)(2,1)S(1)}, u32[]{:S(2)}, u32[]{:S(2)}) %collective-permute-start.1) | collective-permute-done | bytes 524320 | tf_op jit(solution)/shard_map/ppermute | solution.py:20
  97.4 1.2 collective-permute-start.13
  98.6 12.4 %collective-permute-done.5.refs_3_ = bf16[1024,512]{1,0:T(8,128)(2,1)S(1)} collective-permute-done((bf16[1024,512]{1,0:T(8,128)(2,1)}, bf16[1024,512]{1,0:T(8,128)(2,1)S(1)}, u32[]{:S(2)}, u32[]{:S(2)}) %collective-permute-start.5) | collective-permute-done | bytes 1048608 | tf_op jit(solution)/shard_map/ppermute | solution.py:24
  111.0 2.4 %forward.1 = (bf16[512,512]{1,0:T(8,128)(2,1)S(1)}, bf16[1024,512]{1,0:T(8,128)(2,1)S(1)}, bf16[1024,512]{1,0:T(8,128)(2,1)S(1)}) custom-call(bf16[512,512]{1,0:T(8,128)(2,1)} %collective-permute-done.refs_0_, bf16[512,512]{1,0:T(8,128)(2,1)S(1)} %collective-permute-done.1.refs_1_, bf16[512,512]{1,0:T(8,128)(2,1)} %collective-permute-done.2.refs_2_, ...), custom_call_target="tpu_custom_call" | custom-call | flops 536870912 | bytes 2097152 | tf_op jit(solution)/shard_map/forward/pallas_call | solution.py:226
  113.5 0.5 part.10
  113.9 1.3 collective-permute-start.15
  116.0 0.5 part.9
  116.6 6.9 %collective-permute-done.15.refs_2_ = bf16[256,1024]{1,0:T(8,128)(2,1)S(1)} collective-permute-done((bf16[256,1024]{1,0:T(8,128)(2,1)S(1)}, bf16[256,1024]{1,0:T(8,128)(2,1)S(1)}, u32[]{:S(2)}, u32[]{:S(2)}) %collective-permute-start.15) | collective-permute-done | bytes 524320 | tf_op jit(solution)/shard_map/ppermute | solution.py:20
  123.5 0.5 part.11
  124.0 5.4 %collective-permute-done.12.refs_2_ = bf16[256,1024]{1,0:T(8,128)(2,1)S(1)} collective-permute-done((bf16[256,1024]{1,0:T(8,128)(2,1)S(1)}, bf16[256,1024]{1,0:T(8,128)(2,1)S(1)}, u32[]{:S(2)}, u32[]{:S(2)}) %collective-permute-start.12) | collective-permute-done | bytes 524320 | tf_op jit(solution)/shard_map/ppermute | solution.py:20
  129.4 0.5 part.7.rest_1_
  129.8 0.7 gradient.1.grad
  130.6 4.8 %collective-permute-done.16.rest_3_ = bf16[256,1024]{1,0:T(8,128)(2,1)S(1)} collective-permute-done((bf16[256,1024]{1,0:T(8,128)(2,1)S(1)}, bf16[256,1024]{1,0:T(8,128)(2,1)S(1)}, u32[]{:S(2)}, u32[]{:S(2)}) %collective-permute-start.16) | collective-permute-done | bytes 524320 | tf_op jit(solution)/shard_map/ppermute | solution.py:20
  135.4 11.6 %collective-permute-done.11.rest_0_ = bf16[2,1024,512]{2,1,0:T(8,128)(2,1)S(1)} collective-permute-done((bf16[2,1024,512]{2,1,0:T(8,128)(2,1)S(1)}, bf16[2,1024,512]{2,1,0:T(8,128)(2,1)S(1)}, u32[]{:S(2)}, u32[]{:S(2)}) %collective-permute-start.11) | collective-permute-done | bytes 2097184 | tf_op jit(solution)/shard_map/ppermute | solution.py:24
  147.0 3.2 %finish.1 = (bf16[1024,512]{1,0:T(8,128)(2,1)}, f32[1024,512]{1,0:T(8,128)}, f32[1024,512]{1,0:T(8,128)}, bf16[3,256,1024]{2,1,0:T(8,128)(2,1)}) custom-call(f32[1024,512]{1,0:T(8,128)S(1)} %gradient.1.grad, bf16[1024,512]{1,0:T(8,128)(2,1)S(1)} %get-tuple-element.28.refs_1_.w, bf16[2,1024,512]{2,1,0:T(8,128)(2,1)S(1)} %collective-permute-done.9.mv_even, ...), custom_call_target="tpu_custom_call" | custom-call | flops 15728640 | bytes 8388608 | tf_op jit(solution)/shard_map/finish/pallas_call | solution.py:308
  (30 shorter events, 1.5 us)
Async XLA Ops:
  0.6 9.8 %collective-permute-start.3 = (bf16[512,1024]{1,0:T(8,128)(2,1)}, bf16[512,1024]{1,0:T(8,128)(2,1)S(1)}, u32[]{:S(2)}, u32[]{:S(2)}) collective-permute-start(bf16[512,1024]{1,0:T(8,128)(2,1)} %refs_0_.1), channel_id=1, source_target_pairs={{2,0},{6,4},{10,8},{14,12},{18,16},{22,20},{26,24},{30,28},{3,1},{... | collective-permute-start | bytes 3145736 | tf_op jit(solution)/shard_map/ppermute | solution.py:24
  2.6 7.8 %collective-permute-start.4 = (bf16[512,512]{1,0:T(8,128)(2,1)}, bf16[512,512]{1,0:T(8,128)(2,1)S(1)}, u32[]{:S(2)}, u32[]{:S(2)}) collective-permute-start(bf16[512,512]{1,0:T(8,128)(2,1)} %refs_1_.1), channel_id=1, source_target_pairs={{2,0},{6,4},{10,8},{14,12},{18,16},{22,20},{26,24},{30,28},{3,1},{... | collective-permute-start | bytes 1572872 | tf_op jit(solution)/shard_map/ppermute | solution.py:24
  10.5 0.8 copy-start.7
  10.5 1.1 copy-start.6
  11.8 71.7 %collective-permute-start.9 = (bf16[2,1024,512]{2,1,0:T(8,128)(2,1)}, bf16[2,1024,512]{2,1,0:T(8,128)(2,1)S(1)}, u32[]{:S(2)}, u32[]{:S(2)}) collective-permute-start(bf16[2,1024,512]{2,1,0:T(8,128)(2,1)} %get-tuple-element.29), channel_id=1, source_target_pairs={{0,6},{4,2},{8,14},{12,10},{16,22},{20,18},{24,30},{28,26},{1,7},{... | collective-permute-start | bytes 6291464 | tf_op jit(solution)/shard_map/ppermute | solution.py:24
  13.1 60.0 %collective-permute-start.6 = (bf16[512,1024]{1,0:T(8,128)(2,1)}, bf16[512,1024]{1,0:T(8,128)(2,1)}, u32[]{:S(2)}, u32[]{:S(2)}) collective-permute-start(bf16[512,1024]{1,0:T(8,128)(2,1)} %refs_0_.1), channel_id=1, source_target_pairs={{0,30},{4,2},{8,6},{12,10},{16,14},{20,18},{24,22},{28,26},{1,31},... | collective-permute-start | bytes 3145736 | tf_op jit(solution)/shard_map/ppermute | solution.py:24
  14.4 58.7 %collective-permute-start.7 = (bf16[512,512]{1,0:T(8,128)(2,1)}, bf16[512,512]{1,0:T(8,128)(2,1)}, u32[]{:S(2)}, u32[]{:S(2)}) collective-permute-start(bf16[512,512]{1,0:T(8,128)(2,1)} %refs_1_.1), channel_id=1, source_target_pairs={{0,30},{4,2},{8,6},{12,10},{16,14},{20,18},{24,22},{28,26},{1,31},... | collective-permute-start | bytes 1572872 | tf_op jit(solution)/shard_map/ppermute | solution.py:24
  15.7 66.4 %collective-permute-start.2 = (bf16[512,512]{1,0:T(8,128)(2,1)}, bf16[512,512]{1,0:T(8,128)(2,1)}, u32[]{:S(2)}, u32[]{:S(2)}) collective-permute-start(bf16[512,512]{1,0:T(8,128)(2,1)} %refs_1_.1), channel_id=1, source_target_pairs={{0,2},{2,4},{4,6},{6,8},{8,10},{10,12},{12,14},{14,16},{16,18},{18... | collective-permute-start | bytes 1572872 | tf_op jit(solution)/shard_map/ppermute | solution.py:20
  25.5 62.5 %copy-start = (bf16[1024,512]{1,0:T(8,128)(2,1)S(1)}, bf16[1024,512]{1,0:T(8,128)(2,1)}, u32[]{:S(2)}) copy-start(bf16[1024,512]{1,0:T(8,128)(2,1)} %get-tuple-element.22.refs_2_) | copy-start | bytes 3145732
  25.5 62.5 %copy-start.3 = (bf16[512,512]{1,0:T(8,128)(2,1)S(1)}, bf16[512,512]{1,0:T(8,128)(2,1)}, u32[]{:S(2)}) copy-start(bf16[512,512]{1,0:T(8,128)(2,1)} %get-tuple-element.32.refs_0_) | copy-start | bytes 1572868
  25.5 61.2 %collective-permute-start = (bf16[512,512]{1,0:T(8,128)(2,1)}, bf16[512,512]{1,0:T(8,128)(2,1)}, u32[]{:S(2)}, u32[]{:S(2)}) collective-permute-start(bf16[512,512]{1,0:T(8,128)(2,1)} %get-tuple-element.21), channel_id=1, source_target_pairs={{0,2},{2,4},{4,6},{6,8},{8,10},{10,12},{12,14},{14,16},{16,18},{18... | collective-permute-start | bytes 1572872 | tf_op jit(solution)/shard_map/ppermute | solution.py:20
  79.4 19.2 %collective-permute-start.8 = (bf16[1024,512]{1,0:T(8,128)(2,1)}, bf16[1024,512]{1,0:T(8,128)(2,1)S(1)}, u32[]{:S(2)}, u32[]{:S(2)}) collective-permute-start(bf16[1024,512]{1,0:T(8,128)(2,1)} %get-tuple-element.25), channel_id=1, source_target_pairs={{2,8},{6,12},{10,16},{14,20},{18,24},{22,28},{26,0},{30,4},{3,9},{... | collective-permute-start | bytes 3145736 | tf_op jit(solution)/shard_map/ppermute | solution.py:24
  80.8 30.3 %collective-permute-start.5 = (bf16[1024,512]{1,0:T(8,128)(2,1)}, bf16[1024,512]{1,0:T(8,128)(2,1)S(1)}, u32[]{:S(2)}, u32[]{:S(2)}) collective-permute-start(bf16[1024,512]{1,0:T(8,128)(2,1)} %get-tuple-element.24), channel_id=1, source_target_pairs={{0,6},{4,10},{8,14},{12,18},{16,22},{20,26},{24,30},{28,2},{1,7},{... | collective-permute-start | bytes 3145736 | tf_op jit(solution)/shard_map/ppermute | solution.py:24
  82.1 48.5 %collective-permute-start.10 = (bf16[2,1024,512]{2,1,0:T(8,128)(2,1)}, bf16[2,1024,512]{2,1,0:T(8,128)(2,1)S(1)}, u32[]{:S(2)}, u32[]{:S(2)}) collective-permute-start(bf16[2,1024,512]{2,1,0:T(8,128)(2,1)} %get-tuple-element.30), channel_id=1, source_target_pairs={{2,8},{6,12},{10,16},{14,20},{18,24},{22,28},{26,0},{30,4},{3,9},{... | collective-permute-start | bytes 6291464 | tf_op jit(solution)/shard_map/ppermute | solution.py:24
  83.5 63.4 %collective-permute-start.11 = (bf16[2,1024,512]{2,1,0:T(8,128)(2,1)S(1)}, bf16[2,1024,512]{2,1,0:T(8,128)(2,1)S(1)}, u32[]{:S(2)}, u32[]{:S(2)}) collective-permute-start(bf16[2,1024,512]{2,1,0:T(8,128)(2,1)S(1)} %collective-permute-done.9.mv_even), channel_id=1, source_target_pairs={{2,10},{10,18},{18,26},{26,2},{3,11},{11,19},{19,27},{27,3}} | collective-permute-start | bytes 6291464 | tf_op jit(solution)/shard_map/ppermute | solution.py:24
  86.7 10.7 %collective-permute-start.1 = (bf16[512,512]{1,0:T(8,128)(2,1)}, bf16[512,512]{1,0:T(8,128)(2,1)S(1)}, u32[]{:S(2)}, u32[]{:S(2)}) collective-permute-start(bf16[512,512]{1,0:T(8,128)(2,1)} %collective-permute-done.refs_0_), channel_id=1, source_target_pairs={{0,1},{1,0},{2,3},{3,2},{4,5},{5,4},{6,7},{7,6},{8,9},{9,8},{10,11... | collective-permute-start | bytes 1572872 | tf_op jit(solution)/shard_map/ppermute | solution.py:20
  88.0 1.0 copy-start.4
  89.6 25.7 %copy-start.1 = (bf16[1,1024,512]{2,1,0:T(8,128)(2,1)S(1)}, bf16[1,1024,512]{2,1,0:T(8,128)(2,1)}, u32[]{:S(2)}) copy-start(bf16[1,1024,512]{2,1,0:T(8,128)(2,1)} %param.7) | copy-start | bytes 3145732
  89.6 25.6 %copy-start.2 = (bf16[512,512]{1,0:T(8,128)(2,1)S(1)}, bf16[512,512]{1,0:T(8,128)(2,1)}, u32[]{:S(2)}) copy-start(bf16[512,512]{1,0:T(8,128)(2,1)} %get-tuple-element.31.refs_0_) | copy-start | bytes 1572868
  97.4 18.6 %collective-permute-start.13 = (bf16[256,1024]{1,0:T(8,128)(2,1)S(1)}, bf16[256,1024]{1,0:T(8,128)(2,1)S(1)}, u32[]{:S(2)}, u32[]{:S(2)}) collective-permute-start(bf16[256,1024]{1,0:T(8,128)(2,1)S(1)} %part.8), channel_id=1, source_target_pairs={{0,1},{1,0},{2,3},{3,2},{4,5},{5,4},{6,7},{7,6},{8,9},{9,8},{10,11... | collective-permute-start | bytes 1572872 | tf_op jit(solution)/shard_map/ppermute | solution.py:20
  113.4 2.6 %copy-start.5 = (bf16[512,512]{1,0:T(8,128)(2,1)S(1)}, bf16[512,512]{1,0:T(8,128)(2,1)}, u32[]{:S(2)}) copy-start(bf16[512,512]{1,0:T(8,128)(2,1)} %get-tuple-element.33.refs_1_) | copy-start | bytes 1572868
  113.9 9.5 %collective-permute-start.15 = (bf16[256,1024]{1,0:T(8,128)(2,1)S(1)}, bf16[256,1024]{1,0:T(8,128)(2,1)S(1)}, u32[]{:S(2)}, u32[]{:S(2)}) collective-permute-start(bf16[256,1024]{1,0:T(8,128)(2,1)S(1)} %part.10), channel_id=1, source_target_pairs={{0,1},{1,0},{2,3},{3,2},{4,5},{5,4},{6,7},{7,6},{8,9},{9,8},{10,11... | collective-permute-start | bytes 1572872 | tf_op jit(solution)/shard_map/ppermute | solution.py:20
  115.7 13.7 %collective-permute-start.12 = (bf16[256,1024]{1,0:T(8,128)(2,1)S(1)}, bf16[256,1024]{1,0:T(8,128)(2,1)S(1)}, u32[]{:S(2)}, u32[]{:S(2)}) collective-permute-start(bf16[256,1024]{1,0:T(8,128)(2,1)S(1)} %part.6), channel_id=1, source_target_pairs={{0,1},{1,0},{2,3},{3,2},{4,5},{5,4},{6,7},{7,6},{8,9},{9,8},{10,11... | collective-permute-start | bytes 1572872 | tf_op jit(solution)/shard_map/ppermute | solution.py:20
  116.5 14.1 %collective-permute-start.14 = (bf16[256,1024]{1,0:T(8,128)(2,1)S(1)}, bf16[256,1024]{1,0:T(8,128)(2,1)S(1)}, u32[]{:S(2)}, u32[]{:S(2)}) collective-permute-start(bf16[256,1024]{1,0:T(8,128)(2,1)S(1)} %part.9), channel_id=1, source_target_pairs={{0,2},{2,4},{4,6},{6,8},{8,10},{10,12},{12,14},{14,16},{16,18},{18... | collective-permute-start | bytes 1572872 | tf_op jit(solution)/shard_map/ppermute | solution.py:20
  123.9 11.5 %collective-permute-start.16 = (bf16[256,1024]{1,0:T(8,128)(2,1)S(1)}, bf16[256,1024]{1,0:T(8,128)(2,1)S(1)}, u32[]{:S(2)}, u32[]{:S(2)}) collective-permute-start(bf16[256,1024]{1,0:T(8,128)(2,1)S(1)} %part.11), channel_id=1, source_target_pairs={{0,30},{2,0},{4,2},{6,4},{8,6},{10,8},{12,10},{14,12},{16,14},{18,... | collective-permute-start | bytes 1572872 | tf_op jit(solution)/shard_map/ppermute | solution.py:20

commit v3 on v2

v3 whole, which is shorter than its diff:
```python
import functools

import jax
import jax.numpy as jnp
from jax import lax
from jax.experimental import pallas as pl
from jax.experimental.pallas import tpu as pltpu
from jax.sharding import PartitionSpec as P


HOPS = 3
F32, BF16 = jnp.float32, jnp.bfloat16
ANY = pl.BlockSpec(memory_space=pl.ANY)
WHOLE = pl.BlockSpec(memory_space=pltpu.VMEM)
MIB = 1024 * 1024


def passed_along(part, axis, by):
    devices = lax.axis_size(axis)
    return lax.ppermute(part, axis, [(i, (i + by) % devices) for i in range(devices)])


def routed(part, route):
    return jax.tree.map(lambda one: lax.ppermute(one, "blk", sorted(route.items())), part)


def only_if(chosen, body):
    if chosen is None:
        body()
    else:
        pl.when(chosen)(body)


def gelu_slope(values):
    square = values * values
    tanh_part = jnp.tanh(values * (0.7978845608 + 0.7978845608 * 0.044715 * square))
    return (0.5 + 0.5 * tanh_part) + (values * (1.0 - tanh_part * tanh_part)) * (
        0.5 * 0.7978845608 + 0.5 * 0.7978845608 * 0.134145 * square
    )


def blocks(size, step):
    step = step if size % step == 0 else size
    return [pl.ds(at, step) for at in range(0, size, step)]


def slopes_body(x, g, w, z, s):
    for cols in blocks(g.shape[1], 256):
        z[:, cols] = jnp.dot(x[...], w[:, cols], preferred_element_type=F32)
        for rows in blocks(x.shape[0], 64):
            s[rows, cols] = (g[rows, cols].astype(F32) * gelu_slope(z[rows, cols])).astype(BF16)


def update_rows(grad, w, m, v, w_new, m_new, v_new, rows):
    for at in blocks(rows.size, 32):
        at = pl.ds(rows.start + at.start, at.size)
        gradient = grad[at, :]
        first = 0.9 * m[at, :].astype(F32) + 0.1 * gradient
        second = 0.95 * v[at, :].astype(F32) + 0.05 * (gradient * gradient)
        m_new[at, :] = first.astype(m_new.dtype)
        v_new[at, :] = second.astype(v_new.dtype)
        root = second * lax.rsqrt(second)
        inverse = lax.rsqrt(second + 1e-08 * (2.0 * root + 1e-08))
        w_new[at, :] = (w[at, :].astype(F32) - (0.01 * first) * inverse).astype(BF16)


def copies_of(parts, whole, sems):
    if len(parts) == 1:
        return [pltpu.make_async_copy(parts[0], whole, sems[0])]
    shards = len(parts)
    me = lax.axis_index("shard")
    share = parts[0].shape[1]
    copies = []
    for k, one in enumerate(parts):
        owner = lax.rem(me + (shards - k), shards)
        at = pl.ds(pl.multiple_of(owner * share, share), share)
        copies.append(pltpu.make_async_copy(one, whole.at[:, at], sems[k]))
    return copies


def train_body(x_in, g_in, w_in, m_in, v_in, w_out, m_out, v_out, s_out,
               x, xt, g, w, m, v, z, s, grad, w_new, m_new, v_new, sem):
    bands = blocks(w.shape[0], 256)
    n = len(bands)
    last = 3 + 5 * n
    get_x = copies_of(x_in, x, [sem.at[last + k] for k in range(len(x_in))])
    get_w, get_g = [
        pltpu.make_async_copy(one, ref, sem.at[1 + i]) for i, (one, ref) in enumerate(((w_in, w), (g_in, g)))
    ]
    gets = [
        [
            pltpu.make_async_copy(one.at[band], ref.at[band], sem.at[3 + 2 * i + k])
            for k, (one, ref) in enumerate(((m_in, m), (v_in, v)))
        ]
        for i, band in enumerate(bands)
    ]
    for get in get_x + [get_w, get_g]:
        get.start()
    for get in get_x:
        get.wait()
    for get in gets[0]:
        get.start()
    puts = []
    xt[...] = x[...].T
    get_w.wait()
    get_g.wait()
    for pair in gets[1:]:
        for get in pair:
            get.start()
    slopes_body(x, g, w, z, s)
    puts.append(pltpu.make_async_copy(s, s_out, sem.at[0]))
    puts[-1].start()
    for i, band in enumerate(bands):
        grad[band, :] = jnp.dot(xt[band, :], s[...], preferred_element_type=F32)
        for get in gets[i]:
            get.wait()
        update_rows(grad, w, m, v, w_new, m_new, v_new, band)
        new = [
            pltpu.make_async_copy(one.at[band], out.at[band], sem.at[3 + 2 * n + 3 * i + k])
            for k, (one, out) in enumerate(((w_new, w_out), (m_new, m_out), (v_new, v_out)))
        ]
        for put in new:
            put.start()
        puts += new
    for put in puts:
        put.wait()


def train(inputs, grad_out, kernel, first, second, out_dtype, parity=None):
    (tokens, width), depth = grad_out.shape, kernel.shape[0]
    k = len(inputs)
    n = len(blocks(depth, 256))
    outs = [
        jax.ShapeDtypeStruct((depth, width), BF16),
        jax.ShapeDtypeStruct((depth, width), out_dtype),
        jax.ShapeDtypeStruct((depth, width), out_dtype),
        jax.ShapeDtypeStruct((tokens, width), BF16),
    ]

    def body(*refs):
        only_if(
            None if parity is None else lax.rem(lax.axis_index("blk"), 2) == parity,
            lambda: train_body(refs[:k], *refs[k:]),
        )

    return pl.pallas_call(
        body,
        out_shape=tuple(outs),
        in_specs=[ANY] * (k + 4),
        out_specs=(ANY,) * len(outs),
        scratch_shapes=[
            pltpu.VMEM((tokens, depth), BF16),
            pltpu.VMEM((depth, tokens), BF16),
            pltpu.VMEM((tokens, width), BF16),
            pltpu.VMEM((depth, width), BF16),
            pltpu.VMEM((depth, width), F32),
            pltpu.VMEM((depth, width), F32),
            pltpu.VMEM((tokens, width), F32),
            pltpu.VMEM((tokens, width), BF16),
            pltpu.VMEM((depth, width), F32),
            pltpu.VMEM((depth, width), BF16),
            pltpu.VMEM((depth, width), out_dtype),
            pltpu.VMEM((depth, width), out_dtype),
            pltpu.SemaphoreType.DMA((3 + 5 * n + k,)),
        ],
        compiler_params=pltpu.CompilerParams(vmem_limit_bytes=(60 if parity is None else 48) * MIB),
        cost_estimate=pl.CostEstimate(
            flops=4 * tokens * depth * width, bytes_accessed=16 * depth * width, transcendentals=0
        ),
    )(*inputs, grad_out, kernel, first, second)


def part_kernel(shift, n, several, *refs):
    slopes, (w_in, *arrived, out) = refs[:several], refs[several:]
    owner = lax.rem(lax.axis_index("shard") + shift, n)
    rows = slopes[0].shape[0] // n
    at = pl.ds(pl.multiple_of(owner * rows, rows), rows)
    for parity, s_in in enumerate(slopes):

        def body(s_in=s_in):
            total = lax.dot_general(s_in[at, :], w_in[...], (((1,), (1,)), ((), ())), preferred_element_type=F32)
            for piece in arrived:
                total = total + piece[...].astype(F32)
            out[...] = total.astype(BF16)

        only_if(None if several == 1 else lax.rem(lax.axis_index("blk"), 2) == parity, body)


def part(slopes, kernel, shift, arrived=()):
    n = lax.axis_size("shard")
    rows, depth = slopes[0].shape[0] // n, kernel.shape[0]
    return pl.pallas_call(
        functools.partial(part_kernel, shift, n, len(slopes)),
        out_shape=jax.ShapeDtypeStruct((rows, depth), BF16),
        compiler_params=pltpu.CompilerParams(vmem_limit_bytes=16 * MIB),
        cost_estimate=pl.CostEstimate(flops=2 * rows * kernel.size, bytes_accessed=2 * kernel.size, transcendentals=0),
        name="part",
    )(*slopes, kernel, *arrived)


def from_one_of(chosen, dst, sem):
    for condition, src in chosen:
        pl.when(condition)(lambda src=src: pltpu.make_async_copy(src, dst, sem).start())
    return pltpu.make_async_copy(chosen[0][1], dst, sem)


def sources():
    n = lax.axis_size("blk")
    return lax.rem(lax.axis_index("blk") + (n - HOPS % n), n)


def forward_kernel(shards, *refs):
    across, (x_near, g_across, g_near, w_even, w_odd, s, w, xt, x, g, z, sem) = refs[:shards], refs[shards:]
    odd_here = lax.rem(lax.axis_index("blk"), 2) == 1
    odd_source = lax.rem(sources(), 2) == 1

    def start(copies):
        for copy in copies:
            copy.start()

    def wait(copies):
        for copy in copies:
            copy.wait()

    sems = [sem.at[k] for k in range(shards)]
    pl.when(odd_here)(lambda: start(copies_of([x_near], x, sems)))
    pl.when(jnp.logical_not(odd_here))(lambda: start(copies_of(across, x, sems)))
    gets = [
        from_one_of([(jnp.logical_not(odd_here), g_across), (odd_here, g_near)], g, sem.at[shards]),
        from_one_of([(jnp.logical_not(odd_source), w_even), (odd_source, w_odd)], w, sem.at[shards + 1]),
    ]
    pl.when(odd_here)(lambda: wait(copies_of([x_near], x, sems)))
    pl.when(jnp.logical_not(odd_here))(lambda: wait(copies_of(across, x, sems)))
    wait(gets)
    slopes_body(x, g, w, z, s)
    xt[...] = x[...].T


def forward(across, x_near, g_across, g_near, even, odd):
    (tokens, width), depth = g_near.shape, even.shape[0]
    n = len(across)
    return pl.pallas_call(
        functools.partial(forward_kernel, n),
        out_shape=(
            jax.ShapeDtypeStruct((tokens, width), BF16),
            jax.ShapeDtypeStruct((depth, width), BF16),
            jax.ShapeDtypeStruct((depth, tokens), BF16),
        ),
        in_specs=[ANY] * (n + 5),
        out_specs=(WHOLE,) * 3,
        scratch_shapes=[
            pltpu.VMEM((tokens, depth), BF16),
            pltpu.VMEM((tokens, width), BF16),
            pltpu.VMEM((tokens, width), F32),
            pltpu.SemaphoreType.DMA((n + 2,)),
        ],
        compiler_params=pltpu.CompilerParams(vmem_limit_bytes=16 * MIB),
        cost_estimate=pl.CostEstimate(
            flops=2 * tokens * depth * width, bytes_accessed=4 * depth * width, transcendentals=0
        ),
        name="forward",
    )(*across, x_near, g_across, g_near, even, odd)


def gradient_kernel(xt, s, grad):
    grad[...] = jnp.dot(xt[...], s[...], preferred_element_type=F32)


def gradient(transposed, slopes):
    depth, tokens = transposed.shape
    width = slopes.shape[1]
    return pl.pallas_call(
        gradient_kernel,
        out_shape=jax.ShapeDtypeStruct((depth, width), F32),
        compiler_params=pltpu.CompilerParams(vmem_limit_bytes=16 * MIB),
        cost_estimate=pl.CostEstimate(
            flops=2 * tokens * depth * width, bytes_accessed=4 * depth * width, transcendentals=0
        ),
        name="gradient",
    )(transposed, slopes)


def finish_kernel(shards, moments, grad, w, *refs):
    given, refs = refs[:moments], refs[moments:]
    home, back, refs = refs[0], refs[1], refs[2:]
    last, (w_out, m_out, v_out, r_out, m, v, w_new, m_new, v_new, r, sem) = refs[:shards], refs[shards:]
    m_even, v_even, m_odd, v_odd, *m_detour = given
    bands = blocks(w.shape[0], 256)
    n = len(bands)
    origin = sources()
    even, odd = lax.rem(origin, 2) == 0, lax.rem(origin, 2) == 1
    m_from, v_from = [(odd, m_odd)], [(even, v_even), (odd, v_odd)]
    if m_detour:
        m_from += [(lax.rem(origin, 4) == 0, m_even), (lax.rem(origin, 4) == 2, m_detour[0])]
    else:
        m_from += [(even, m_even)]
    gets = [
        [
            from_one_of([(when, one.at[band]) for when, one in chosen], ref.at[band], sem.at[5 * i + k])
            for k, (chosen, ref) in enumerate(((m_from, m), (v_from, v)))
        ]
        for i, band in enumerate(bands)
    ]
    total = last[0][...].astype(F32)
    for piece in last[1:]:
        total = total + piece[...].astype(F32)
    r[...] = total.astype(BF16)
    puts = [
        pltpu.make_async_copy(one, r_out.at[i], sem.at[5 * n + i]) for i, one in enumerate((home, back, r))
    ]
    for put in puts:
        put.start()
    for i, band in enumerate(bands):
        for get in gets[i]:
            get.wait()
        update_rows(grad, w, m, v, w_new, m_new, v_new, band)
        new = [
            pltpu.make_async_copy(one.at[band], out.at[band], sem.at[5 * i + 2 + k])
            for k, (one, out) in enumerate(((w_new, w_out), (m_new, m_out), (v_new, v_out)))
        ]
        for put in new:
            put.start()
        puts += new
    for put in puts:
        put.wait()


def finish(grad, kernel, moments, home, back, last):
    depth, width = kernel.shape
    rows = home.shape
    n = len(blocks(depth, 256))
    return pl.pallas_call(
        functools.partial(finish_kernel, len(last), len(moments)),
        out_shape=(
            jax.ShapeDtypeStruct((depth, width), BF16),
            jax.ShapeDtypeStruct((depth, width), F32),
            jax.ShapeDtypeStruct((depth, width), F32),
            jax.ShapeDtypeStruct((HOPS,) + rows, BF16),
        ),
        in_specs=[WHOLE] * 2 + [ANY] * len(moments) + [WHOLE] * (2 + len(last)),
        out_specs=(ANY,) * 4,
        scratch_shapes=[
            pltpu.VMEM((depth, width), BF16),
            pltpu.VMEM((depth, width), BF16),
            pltpu.VMEM((depth, width), BF16),
            pltpu.VMEM((depth, width), F32),
            pltpu.VMEM((depth, width), F32),
            pltpu.VMEM(rows, BF16),
            pltpu.SemaphoreType.DMA((5 * n + HOPS,)),
        ],
        compiler_params=pltpu.CompilerParams(vmem_limit_bytes=24 * MIB),
        cost_estimate=pl.CostEstimate(flops=30 * depth * width, bytes_accessed=16 * depth * width, transcendentals=0),
        name="finish",
    )(grad, kernel, *moments, home, back, *last)


def shards(cut_acts, upstream, weights, moment_one, moment_two):
    kernel, first, second = weights[0], moment_one[0], moment_two[0]
    n, m = lax.axis_size("blk"), lax.axis_size("shard")
    evens, odds = range(0, n, 2), range(1, n, 2)
    share = cut_acts.shape[1] // m
    half = lax.dynamic_slice_in_dim(cut_acts, lax.axis_index("shard") * share, share, 1)
    pairs = n - n % 2
    partner = {i: i ^ 1 if i < pairs else i for i in range(n)}
    neighbour = {i: (i + 1) % n if i % 2 else (i - 1) % n for i in range(n)}
    across = [routed(half, neighbour)]
    across_g = passed_along(upstream, "blk", -1)
    near_x, near_g = routed(cut_acts, partner), routed(upstream, partner)
    kernel1, first1, second1, slopes0 = train([cut_acts], upstream, kernel, first, second, F32)
    across += [passed_along(across[0], "shard", k) for k in range(1, m)]
    before_g = passed_along(upstream, "blk", 1)

    detour = n % 4 == 0
    even_to, odd_to = {i: (i + HOPS) % n for i in evens}, {i: (i + HOPS) % n for i in odds}
    first_to = {i: i - 1 if detour and i % 4 == 2 else to for i, to in even_to.items()}
    odd_to |= {i: partner[i] for i in evens}
    even_to |= {i: partner[i] for i in odds}
    first_to |= {i: partner[i] for i in odds}
    even_w, even_m, even_v, slopes_even = train([near_x], near_g, kernel1, first1, second1, BF16, parity=0)
    even_w = routed(even_w, even_to)
    even_m = routed(even_m, first_to)
    even_v = routed(even_v, even_to)
    odd_w, odd_m, odd_v, slopes_odd = train(across, across_g, kernel1, first1, second1, BF16, parity=1)
    odd_w = routed(odd_w, odd_to)
    odd_m = routed(odd_m, odd_to)
    odd_v = routed(odd_v, odd_to)
    moments = (even_m, even_v, odd_m, odd_v)
    if detour:
        moments += (routed(even_m, {i: (i + 1 + HOPS) % n for i in range(1, n, 4)}),)

    def summed(slopes, kernel):
        parts = [part(slopes, kernel, k) for k in range(1, m)]
        parts = [passed_along(one, "shard", k + 1) for k, one in enumerate(parts)]
        return part(slopes, kernel, 0, parts)

    home = summed([slopes0], kernel)
    back = summed([slopes_even, slopes_odd], kernel1)
    back = passed_along(back, "blk", 1)

    slopes2, moved, transposed = forward(across, near_x, before_g, near_g, even_w, odd_w)
    last = passed_along(summed([slopes2], moved), "blk", -1)
    grad2 = gradient(transposed, slopes2)
    kernel3, first3, second3, returned = finish(grad2, moved, moments, home, back, [last])
    return (kernel3[None], first3[None], second3[None], returned)


def solution(mesh):
    placed = (
        P("blk", None),
        P("blk", "shard"),
        P("blk", None, "shard"),
        P("blk", None, "shard"),
        P("blk", None, "shard"),
    )
    return jax.shard_map(
        shards,
        mesh=mesh,
        in_specs=placed,
        out_specs=(
            P("blk", None, "shard"),
            P("blk", None, "shard"),
            P("blk", None, "shard"),
            P(None, ("blk", "shard"), None),
        ),
        check_vma=False,
    )
```

time: 151 us -> 124 us (0.82)
  the two profiles are of different devices: /device:TPU:1 before, /device:TPU:0 now
where the time goes in v3:
time: 124 us
  waiting for transfers between devices  71.9 us (58%)
  starting transfers between devices  29 us (23%)
  Pallas kernels  20.5 us (17%)
    ppermute x8, waiting for transfers between devices, passed_along(): lax.ppermute(part, axis, [(i, (i + by) % devices) for i in range(devices)])  65.6 us
    ppermute x10, starting transfers between devices, routed(): lax.ppermute(one, 'blk', sorted(route.items()))  21.8 us
    pallas_call x3, Pallas kernels, train(): pl.pallas_call(body, out_shape=tuple(outs), in_specs=[ANY] * (k + 4), out...  12.2 us
    ppermute x8, starting transfers between devices, passed_along(): lax.ppermute(part, axis, [(i, (i + by) % devices) for i in range(devices)])  7.19 us
    ppermute x10, waiting for transfers between devices, routed(): lax.ppermute(one, 'blk', sorted(route.items()))  6.23 us
    pallas_call x1, Pallas kernels, finish(): pl.pallas_call(functools.partial(finish_kernel, len(last), len(moments)),...  3.2 us
    pallas_call x6, Pallas kernels, part(): pl.pallas_call(functools.partial(part_kernel, shift, n, len(slopes)), out...  3 us
  transfers between devices with their start and end apart: 18, of which 6 were waited for; matrix products, arithmetic and copies ran while one was open for 0% of the time, Pallas kernels for 14%

profile of v3, /device:TPU:0, one launch (start us, length us, event | category | flops | bytes accessed | tf_op | source)
XLA Modules:
  0.0 123.6 jit_solution(5687023971433497300)
XLA Ops:
  0.6 1.1 constant_dynamic-slice_fusion
  1.7 5.5 %collective-permute-start = (bf16[512,512]{1,0:T(8,128)(2,1)S(1)}, bf16[512,512]{1,0:T(8,128)(2,1)S(1)}, u32[]{:S(2)}, u32[]{:S(2)}) collective-permute-start(bf16[512,512]{1,0:T(8,128)(2,1)S(1)} %constant_dynamic-slice_fusion), channel_id=1, source_target_pairs={{0,30},{2,4},{4,2},{6,8},{8,6},{10,12},{12,10},{14,16},{16,14},{18... | collective-permute-start | bytes 1572872 | tf_op jit(solution)/shard_map/ppermute | solution.py:24
  7.3 0.8 collective-permute-start.6
  8.0 6.2 %collective-permute-done.refs_0_ = bf16[512,512]{1,0:T(8,128)(2,1)S(1)} collective-permute-done((bf16[512,512]{1,0:T(8,128)(2,1)S(1)}, bf16[512,512]{1,0:T(8,128)(2,1)S(1)}, u32[]{:S(2)}, u32[]{:S(2)}) %collective-permute-start) | collective-permute-done | bytes 524320 | tf_op jit(solution)/shard_map/ppermute | solution.py:24
  14.2 1.9 %collective-permute-start.1 = (bf16[512,512]{1,0:T(8,128)(2,1)S(1)}, bf16[512,512]{1,0:T(8,128)(2,1)S(1)}, u32[]{:S(2)}, u32[]{:S(2)}) collective-permute-start(bf16[512,512]{1,0:T(8,128)(2,1)S(1)} %collective-permute-done.refs_0_), channel_id=1, source_target_pairs={{0,1},{1,0},{2,3},{3,2},{4,5},{5,4},{6,7},{7,6},{8,9},{9,8},{10,11... | collective-permute-start | bytes 1572872 | tf_op jit(solution)/shard_map/ppermute | solution.py:20
  16.2 7.3 %collective-permute-start.4 = (bf16[512,512]{1,0:T(8,128)(2,1)}, bf16[512,512]{1,0:T(8,128)(2,1)S(1)}, u32[]{:S(2)}, u32[]{:S(2)}) collective-permute-start(bf16[512,512]{1,0:T(8,128)(2,1)} %refs_1_.1), channel_id=1, source_target_pairs={{0,2},{2,0},{4,6},{6,4},{8,10},{10,8},{12,14},{14,12},{16,18},{18,... | collective-permute-start | bytes 1572872 | tf_op jit(solution)/shard_map/ppermute | solution.py:24
  23.5 6.5 %shard_map.84 = (bf16[1024,512]{1,0:T(8,128)(2,1)}, f32[1024,512]{1,0:T(8,128)}, f32[1024,512]{1,0:T(8,128)}, bf16[512,512]{1,0:T(8,128)(2,1)}) custom-call(bf16[512,1024]{1,0:T(8,128)(2,1)} %refs_0_.1, bf16[512,512]{1,0:T(8,128)(2,1)} %refs_1_.1, bf16[1024,512]{1,0:T(8,128)(2,1)} %bitcast.6, f32[1024,512]{1,0:T(8,128)} %bitcast.9, f32[1024,512]{1,0:T(8,128)} %bitcast.10), custom_call_target="tpu_custom_call" | custom-call | flops 1073741824 | bytes 8388608 | tf_op jit(solution)/shard_map/pallas_call | solution.py:146
  30.0 0.2 shard_map.86
  30.2 5.7 %collective-permute-start.7 = (bf16[1024,512]{1,0:T(8,128)(2,1)S(1)}, bf16[1024,512]{1,0:T(8,128)(2,1)S(1)}, u32[]{:S(2)}, u32[]{:S(2)}) collective-permute-start(bf16[1024,512]{1,0:T(8,128)(2,1)S(1)} %get-tuple-element.27), channel_id=1, source_target_pairs={{0,2},{2,8},{4,6},{6,12},{8,10},{10,16},{12,14},{14,20},{16,18},{1... | collective-permute-start | bytes 3145736 | tf_op jit(solution)/shard_map/ppermute | solution.py:24
  36.0 5.5 %shard_map.85 = (bf16[1024,512]{1,0:T(8,128)(2,1)S(1)}, bf16[1024,512]{1,0:T(8,128)(2,1)S(1)}, bf16[1024,512]{1,0:T(8,128)(2,1)S(1)}, bf16[512,512]{1,0:T(8,128)(2,1)S(1)}) custom-call(bf16[512,1024]{1,0:T(8,128)(2,1)S(1)} %collective-permute-done.2.refs_0_.refs_2_, bf16[512,512]{1,0:T(8,128)(2,1)S(1)} %collective-permute-done.4.refs_1_.refs_4_, ...), custom_call_target="tpu_custom_call" | custom-call | flops 1073741824 | bytes 8388608 | tf_op jit(solution)/shard_map/pallas_call | solution.py:146
  41.5 0.1 collective-permute-start.5
  41.5 0.5 collective-permute-start.3
  42.0 2.4 %collective-permute-start.8 = (bf16[1024,512]{1,0:T(8,128)(2,1)S(1)}, bf16[1024,512]{1,0:T(8,128)(2,1)S(1)}, u32[]{:S(2)}, u32[]{:S(2)}) collective-permute-start(bf16[1024,512]{1,0:T(8,128)(2,1)S(1)} %get-tuple-element.31), channel_id=1, source_target_pairs={{0,6},{2,0},{4,2},{6,4},{8,14},{10,8},{12,10},{14,12},{16,22},{18,... | collective-permute-start | bytes 3145736 | tf_op jit(solution)/shard_map/ppermute | solution.py:24
  44.5 0.5 part.6
  44.9 1.4 %collective-permute-start.13 = (bf16[256,1024]{1,0:T(8,128)(2,1)S(1)}, bf16[256,1024]{1,0:T(8,128)(2,1)S(1)}, u32[]{:S(2)}, u32[]{:S(2)}) collective-permute-start(bf16[256,1024]{1,0:T(8,128)(2,1)S(1)} %part.6), channel_id=1, source_target_pairs={{0,1},{1,0},{2,3},{3,2},{4,5},{5,4},{6,7},{7,6},{8,9},{9,8},{10,11... | collective-permute-start | bytes 1572872 | tf_op jit(solution)/shard_map/ppermute | solution.py:20
  46.4 0.7 part.8
  47.0 23.2 %collective-permute-done.3.refs_3_ = bf16[512,512]{1,0:T(8,128)(2,1)S(1)} collective-permute-done((bf16[512,512]{1,0:T(8,128)(2,1)S(1)}, bf16[512,512]{1,0:T(8,128)(2,1)S(1)}, u32[]{:S(2)}, u32[]{:S(2)}) %collective-permute-start.3) | collective-permute-done | bytes 524320 | tf_op jit(solution)/shard_map/ppermute | solution.py:20
  70.2 0.5 collective-permute-start.14
  70.8 1.5 %forward.1 = (bf16[512,512]{1,0:T(8,128)(2,1)S(1)}, bf16[1024,512]{1,0:T(8,128)(2,1)S(1)}, bf16[1024,512]{1,0:T(8,128)(2,1)S(1)}) custom-call(bf16[512,512]{1,0:T(8,128)(2,1)S(1)} %collective-permute-done.refs_0_, bf16[512,512]{1,0:T(8,128)(2,1)S(1)} %collective-permute-done.1.refs_1_, bf16[512,1024]{1,0:T(8,128)(2,1)S(1)} %collective-permute-done.2.refs_0_.refs_2_, ...), custom_call_target="tpu_custom_call" | custom-call | flops 536870912 | bytes 2097152 | tf_op jit(solution)/shard_map/forward/pallas_call | solution.py:242
  72.3 0.5 part.10
  72.7 1.6 %collective-permute-start.16 = (bf16[256,1024]{1,0:T(8,128)(2,1)S(1)}, bf16[256,1024]{1,0:T(8,128)(2,1)S(1)}, u32[]{:S(2)}, u32[]{:S(2)}) collective-permute-start(bf16[256,1024]{1,0:T(8,128)(2,1)S(1)} %part.10), channel_id=1, source_target_pairs={{0,1},{1,0},{2,3},{3,2},{4,5},{5,4},{6,7},{7,6},{8,9},{9,8},{10,11... | collective-permute-start | bytes 1572872 | tf_op jit(solution)/shard_map/ppermute | solution.py:20
  74.3 9.3 %collective-permute-done.14.refs_3_ = bf16[256,1024]{1,0:T(8,128)(2,1)S(1)} collective-permute-done((bf16[256,1024]{1,0:T(8,128)(2,1)S(1)}, bf16[256,1024]{1,0:T(8,128)(2,1)S(1)}, u32[]{:S(2)}, u32[]{:S(2)}) %collective-permute-start.14) | collective-permute-done | bytes 524320 | tf_op jit(solution)/shard_map/ppermute | solution.py:20
  83.6 0.5 part.9
  84.2 0.5 collective-permute-start.15
  84.7 6.0 %collective-permute-done.16.refs_2_ = bf16[256,1024]{1,0:T(8,128)(2,1)S(1)} collective-permute-done((bf16[256,1024]{1,0:T(8,128)(2,1)S(1)}, bf16[256,1024]{1,0:T(8,128)(2,1)S(1)}, u32[]{:S(2)}, u32[]{:S(2)}) %collective-permute-start.16) | collective-permute-done | bytes 524320 | tf_op jit(solution)/shard_map/ppermute | solution.py:20
  90.7 0.7 collective-permute-start.12
  91.4 0.5 part.11
  91.9 21.7 %collective-permute-done.15.refs_6_ = bf16[256,1024]{1,0:T(8,128)(2,1)S(1)} collective-permute-done((bf16[256,1024]{1,0:T(8,128)(2,1)S(1)}, bf16[256,1024]{1,0:T(8,128)(2,1)S(1)}, u32[]{:S(2)}, u32[]{:S(2)}) %collective-permute-start.15) | collective-permute-done | bytes 524320 | tf_op jit(solution)/shard_map/ppermute | solution.py:20
  113.5 0.5 part.7.refs_5_
  114.0 0.7 gradient.1.grad
  114.8 5.5 %collective-permute-done.17.refs_7_ = bf16[256,1024]{1,0:T(8,128)(2,1)S(1)} collective-permute-done((bf16[256,1024]{1,0:T(8,128)(2,1)S(1)}, bf16[256,1024]{1,0:T(8,128)(2,1)S(1)}, u32[]{:S(2)}, u32[]{:S(2)}) %collective-permute-start.17) | collective-permute-done | bytes 524320 | tf_op jit(solution)/shard_map/ppermute | solution.py:20
  120.2 3.2 %finish.1 = (bf16[1024,512]{1,0:T(8,128)(2,1)}, f32[1024,512]{1,0:T(8,128)}, f32[1024,512]{1,0:T(8,128)}, bf16[3,256,1024]{2,1,0:T(8,128)(2,1)}) custom-call(f32[1024,512]{1,0:T(8,128)S(1)} %gradient.1.grad, bf16[1024,512]{1,0:T(8,128)(2,1)S(1)} %get-tuple-element.30.refs_1_.w, bf16[1024,512]{1,0:T(8,128)(2,1)S(1)} %collective-permute-done.8.refs_0_, ...), custom_call_target="tpu_custom_call" | custom-call | flops 15728640 | bytes 8388608 | tf_op jit(solution)/shard_map/finish/pallas_call | solution.py:332
  (25 shorter events, 0.1 us)
Async XLA Ops:
  1.7 12.5 %collective-permute-start = (bf16[512,512]{1,0:T(8,128)(2,1)S(1)}, bf16[512,512]{1,0:T(8,128)(2,1)S(1)}, u32[]{:S(2)}, u32[]{:S(2)}) collective-permute-start(bf16[512,512]{1,0:T(8,128)(2,1)S(1)} %constant_dynamic-slice_fusion), channel_id=1, source_target_pairs={{0,30},{2,4},{4,2},{6,8},{8,6},{10,12},{12,10},{14,16},{16,14},{18... | collective-permute-start | bytes 1572872 | tf_op jit(solution)/shard_map/ppermute | solution.py:24
  7.3 28.7 %collective-permute-start.2 = (bf16[512,1024]{1,0:T(8,128)(2,1)}, bf16[512,1024]{1,0:T(8,128)(2,1)S(1)}, u32[]{:S(2)}, u32[]{:S(2)}) collective-permute-start(bf16[512,1024]{1,0:T(8,128)(2,1)} %refs_0_.1), channel_id=1, source_target_pairs={{0,2},{2,0},{4,6},{6,4},{8,10},{10,8},{12,14},{14,12},{16,18},{18,... | collective-permute-start | bytes 3145736 | tf_op jit(solution)/shard_map/ppermute | solution.py:24
  7.3 22.7 %collective-permute-start.6 = (bf16[512,512]{1,0:T(8,128)(2,1)}, bf16[512,512]{1,0:T(8,128)(2,1)S(1)}, u32[]{:S(2)}, u32[]{:S(2)}) collective-permute-start(bf16[512,512]{1,0:T(8,128)(2,1)} %refs_1_.1), channel_id=1, source_target_pairs={{0,30},{2,0},{4,2},{6,4},{8,6},{10,8},{12,10},{14,12},{16,14},{18,... | collective-permute-start | bytes 1572872 | tf_op jit(solution)/shard_map/ppermute | solution.py:20
  14.2 15.7 %collective-permute-start.1 = (bf16[512,512]{1,0:T(8,128)(2,1)S(1)}, bf16[512,512]{1,0:T(8,128)(2,1)S(1)}, u32[]{:S(2)}, u32[]{:S(2)}) collective-permute-start(bf16[512,512]{1,0:T(8,128)(2,1)S(1)} %collective-permute-done.refs_0_), channel_id=1, source_target_pairs={{0,1},{1,0},{2,3},{3,2},{4,5},{5,4},{6,7},{7,6},{8,9},{9,8},{10,11... | collective-permute-start | bytes 1572872 | tf_op jit(solution)/shard_map/ppermute | solution.py:20
  16.2 19.8 %collective-permute-start.4 = (bf16[512,512]{1,0:T(8,128)(2,1)}, bf16[512,512]{1,0:T(8,128)(2,1)S(1)}, u32[]{:S(2)}, u32[]{:S(2)}) collective-permute-start(bf16[512,512]{1,0:T(8,128)(2,1)} %refs_1_.1), channel_id=1, source_target_pairs={{0,2},{2,0},{4,6},{6,4},{8,10},{10,8},{12,14},{14,12},{16,18},{18,... | collective-permute-start | bytes 1572872 | tf_op jit(solution)/shard_map/ppermute | solution.py:24
  30.2 11.3 %copy-start.3 = (bf16[512,512]{1,0:T(8,128)(2,1)S(1)}, bf16[512,512]{1,0:T(8,128)(2,1)}, u32[]{:S(2)}) copy-start(bf16[512,512]{1,0:T(8,128)(2,1)} %refs_1_.1) | copy-start | bytes 1572868
  30.2 14.3 %copy-start.1 = (bf16[1,1024,512]{2,1,0:T(8,128)(2,1)S(1)}, bf16[1,1024,512]{2,1,0:T(8,128)(2,1)}, u32[]{:S(2)}) copy-start(bf16[1,1024,512]{2,1,0:T(8,128)(2,1)} %param.7) | copy-start | bytes 3145732
  30.2 14.2 %copy-start.2 = (bf16[512,512]{1,0:T(8,128)(2,1)S(1)}, bf16[512,512]{1,0:T(8,128)(2,1)}, u32[]{:S(2)}) copy-start(bf16[512,512]{1,0:T(8,128)(2,1)} %get-tuple-element.35.refs_0_) | copy-start | bytes 1572868
  30.2 40.5 %collective-permute-start.7 = (bf16[1024,512]{1,0:T(8,128)(2,1)S(1)}, bf16[1024,512]{1,0:T(8,128)(2,1)S(1)}, u32[]{:S(2)}, u32[]{:S(2)}) collective-permute-start(bf16[1024,512]{1,0:T(8,128)(2,1)S(1)} %get-tuple-element.27), channel_id=1, source_target_pairs={{0,2},{2,8},{4,6},{6,12},{8,10},{10,16},{12,14},{14,20},{16,18},{1... | collective-permute-start | bytes 3145736 | tf_op jit(solution)/shard_map/ppermute | solution.py:24
  41.4 4.9 %copy-start = (bf16[1024,512]{1,0:T(8,128)(2,1)S(1)}, bf16[1024,512]{1,0:T(8,128)(2,1)}, u32[]{:S(2)}) copy-start(bf16[1024,512]{1,0:T(8,128)(2,1)} %get-tuple-element.23.refs_2_.refs_3_) | copy-start | bytes 3145732
  41.5 29.3 %collective-permute-start.5 = (bf16[1024,512]{1,0:T(8,128)(2,1)S(1)}, bf16[1024,512]{1,0:T(8,128)(2,1)S(1)}, u32[]{:S(2)}, u32[]{:S(2)}) collective-permute-start(bf16[1024,512]{1,0:T(8,128)(2,1)S(1)} %get-tuple-element.26), channel_id=1, source_target_pairs={{0,6},{2,0},{4,10},{6,4},{8,14},{10,8},{12,18},{14,12},{16,22},{18... | collective-permute-start | bytes 3145736 | tf_op jit(solution)/shard_map/ppermute | solution.py:24
  41.5 28.7 %collective-permute-start.3 = (bf16[512,512]{1,0:T(8,128)(2,1)S(1)}, bf16[512,512]{1,0:T(8,128)(2,1)S(1)}, u32[]{:S(2)}, u32[]{:S(2)}) collective-permute-start(bf16[512,512]{1,0:T(8,128)(2,1)S(1)} %copy-done.3), channel_id=1, source_target_pairs={{0,2},{2,4},{4,6},{6,8},{8,10},{10,12},{12,14},{14,16},{16,18},{18... | collective-permute-start | bytes 1572872 | tf_op jit(solution)/shard_map/ppermute | solution.py:20
  42.0 42.2 %collective-permute-start.8 = (bf16[1024,512]{1,0:T(8,128)(2,1)S(1)}, bf16[1024,512]{1,0:T(8,128)(2,1)S(1)}, u32[]{:S(2)}, u32[]{:S(2)}) collective-permute-start(bf16[1024,512]{1,0:T(8,128)(2,1)S(1)} %get-tuple-element.31), channel_id=1, source_target_pairs={{0,6},{2,0},{4,2},{6,4},{8,14},{10,8},{12,10},{14,12},{16,22},{18,... | collective-permute-start | bytes 3145736 | tf_op jit(solution)/shard_map/ppermute | solution.py:24
  44.9 39.2 %collective-permute-start.13 = (bf16[256,1024]{1,0:T(8,128)(2,1)S(1)}, bf16[256,1024]{1,0:T(8,128)(2,1)S(1)}, u32[]{:S(2)}, u32[]{:S(2)}) collective-permute-start(bf16[256,1024]{1,0:T(8,128)(2,1)S(1)} %part.6), channel_id=1, source_target_pairs={{0,1},{1,0},{2,3},{3,2},{4,5},{5,4},{6,7},{7,6},{8,9},{9,8},{10,11... | collective-permute-start | bytes 1572872 | tf_op jit(solution)/shard_map/ppermute | solution.py:20
  70.2 13.4 %collective-permute-start.14 = (bf16[256,1024]{1,0:T(8,128)(2,1)S(1)}, bf16[256,1024]{1,0:T(8,128)(2,1)S(1)}, u32[]{:S(2)}, u32[]{:S(2)}) collective-permute-start(bf16[256,1024]{1,0:T(8,128)(2,1)S(1)} %part.8), channel_id=1, source_target_pairs={{0,1},{1,0},{2,3},{3,2},{4,5},{5,4},{6,7},{7,6},{8,9},{9,8},{10,11... | collective-permute-start | bytes 1572872 | tf_op jit(solution)/shard_map/ppermute | solution.py:20
  72.7 17.9 %collective-permute-start.16 = (bf16[256,1024]{1,0:T(8,128)(2,1)S(1)}, bf16[256,1024]{1,0:T(8,128)(2,1)S(1)}, u32[]{:S(2)}, u32[]{:S(2)}) collective-permute-start(bf16[256,1024]{1,0:T(8,128)(2,1)S(1)} %part.10), channel_id=1, source_target_pairs={{0,1},{1,0},{2,3},{3,2},{4,5},{5,4},{6,7},{7,6},{8,9},{9,8},{10,11... | collective-permute-start | bytes 1572872 | tf_op jit(solution)/shard_map/ppermute | solution.py:20
  74.3 40.4 %collective-permute-start.10 = (bf16[1024,512]{1,0:T(8,128)(2,1)S(1)}, bf16[1024,512]{1,0:T(8,128)(2,1)S(1)}, u32[]{:S(2)}, u32[]{:S(2)}) collective-permute-start(bf16[1024,512]{1,0:T(8,128)(2,1)S(1)} %get-tuple-element.33), channel_id=1, source_target_pairs={{0,2},{2,8},{4,6},{6,12},{8,10},{10,16},{12,14},{14,20},{16,18},{1... | collective-permute-start | bytes 3145736 | tf_op jit(solution)/shard_map/ppermute | solution.py:24
  83.6 31.1 %collective-permute-start.11 = (bf16[1024,512]{1,0:T(8,128)(2,1)S(1)}, bf16[1024,512]{1,0:T(8,128)(2,1)S(1)}, u32[]{:S(2)}, u32[]{:S(2)}) collective-permute-start(bf16[1024,512]{1,0:T(8,128)(2,1)S(1)} %get-tuple-element.34), channel_id=1, source_target_pairs={{0,2},{2,8},{4,6},{6,12},{8,10},{10,16},{12,14},{14,20},{16,18},{1... | collective-permute-start | bytes 3145736 | tf_op jit(solution)/shard_map/ppermute | solution.py:24
  84.1 30.6 %collective-permute-start.9 = (bf16[1024,512]{1,0:T(8,128)(2,1)S(1)}, bf16[1024,512]{1,0:T(8,128)(2,1)S(1)}, u32[]{:S(2)}, u32[]{:S(2)}) collective-permute-start(bf16[1024,512]{1,0:T(8,128)(2,1)S(1)} %get-tuple-element.32), channel_id=1, source_target_pairs={{0,6},{2,0},{4,10},{6,4},{8,14},{10,8},{12,18},{14,12},{16,22},{18... | collective-permute-start | bytes 3145736 | tf_op jit(solution)/shard_map/ppermute | solution.py:24
  84.2 29.3 %collective-permute-start.15 = (bf16[256,1024]{1,0:T(8,128)(2,1)S(1)}, bf16[256,1024]{1,0:T(8,128)(2,1)S(1)}, u32[]{:S(2)}, u32[]{:S(2)}) collective-permute-start(bf16[256,1024]{1,0:T(8,128)(2,1)S(1)} %part.9), channel_id=1, source_target_pairs={{0,2},{2,4},{4,6},{6,8},{8,10},{10,12},{12,14},{14,16},{16,18},{18... | collective-permute-start | bytes 1572872 | tf_op jit(solution)/shard_map/ppermute | solution.py:20
  90.7 24.1 %collective-permute-start.12 = (bf16[1024,512]{1,0:T(8,128)(2,1)S(1)}, bf16[1024,512]{1,0:T(8,128)(2,1)S(1)}, u32[]{:S(2)}, u32[]{:S(2)}) collective-permute-start(bf16[1024,512]{1,0:T(8,128)(2,1)S(1)} %collective-permute-done.8.refs_0_), channel_id=1, source_target_pairs={{2,10},{10,18},{18,26},{26,2},{3,11},{11,19},{19,27},{27,3}} | collective-permute-start | bytes 3145736 | tf_op jit(solution)/shard_map/ppermute | solution.py:24
  113.5 6.7 %collective-permute-start.17 = (bf16[256,1024]{1,0:T(8,128)(2,1)S(1)}, bf16[256,1024]{1,0:T(8,128)(2,1)S(1)}, u32[]{:S(2)}, u32[]{:S(2)}) collective-permute-start(bf16[256,1024]{1,0:T(8,128)(2,1)S(1)} %part.11), channel_id=1, source_target_pairs={{0,30},{2,0},{4,2},{6,4},{8,6},{10,8},{12,10},{14,12},{16,14},{18,... | collective-permute-start | bytes 1572872 | tf_op jit(solution)/shard_map/ppermute | solution.py:20

commit v4 on v3

--- a/solution.py
+++ b/solution.py
@@ -13,6 +13,7 @@
 ANY = pl.BlockSpec(memory_space=pl.ANY)
 WHOLE = pl.BlockSpec(memory_space=pltpu.VMEM)
 MIB = 1024 * 1024
+CUT_FLOPS = 4 * 10**9
 
 
 def passed_along(part, axis, by):
@@ -78,96 +79,82 @@
     return copies
 
 
-def train_body(x_in, g_in, w_in, m_in, v_in, w_out, m_out, v_out, s_out,
-               x, xt, g, w, m, v, z, s, grad, w_new, m_new, v_new, sem):
-    bands = blocks(w.shape[0], 256)
-    n = len(bands)
-    last = 3 + 5 * n
-    get_x = copies_of(x_in, x, [sem.at[last + k] for k in range(len(x_in))])
-    get_w, get_g = [
-        pltpu.make_async_copy(one, ref, sem.at[1 + i]) for i, (one, ref) in enumerate(((w_in, w), (g_in, g)))
-    ]
-    gets = [
-        [
-            pltpu.make_async_copy(one.at[band], ref.at[band], sem.at[3 + 2 * i + k])
-            for k, (one, ref) in enumerate(((m_in, m), (v_in, v)))
-        ]
-        for i, band in enumerate(bands)
-    ]
-    for get in get_x + [get_w, get_g]:
-        get.start()
-    for get in get_x:
-        get.wait()
-    for get in gets[0]:
-        get.start()
-    puts = []
+def train_body(fetched, x_in, g_in, w, m, v, w_new, m_new, v_new, s, xt, z, grad, *scratch):
+    if fetched:
+        x, g, sem = scratch
+        gets = copies_of(x_in, x, [sem.at[1 + k] for k in range(len(x_in))])
+        gets.append(pltpu.make_async_copy(g_in, g, sem.at[0]))
+        for get in gets:
+            get.start()
+        for get in gets:
+            get.wait()
+    else:
+        x, g = x_in[0], g_in
     xt[...] = x[...].T
-    get_w.wait()
-    get_g.wait()
-    for pair in gets[1:]:
-        for get in pair:
-            get.start()
     slopes_body(x, g, w, z, s)
-    puts.append(pltpu.make_async_copy(s, s_out, sem.at[0]))
-    puts[-1].start()
-    for i, band in enumerate(bands):
+    for band in blocks(w.shape[0], 256):
         grad[band, :] = jnp.dot(xt[band, :], s[...], preferred_element_type=F32)
-        for get in gets[i]:
-            get.wait()
         update_rows(grad, w, m, v, w_new, m_new, v_new, band)
-        new = [
-            pltpu.make_async_copy(one.at[band], out.at[band], sem.at[3 + 2 * n + 3 * i + k])
-            for k, (one, out) in enumerate(((w_new, w_out), (m_new, m_out), (v_new, v_out)))
-        ]
-        for put in new:
-            put.start()
-        puts += new
-    for put in puts:
-        put.wait()
 
 
 def train(inputs, grad_out, kernel, first, second, out_dtype, parity=None):
     (tokens, width), depth = grad_out.shape, kernel.shape[0]
     k = len(inputs)
-    n = len(blocks(depth, 256))
-    outs = [
-        jax.ShapeDtypeStruct((depth, width), BF16),
-        jax.ShapeDtypeStruct((depth, width), out_dtype),
-        jax.ShapeDtypeStruct((depth, width), out_dtype),
-        jax.ShapeDtypeStruct((tokens, width), BF16),
-    ]
 
     def body(*refs):
         only_if(
             None if parity is None else lax.rem(lax.axis_index("blk"), 2) == parity,
-            lambda: train_body(refs[:k], *refs[k:]),
+            lambda: train_body(parity is not None, refs[:k], *refs[k:]),
         )
 
+    scratch = [
+        pltpu.VMEM((depth, tokens), BF16),
+        pltpu.VMEM((tokens, width), F32),
+        pltpu.VMEM((depth, width), F32),
+    ]
+    if parity is not None:
+        scratch += [
+            pltpu.VMEM((tokens, depth), BF16),
+            pltpu.VMEM((tokens, width), BF16),
+            pltpu.SemaphoreType.DMA((1 + k,)),
+        ]
     return pl.pallas_call(
         body,
-        out_shape=tuple(outs),
-        in_specs=[ANY] * (k + 4),
-        out_specs=(ANY,) * len(outs),
-        scratch_shapes=[
-            pltpu.VMEM((tokens, depth), BF16),
-            pltpu.VMEM((depth, tokens), BF16),
-            pltpu.VMEM((tokens, width), BF16),
-            pltpu.VMEM((depth, width), BF16),
-            pltpu.VMEM((depth, width), F32),
-            pltpu.VMEM((depth, width), F32),
-            pltpu.VMEM((tokens, width), F32),
-            pltpu.VMEM((tokens, width), BF16),
-            pltpu.VMEM((depth, width), F32),
-            pltpu.VMEM((depth, width), BF16),
-            pltpu.VMEM((depth, width), out_dtype),
-            pltpu.VMEM((depth, width), out_dtype),
-            pltpu.SemaphoreType.DMA((3 + 5 * n + k,)),
-        ],
-        compiler_params=pltpu.CompilerParams(vmem_limit_bytes=(60 if parity is None else 48) * MIB),
+        out_shape=(
+            jax.ShapeDtypeStruct((depth, width), BF16),
+            jax.ShapeDtypeStruct((depth, width), out_dtype),
+            jax.ShapeDtypeStruct((depth, width), out_dtype),
+            jax.ShapeDtypeStruct((tokens, width), BF16),
+        ),
+        in_specs=[WHOLE if parity is None else ANY] * (k + 1) + [WHOLE] * 3,
+        out_specs=(WHOLE,) * 4,
+        scratch_shapes=scratch,
+        compiler_params=pltpu.CompilerParams(vmem_limit_bytes=24 * MIB),
         cost_estimate=pl.CostEstimate(
             flops=4 * tokens * depth * width, bytes_accessed=16 * depth * width, transcendentals=0
         ),
     )(*inputs, grad_out, kernel, first, second)
+
+
+def cut_kernel(x_in, out, sem):
+    share = out.shape[1]
+    at = pl.multiple_of(lax.axis_index("shard") * share, share)
+    get = pltpu.make_async_copy(x_in.at[:, pl.ds(at, share)], out, sem)
+    get.start()
+    get.wait()
+
+
+def cut(inputs, share):
+    return pl.pallas_call(
+        cut_kernel,
+        out_shape=jax.ShapeDtypeStruct((inputs.shape[0], share), BF16),
+        in_specs=[ANY],
+        out_specs=WHOLE,
+        scratch_shapes=[pltpu.SemaphoreType.DMA],
+        compiler_params=pltpu.CompilerParams(vmem_limit_bytes=8 * MIB),
+        cost_estimate=pl.CostEstimate(flops=CUT_FLOPS, bytes_accessed=4 * inputs.size, transcendentals=0),
+        name="cut",
+    )(inputs)
 
 
 def part_kernel(shift, n, several, *refs):
@@ -359,7 +346,7 @@
     n, m = lax.axis_size("blk"), lax.axis_size("shard")
     evens, odds = range(0, n, 2), range(1, n, 2)
     share = cut_acts.shape[1] // m
-    half = lax.dynamic_slice_in_dim(cut_acts, lax.axis_index("shard") * share, share, 1)
+    half = cut(cut_acts, share)
     pairs = n - n % 2
     partner = {i: i ^ 1 if i < pairs else i for i in range(n)}
     neighbour = {i: (i + 1) % n if i % 2 else (i - 1) % n for i in range(n)}
@@ -372,10 +359,10 @@
 
     detour = n % 4 == 0
     even_to, odd_to = {i: (i + HOPS) % n for i in evens}, {i: (i + HOPS) % n for i in odds}
-    first_to = {i: i - 1 if detour and i % 4 == 2 else to for i, to in even_to.items()}
+    first_to = {i: i - 2 if detour and i % 4 == 2 else to for i, to in even_to.items()}
     odd_to |= {i: partner[i] for i in evens}
     even_to |= {i: partner[i] for i in odds}
-    first_to |= {i: partner[i] for i in odds}
+    first_to |= {i: i if detour and i % 4 == 1 else partner[i] for i in odds}
     even_w, even_m, even_v, slopes_even = train([near_x], near_g, kernel1, first1, second1, BF16, parity=0)
     even_w = routed(even_w, even_to)
     even_m = routed(even_m, first_to)
@@ -386,7 +373,7 @@
     odd_v = routed(odd_v, odd_to)
     moments = (even_m, even_v, odd_m, odd_v)
     if detour:
-        moments += (routed(even_m, {i: (i + 1 + HOPS) % n for i in range(1, n, 4)}),)
+        moments += (routed(even_m, {i: (i + 2 + HOPS) % n for i in range(0, n, 4)}),)
 
     def summed(slopes, kernel):
         parts = [part(slopes, kernel, k) for k in range(1, m)]

time: 124 us -> 120 us (0.968)
  Pallas kernels: 20.5 us -> 16.5 us
  starting transfers between devices: 29 us -> 31.7 us
  waiting for transfers between devices: 71.9 us -> 70.5 us
    pallas_call x3 -> x4, Pallas kernels: 12.2 us -> 8.17 us  [the longest x3 6.96 us: train(): pl.pallas_call(body, out_shape=(jax.ShapeDtypeStruct((depth, width), BF16...]
    ppermute x10, starting transfers between devices: 21.8 us -> 24.4 us  [routed(): lax.ppermute(one, 'blk', sorted(route.items()))]
    ppermute x8, waiting for transfers between devices: 65.6 us -> 64.3 us  [passed_along(): lax.ppermute(part, axis, [(i, (i + by) % devices) for i in range(devices)])]
  transfers between devices with their start and end apart: 18 -> 18, of which waited for: 6 -> 6; matrix products, arithmetic and copies ran while one was open for 0% -> 0% of each run, Pallas kernels for 14% -> 10%
where the time goes in v4:
time: 120 us
  waiting for transfers between devices  70.5 us (59%)
  starting transfers between devices  31.7 us (26%)
  Pallas kernels  16.5 us (14%)
    ppermute x8, waiting for transfers between devices, passed_along(): lax.ppermute(part, axis, [(i, (i + by) % devices) for i in range(devices)])  64.3 us
    ppermute x10, starting transfers between devices, routed(): lax.ppermute(one, 'blk', sorted(route.items()))  24.4 us
    ppermute x8, starting transfers between devices, passed_along(): lax.ppermute(part, axis, [(i, (i + by) % devices) for i in range(devices)])  7.33 us
    pallas_call x3, Pallas kernels, train(): pl.pallas_call(body, out_shape=(jax.ShapeDtypeStruct((depth, width), BF16...  6.96 us
    ppermute x10, waiting for transfers between devices, routed(): lax.ppermute(one, 'blk', sorted(route.items()))  6.23 us
    pallas_call x1, Pallas kernels, finish(): pl.pallas_call(functools.partial(finish_kernel, len(last), len(moments)),...  3.2 us
    pallas_call x6, Pallas kernels, part(): pl.pallas_call(functools.partial(part_kernel, shift, n, len(slopes)), out...  3 us
  transfers between devices with their start and end apart: 18, of which 6 were waited for; matrix products, arithmetic and copies ran while one was open for 0% of the time, Pallas kernels for 10%

profile of v4, /device:TPU:0, one launch (start us, length us, event | category | flops | bytes accessed | tf_op | source)
XLA Modules:
  0.0 119.8 jit_solution(9998414791696944682)
XLA Ops:
  0.7 1.2 %cut.1 = bf16[512,512]{1,0:T(8,128)(2,1)S(1)} custom-call(bf16[512,1024]{1,0:T(8,128)(2,1)} %refs_0_.1), custom_call_target="tpu_custom_call" | custom-call | flops 4000000000 | bytes 2097152 | tf_op jit(solution)/shard_map/cut/pallas_call | solution.py:148
  1.9 5.5 %collective-permute-start = (bf16[512,512]{1,0:T(8,128)(2,1)S(1)}, bf16[512,512]{1,0:T(8,128)(2,1)S(1)}, u32[]{:S(2)}, u32[]{:S(2)}) collective-permute-start(bf16[512,512]{1,0:T(8,128)(2,1)S(1)} %cut.1), channel_id=1, source_target_pairs={{0,30},{2,4},{4,2},{6,8},{8,6},{10,12},{12,10},{14,16},{16,14},{18... | collective-permute-start | bytes 1572872 | tf_op jit(solution)/shard_map/ppermute | solution.py:25
  7.4 0.8 collective-permute-start.6
  8.2 6.2 %collective-permute-done.refs_0_ = bf16[512,512]{1,0:T(8,128)(2,1)S(1)} collective-permute-done((bf16[512,512]{1,0:T(8,128)(2,1)S(1)}, bf16[512,512]{1,0:T(8,128)(2,1)S(1)}, u32[]{:S(2)}, u32[]{:S(2)}) %collective-permute-start) | collective-permute-done | bytes 524320 | tf_op jit(solution)/shard_map/ppermute | solution.py:25
  14.4 1.9 %collective-permute-start.1 = (bf16[512,512]{1,0:T(8,128)(2,1)S(1)}, bf16[512,512]{1,0:T(8,128)(2,1)S(1)}, u32[]{:S(2)}, u32[]{:S(2)}) collective-permute-start(bf16[512,512]{1,0:T(8,128)(2,1)S(1)} %collective-permute-done.refs_0_), channel_id=1, source_target_pairs={{0,1},{1,0},{2,3},{3,2},{4,5},{5,4},{6,7},{7,6},{8,9},{9,8},{10,11... | collective-permute-start | bytes 1572872 | tf_op jit(solution)/shard_map/ppermute | solution.py:21
  16.3 7.3 %collective-permute-start.4 = (bf16[512,512]{1,0:T(8,128)(2,1)S(1)}, bf16[512,512]{1,0:T(8,128)(2,1)S(1)}, u32[]{:S(2)}, u32[]{:S(2)}) collective-permute-start(bf16[512,512]{1,0:T(8,128)(2,1)S(1)} %copy-done.3), channel_id=1, source_target_pairs={{0,2},{2,0},{4,6},{6,4},{8,10},{10,8},{12,14},{14,12},{16,18},{18,... | collective-permute-start | bytes 1572872 | tf_op jit(solution)/shard_map/ppermute | solution.py:25
  23.6 4.0 %shard_map.84 = (bf16[1024,512]{1,0:T(8,128)(2,1)S(1)}, f32[1024,512]{1,0:T(8,128)S(1)}, f32[1024,512]{1,0:T(8,128)S(1)}, bf16[512,512]{1,0:T(8,128)(2,1)S(1)}) custom-call(bf16[512,1024]{1,0:T(8,128)(2,1)} %refs_0_.1, bf16[512,512]{1,0:T(8,128)(2,1)S(1)} %copy-done.3, bf16[1024,512]{1,0:T(8,128)(2,1)S(1)} %bitcast.6, f32[1024,512]{1,0:T(8,128)S(1)} %bitcast.9, ...), custom_call_target="tpu_custom_call" | custom-call | flops 1073741824 | bytes 8388608 | tf_op jit(solution)/shard_map/pallas_call | solution.py:121
  27.7 5.9 %collective-permute-start.7 = (bf16[1024,512]{1,0:T(8,128)(2,1)S(1)}, bf16[1024,512]{1,0:T(8,128)(2,1)S(1)}, u32[]{:S(2)}, u32[]{:S(2)}) collective-permute-start(bf16[1024,512]{1,0:T(8,128)(2,1)S(1)} %get-tuple-element.27), channel_id=1, source_target_pairs={{0,2},{2,8},{4,6},{6,12},{8,10},{10,16},{12,14},{14,20},{16,18},{1... | collective-permute-start | bytes 3145736 | tf_op jit(solution)/shard_map/ppermute | solution.py:25
  33.6 2.9 %shard_map.85 = (bf16[1024,512]{1,0:T(8,128)(2,1)S(1)}, bf16[1024,512]{1,0:T(8,128)(2,1)S(1)}, bf16[1024,512]{1,0:T(8,128)(2,1)S(1)}, bf16[512,512]{1,0:T(8,128)(2,1)S(1)}) custom-call(bf16[512,1024]{1,0:T(8,128)(2,1)S(1)} %collective-permute-done.2.refs_0_.refs_2_, bf16[512,512]{1,0:T(8,128)(2,1)S(1)} %collective-permute-done.4.refs_1_.refs_4_, ...), custom_call_target="tpu_custom_call" | custom-call | flops 1073741824 | bytes 8388608 | tf_op jit(solution)/shard_map/pallas_call | solution.py:121
  36.5 0.1 collective-permute-start.5
  36.6 0.5 collective-permute-start.3
  37.1 4.2 %collective-permute-start.8 = (bf16[1024,512]{1,0:T(8,128)(2,1)S(1)}, bf16[1024,512]{1,0:T(8,128)(2,1)S(1)}, u32[]{:S(2)}, u32[]{:S(2)}) collective-permute-start(bf16[1024,512]{1,0:T(8,128)(2,1)S(1)} %get-tuple-element.31), channel_id=1, source_target_pairs={{0,6},{2,2},{4,0},{6,4},{8,14},{10,10},{12,8},{14,12},{16,22},{18,... | collective-permute-start | bytes 3145736 | tf_op jit(solution)/shard_map/ppermute | solution.py:25
  41.3 0.5 part.6
  41.8 1.6 %collective-permute-start.13 = (bf16[256,1024]{1,0:T(8,128)(2,1)S(1)}, bf16[256,1024]{1,0:T(8,128)(2,1)S(1)}, u32[]{:S(2)}, u32[]{:S(2)}) collective-permute-start(bf16[256,1024]{1,0:T(8,128)(2,1)S(1)} %part.6), channel_id=1, source_target_pairs={{0,1},{1,0},{2,3},{3,2},{4,5},{5,4},{6,7},{7,6},{8,9},{9,8},{10,11... | collective-permute-start | bytes 1572872 | tf_op jit(solution)/shard_map/ppermute | solution.py:21
  43.3 0.5 part.8
  43.8 22.7 %collective-permute-done.3.refs_3_ = bf16[512,512]{1,0:T(8,128)(2,1)S(1)} collective-permute-done((bf16[512,512]{1,0:T(8,128)(2,1)S(1)}, bf16[512,512]{1,0:T(8,128)(2,1)S(1)}, u32[]{:S(2)}, u32[]{:S(2)}) %collective-permute-start.3) | collective-permute-done | bytes 524320 | tf_op jit(solution)/shard_map/ppermute | solution.py:21
  66.5 1.5 %collective-permute-start.14 = (bf16[256,1024]{1,0:T(8,128)(2,1)S(1)}, bf16[256,1024]{1,0:T(8,128)(2,1)S(1)}, u32[]{:S(2)}, u32[]{:S(2)}) collective-permute-start(bf16[256,1024]{1,0:T(8,128)(2,1)S(1)} %part.8), channel_id=1, source_target_pairs={{0,1},{1,0},{2,3},{3,2},{4,5},{5,4},{6,7},{7,6},{8,9},{9,8},{10,11... | collective-permute-start | bytes 1572872 | tf_op jit(solution)/shard_map/ppermute | solution.py:21
  68.0 1.5 %forward.1 = (bf16[512,512]{1,0:T(8,128)(2,1)S(1)}, bf16[1024,512]{1,0:T(8,128)(2,1)S(1)}, bf16[1024,512]{1,0:T(8,128)(2,1)S(1)}) custom-call(bf16[512,512]{1,0:T(8,128)(2,1)S(1)} %collective-permute-done.refs_0_, bf16[512,512]{1,0:T(8,128)(2,1)S(1)} %collective-permute-done.1.refs_1_, bf16[512,1024]{1,0:T(8,128)(2,1)S(1)} %collective-permute-done.2.refs_0_.refs_2_, ...), custom_call_target="tpu_custom_call" | custom-call | flops 536870912 | bytes 2097152 | tf_op jit(solution)/shard_map/forward/pallas_call | solution.py:229
  69.4 0.5 part.10
  69.9 0.6 collective-permute-start.16
  70.5 9.5 %collective-permute-done.14.refs_3_ = bf16[256,1024]{1,0:T(8,128)(2,1)S(1)} collective-permute-done((bf16[256,1024]{1,0:T(8,128)(2,1)S(1)}, bf16[256,1024]{1,0:T(8,128)(2,1)S(1)}, u32[]{:S(2)}, u32[]{:S(2)}) %collective-permute-start.14) | collective-permute-done | bytes 524320 | tf_op jit(solution)/shard_map/ppermute | solution.py:21
  80.0 0.7 part.9
  80.7 0.1 collective-permute-start.9
  80.8 0.5 collective-permute-start.15
  81.3 4.4 %collective-permute-done.16.refs_2_ = bf16[256,1024]{1,0:T(8,128)(2,1)S(1)} collective-permute-done((bf16[256,1024]{1,0:T(8,128)(2,1)S(1)}, bf16[256,1024]{1,0:T(8,128)(2,1)S(1)}, u32[]{:S(2)}, u32[]{:S(2)}) %collective-permute-start.16) | collective-permute-done | bytes 524320 | tf_op jit(solution)/shard_map/ppermute | solution.py:21
  85.7 1.3 %collective-permute-start.12 = (bf16[1024,512]{1,0:T(8,128)(2,1)S(1)}, bf16[1024,512]{1,0:T(8,128)(2,1)S(1)}, u32[]{:S(2)}, u32[]{:S(2)}) collective-permute-start(bf16[1024,512]{1,0:T(8,128)(2,1)S(1)} %collective-permute-done.8.refs_0_), channel_id=1, source_target_pairs={{0,10},{8,18},{16,26},{24,2},{1,11},{9,19},{17,27},{25,3}} | collective-permute-start | bytes 3145736 | tf_op jit(solution)/shard_map/ppermute | solution.py:25
  87.0 0.5 part.11
  87.5 22.2 %collective-permute-done.15.refs_6_ = bf16[256,1024]{1,0:T(8,128)(2,1)S(1)} collective-permute-done((bf16[256,1024]{1,0:T(8,128)(2,1)S(1)}, bf16[256,1024]{1,0:T(8,128)(2,1)S(1)}, u32[]{:S(2)}, u32[]{:S(2)}) %collective-permute-start.15) | collective-permute-done | bytes 524320 | tf_op jit(solution)/shard_map/ppermute | solution.py:21
  109.7 0.5 part.7.refs_5_
  110.2 0.7 gradient.1.grad
  110.9 5.5 %collective-permute-done.17.refs_7_ = bf16[256,1024]{1,0:T(8,128)(2,1)S(1)} collective-permute-done((bf16[256,1024]{1,0:T(8,128)(2,1)S(1)}, bf16[256,1024]{1,0:T(8,128)(2,1)S(1)}, u32[]{:S(2)}, u32[]{:S(2)}) %collective-permute-start.17) | collective-permute-done | bytes 524320 | tf_op jit(solution)/shard_map/ppermute | solution.py:21
  116.4 3.2 %finish.1 = (bf16[1024,512]{1,0:T(8,128)(2,1)}, f32[1024,512]{1,0:T(8,128)}, f32[1024,512]{1,0:T(8,128)}, bf16[3,256,1024]{2,1,0:T(8,128)(2,1)}) custom-call(f32[1024,512]{1,0:T(8,128)S(1)} %gradient.1.grad, bf16[1024,512]{1,0:T(8,128)(2,1)S(1)} %get-tuple-element.30.refs_1_.w, bf16[1024,512]{1,0:T(8,128)(2,1)S(1)} %collective-permute-done.8.refs_0_, ...), custom_call_target="tpu_custom_call" | custom-call | flops 15728640 | bytes 8388608 | tf_op jit(solution)/shard_map/finish/pallas_call | solution.py:319
  (25 shorter events, 0.1 us)
Async XLA Ops:
  0.6 6.8 %copy-start.3 = (bf16[512,512]{1,0:T(8,128)(2,1)S(1)}, bf16[512,512]{1,0:T(8,128)(2,1)}, u32[]{:S(2)}) copy-start(bf16[512,512]{1,0:T(8,128)(2,1)} %refs_1_.1) | copy-start | bytes 1572868
  0.6 23.0 %copy-start.2 = (f32[1,1024,512]{2,1,0:T(8,128)S(1)}, f32[1,1024,512]{2,1,0:T(8,128)}, u32[]{:S(2)}) copy-start(f32[1,1024,512]{2,1,0:T(8,128)} %param.9) | copy-start | bytes 6291460
  0.7 23.0 %copy-start.1 = (f32[1,1024,512]{2,1,0:T(8,128)S(1)}, f32[1,1024,512]{2,1,0:T(8,128)}, u32[]{:S(2)}) copy-start(f32[1,1024,512]{2,1,0:T(8,128)} %param.8) | copy-start | bytes 6291460
  0.7 23.0 %copy-start = (bf16[1,1024,512]{2,1,0:T(8,128)(2,1)S(1)}, bf16[1,1024,512]{2,1,0:T(8,128)(2,1)}, u32[]{:S(2)}) copy-start(bf16[1,1024,512]{2,1,0:T(8,128)(2,1)} %param.7) | copy-start | bytes 3145732
  1.9 12.5 %collective-permute-start = (bf16[512,512]{1,0:T(8,128)(2,1)S(1)}, bf16[512,512]{1,0:T(8,128)(2,1)S(1)}, u32[]{:S(2)}, u32[]{:S(2)}) collective-permute-start(bf16[512,512]{1,0:T(8,128)(2,1)S(1)} %cut.1), channel_id=1, source_target_pairs={{0,30},{2,4},{4,2},{6,8},{8,6},{10,12},{12,10},{14,16},{16,14},{18... | collective-permute-start | bytes 1572872 | tf_op jit(solution)/shard_map/ppermute | solution.py:25
  7.4 26.1 %collective-permute-start.2 = (bf16[512,1024]{1,0:T(8,128)(2,1)}, bf16[512,1024]{1,0:T(8,128)(2,1)S(1)}, u32[]{:S(2)}, u32[]{:S(2)}) collective-permute-start(bf16[512,1024]{1,0:T(8,128)(2,1)} %refs_0_.1), channel_id=1, source_target_pairs={{0,2},{2,0},{4,6},{6,4},{8,10},{10,8},{12,14},{14,12},{16,18},{18,... | collective-permute-start | bytes 3145736 | tf_op jit(solution)/shard_map/ppermute | solution.py:25
  7.4 20.2 %collective-permute-start.6 = (bf16[512,512]{1,0:T(8,128)(2,1)S(1)}, bf16[512,512]{1,0:T(8,128)(2,1)S(1)}, u32[]{:S(2)}, u32[]{:S(2)}) collective-permute-start(bf16[512,512]{1,0:T(8,128)(2,1)S(1)} %copy-done.3), channel_id=1, source_target_pairs={{0,30},{2,0},{4,2},{6,4},{8,6},{10,8},{12,10},{14,12},{16,14},{18,... | collective-permute-start | bytes 1572872 | tf_op jit(solution)/shard_map/ppermute | solution.py:21
  14.4 13.2 %collective-permute-start.1 = (bf16[512,512]{1,0:T(8,128)(2,1)S(1)}, bf16[512,512]{1,0:T(8,128)(2,1)S(1)}, u32[]{:S(2)}, u32[]{:S(2)}) collective-permute-start(bf16[512,512]{1,0:T(8,128)(2,1)S(1)} %collective-permute-done.refs_0_), channel_id=1, source_target_pairs={{0,1},{1,0},{2,3},{3,2},{4,5},{5,4},{6,7},{7,6},{8,9},{9,8},{10,11... | collective-permute-start | bytes 1572872 | tf_op jit(solution)/shard_map/ppermute | solution.py:21
  16.3 17.2 %collective-permute-start.4 = (bf16[512,512]{1,0:T(8,128)(2,1)S(1)}, bf16[512,512]{1,0:T(8,128)(2,1)S(1)}, u32[]{:S(2)}, u32[]{:S(2)}) collective-permute-start(bf16[512,512]{1,0:T(8,128)(2,1)S(1)} %copy-done.3), channel_id=1, source_target_pairs={{0,2},{2,0},{4,6},{6,4},{8,10},{10,8},{12,14},{14,12},{16,18},{18,... | collective-permute-start | bytes 1572872 | tf_op jit(solution)/shard_map/ppermute | solution.py:25
  27.7 40.3 %collective-permute-start.7 = (bf16[1024,512]{1,0:T(8,128)(2,1)S(1)}, bf16[1024,512]{1,0:T(8,128)(2,1)S(1)}, u32[]{:S(2)}, u32[]{:S(2)}) collective-permute-start(bf16[1024,512]{1,0:T(8,128)(2,1)S(1)} %get-tuple-element.27), channel_id=1, source_target_pairs={{0,2},{2,8},{4,6},{6,12},{8,10},{10,16},{12,14},{14,20},{16,18},{1... | collective-permute-start | bytes 3145736 | tf_op jit(solution)/shard_map/ppermute | solution.py:25
  36.5 31.5 %collective-permute-start.5 = (bf16[1024,512]{1,0:T(8,128)(2,1)S(1)}, bf16[1024,512]{1,0:T(8,128)(2,1)S(1)}, u32[]{:S(2)}, u32[]{:S(2)}) collective-permute-start(bf16[1024,512]{1,0:T(8,128)(2,1)S(1)} %get-tuple-element.26), channel_id=1, source_target_pairs={{0,6},{2,0},{4,10},{6,4},{8,14},{10,8},{12,18},{14,12},{16,22},{18... | collective-permute-start | bytes 3145736 | tf_op jit(solution)/shard_map/ppermute | solution.py:25
  36.6 29.9 %collective-permute-start.3 = (bf16[512,512]{1,0:T(8,128)(2,1)S(1)}, bf16[512,512]{1,0:T(8,128)(2,1)S(1)}, u32[]{:S(2)}, u32[]{:S(2)}) collective-permute-start(bf16[512,512]{1,0:T(8,128)(2,1)S(1)} %copy-done.3), channel_id=1, source_target_pairs={{0,2},{2,4},{4,6},{6,8},{8,10},{10,12},{12,14},{14,16},{16,18},{18... | collective-permute-start | bytes 1572872 | tf_op jit(solution)/shard_map/ppermute | solution.py:21
  37.1 43.7 %collective-permute-start.8 = (bf16[1024,512]{1,0:T(8,128)(2,1)S(1)}, bf16[1024,512]{1,0:T(8,128)(2,1)S(1)}, u32[]{:S(2)}, u32[]{:S(2)}) collective-permute-start(bf16[1024,512]{1,0:T(8,128)(2,1)S(1)} %get-tuple-element.31), channel_id=1, source_target_pairs={{0,6},{2,2},{4,0},{6,4},{8,14},{10,10},{12,8},{14,12},{16,22},{18,... | collective-permute-start | bytes 3145736 | tf_op jit(solution)/shard_map/ppermute | solution.py:25
  41.8 38.9 %collective-permute-start.13 = (bf16[256,1024]{1,0:T(8,128)(2,1)S(1)}, bf16[256,1024]{1,0:T(8,128)(2,1)S(1)}, u32[]{:S(2)}, u32[]{:S(2)}) collective-permute-start(bf16[256,1024]{1,0:T(8,128)(2,1)S(1)} %part.6), channel_id=1, source_target_pairs={{0,1},{1,0},{2,3},{3,2},{4,5},{5,4},{6,7},{7,6},{8,9},{9,8},{10,11... | collective-permute-start | bytes 1572872 | tf_op jit(solution)/shard_map/ppermute | solution.py:21
  66.5 13.6 %collective-permute-start.14 = (bf16[256,1024]{1,0:T(8,128)(2,1)S(1)}, bf16[256,1024]{1,0:T(8,128)(2,1)S(1)}, u32[]{:S(2)}, u32[]{:S(2)}) collective-permute-start(bf16[256,1024]{1,0:T(8,128)(2,1)S(1)} %part.8), channel_id=1, source_target_pairs={{0,1},{1,0},{2,3},{3,2},{4,5},{5,4},{6,7},{7,6},{8,9},{9,8},{10,11... | collective-permute-start | bytes 1572872 | tf_op jit(solution)/shard_map/ppermute | solution.py:21
  69.9 15.7 %collective-permute-start.16 = (bf16[256,1024]{1,0:T(8,128)(2,1)S(1)}, bf16[256,1024]{1,0:T(8,128)(2,1)S(1)}, u32[]{:S(2)}, u32[]{:S(2)}) collective-permute-start(bf16[256,1024]{1,0:T(8,128)(2,1)S(1)} %part.10), channel_id=1, source_target_pairs={{0,1},{1,0},{2,3},{3,2},{4,5},{5,4},{6,7},{7,6},{8,9},{9,8},{10,11... | collective-permute-start | bytes 1572872 | tf_op jit(solution)/shard_map/ppermute | solution.py:21
  70.5 40.4 %collective-permute-start.10 = (bf16[1024,512]{1,0:T(8,128)(2,1)S(1)}, bf16[1024,512]{1,0:T(8,128)(2,1)S(1)}, u32[]{:S(2)}, u32[]{:S(2)}) collective-permute-start(bf16[1024,512]{1,0:T(8,128)(2,1)S(1)} %get-tuple-element.33), channel_id=1, source_target_pairs={{0,2},{2,8},{4,6},{6,12},{8,10},{10,16},{12,14},{14,20},{16,18},{1... | collective-permute-start | bytes 3145736 | tf_op jit(solution)/shard_map/ppermute | solution.py:25
  80.0 30.9 %collective-permute-start.11 = (bf16[1024,512]{1,0:T(8,128)(2,1)S(1)}, bf16[1024,512]{1,0:T(8,128)(2,1)S(1)}, u32[]{:S(2)}, u32[]{:S(2)}) collective-permute-start(bf16[1024,512]{1,0:T(8,128)(2,1)S(1)} %get-tuple-element.34), channel_id=1, source_target_pairs={{0,2},{2,8},{4,6},{6,12},{8,10},{10,16},{12,14},{14,20},{16,18},{1... | collective-permute-start | bytes 3145736 | tf_op jit(solution)/shard_map/ppermute | solution.py:25
  80.7 30.2 %collective-permute-start.9 = (bf16[1024,512]{1,0:T(8,128)(2,1)S(1)}, bf16[1024,512]{1,0:T(8,128)(2,1)S(1)}, u32[]{:S(2)}, u32[]{:S(2)}) collective-permute-start(bf16[1024,512]{1,0:T(8,128)(2,1)S(1)} %get-tuple-element.32), channel_id=1, source_target_pairs={{0,6},{2,0},{4,10},{6,4},{8,14},{10,8},{12,18},{14,12},{16,22},{18... | collective-permute-start | bytes 3145736 | tf_op jit(solution)/shard_map/ppermute | solution.py:25
  80.8 28.9 %collective-permute-start.15 = (bf16[256,1024]{1,0:T(8,128)(2,1)S(1)}, bf16[256,1024]{1,0:T(8,128)(2,1)S(1)}, u32[]{:S(2)}, u32[]{:S(2)}) collective-permute-start(bf16[256,1024]{1,0:T(8,128)(2,1)S(1)} %part.9), channel_id=1, source_target_pairs={{0,2},{2,4},{4,6},{6,8},{8,10},{10,12},{12,14},{14,16},{16,18},{18... | collective-permute-start | bytes 1572872 | tf_op jit(solution)/shard_map/ppermute | solution.py:21
  85.7 25.3 %collective-permute-start.12 = (bf16[1024,512]{1,0:T(8,128)(2,1)S(1)}, bf16[1024,512]{1,0:T(8,128)(2,1)S(1)}, u32[]{:S(2)}, u32[]{:S(2)}) collective-permute-start(bf16[1024,512]{1,0:T(8,128)(2,1)S(1)} %collective-permute-done.8.refs_0_), channel_id=1, source_target_pairs={{0,10},{8,18},{16,26},{24,2},{1,11},{9,19},{17,27},{25,3}} | collective-permute-start | bytes 3145736 | tf_op jit(solution)/shard_map/ppermute | solution.py:25
  109.7 6.7 %collective-permute-start.17 = (bf16[256,1024]{1,0:T(8,128)(2,1)S(1)}, bf16[256,1024]{1,0:T(8,128)(2,1)S(1)}, u32[]{:S(2)}, u32[]{:S(2)}) collective-permute-start(bf16[256,1024]{1,0:T(8,128)(2,1)S(1)} %part.11), channel_id=1, source_target_pairs={{0,30},{2,0},{4,2},{6,4},{8,6},{10,8},{12,10},{14,12},{16,14},{18,... | collective-permute-start | bytes 1572872 | tf_op jit(solution)/shard_map/ppermute | solution.py:21

commit v5 on v4

--- a/solution.py
+++ b/solution.py
@@ -157,32 +157,36 @@
     )(inputs)
 
 
-def part_kernel(shift, n, several, *refs):
-    slopes, (w_in, *arrived, out) = refs[:several], refs[several:]
+def part_kernel(shift, n, parities, *refs):
+    *given, out = refs
+    each = len(given) // len(parities)
     owner = lax.rem(lax.axis_index("shard") + shift, n)
-    rows = slopes[0].shape[0] // n
+    rows = out.shape[0]
     at = pl.ds(pl.multiple_of(owner * rows, rows), rows)
-    for parity, s_in in enumerate(slopes):
-
-        def body(s_in=s_in):
+    for i, parity in enumerate(parities):
+
+        def body(s_in, w_in, *arrived):
             total = lax.dot_general(s_in[at, :], w_in[...], (((1,), (1,)), ((), ())), preferred_element_type=F32)
             for piece in arrived:
                 total = total + piece[...].astype(F32)
             out[...] = total.astype(BF16)
 
-        only_if(None if several == 1 else lax.rem(lax.axis_index("blk"), 2) == parity, body)
-
-
-def part(slopes, kernel, shift, arrived=()):
+        mine = given[i * each : (i + 1) * each]
+        chosen = None if parity is None else lax.rem(lax.axis_index("blk"), 2) == parity
+        only_if(chosen, functools.partial(body, *mine))
+
+
+def part(cases, shift):
     n = lax.axis_size("shard")
-    rows, depth = slopes[0].shape[0] // n, kernel.shape[0]
-    return pl.pallas_call(
-        functools.partial(part_kernel, shift, n, len(slopes)),
+    slopes, kernel = next(iter(cases.values()))[:2]
+    rows, depth = slopes.shape[0] // n, kernel.shape[0]
+    return pl.pallas_call(
+        functools.partial(part_kernel, shift, n, tuple(cases)),
         out_shape=jax.ShapeDtypeStruct((rows, depth), BF16),
         compiler_params=pltpu.CompilerParams(vmem_limit_bytes=16 * MIB),
         cost_estimate=pl.CostEstimate(flops=2 * rows * kernel.size, bytes_accessed=2 * kernel.size, transcendentals=0),
         name="part",
-    )(*slopes, kernel, *arrived)
+    )(*[one for case in cases.values() for one in case])
 
 
 def from_one_of(chosen, dst, sem):
@@ -196,84 +200,71 @@
     return lax.rem(lax.axis_index("blk") + (n - HOPS % n), n)
 
 
-def forward_kernel(shards, *refs):
-    across, (x_near, g_across, g_near, w_even, w_odd, s, w, xt, x, g, z, sem) = refs[:shards], refs[shards:]
-    odd_here = lax.rem(lax.axis_index("blk"), 2) == 1
-    odd_source = lax.rem(sources(), 2) == 1
-
-    def start(copies):
-        for copy in copies:
-            copy.start()
-
-    def wait(copies):
-        for copy in copies:
-            copy.wait()
-
-    sems = [sem.at[k] for k in range(shards)]
-    pl.when(odd_here)(lambda: start(copies_of([x_near], x, sems)))
-    pl.when(jnp.logical_not(odd_here))(lambda: start(copies_of(across, x, sems)))
-    gets = [
-        from_one_of([(jnp.logical_not(odd_here), g_across), (odd_here, g_near)], g, sem.at[shards]),
-        from_one_of([(jnp.logical_not(odd_source), w_even), (odd_source, w_odd)], w, sem.at[shards + 1]),
-    ]
-    pl.when(odd_here)(lambda: wait(copies_of([x_near], x, sems)))
-    pl.when(jnp.logical_not(odd_here))(lambda: wait(copies_of(across, x, sems)))
-    wait(gets)
-    slopes_body(x, g, w, z, s)
-    xt[...] = x[...].T
-
-
-def forward(across, x_near, g_across, g_near, even, odd):
-    (tokens, width), depth = g_near.shape, even.shape[0]
-    n = len(across)
-    return pl.pallas_call(
-        functools.partial(forward_kernel, n),
+def forward_kernel(parity, shards, *refs):
+    x_in, (g, w, s, xt, x, z, sem) = refs[:shards], refs[shards:]
+
+    @pl.when(lax.rem(lax.axis_index("blk"), 2) == parity)
+    def _():
+        gets = copies_of(x_in, x, [sem.at[k] for k in range(shards)])
+        for get in gets:
+            get.start()
+        for get in gets:
+            get.wait()
+        slopes_body(x, g, w, z, s)
+        xt[...] = x[...].T
+
+
+def forward(inputs, grad_out, kernel, parity):
+    (tokens, width), depth = grad_out.shape, kernel.shape[0]
+    n = len(inputs)
+    return pl.pallas_call(
+        functools.partial(forward_kernel, parity, n),
         out_shape=(
             jax.ShapeDtypeStruct((tokens, width), BF16),
-            jax.ShapeDtypeStruct((depth, width), BF16),
             jax.ShapeDtypeStruct((depth, tokens), BF16),
         ),
-        in_specs=[ANY] * (n + 5),
-        out_specs=(WHOLE,) * 3,
+        in_specs=[ANY] * n + [WHOLE] * 2,
+        out_specs=(WHOLE,) * 2,
         scratch_shapes=[
             pltpu.VMEM((tokens, depth), BF16),
-            pltpu.VMEM((tokens, width), BF16),
             pltpu.VMEM((tokens, width), F32),
-            pltpu.SemaphoreType.DMA((n + 2,)),
+            pltpu.SemaphoreType.DMA((n,)),
         ],
         compiler_params=pltpu.CompilerParams(vmem_limit_bytes=16 * MIB),
         cost_estimate=pl.CostEstimate(
             flops=2 * tokens * depth * width, bytes_accessed=4 * depth * width, transcendentals=0
         ),
-        name="forward",
-    )(*across, x_near, g_across, g_near, even, odd)
-
-
-def gradient_kernel(xt, s, grad):
-    grad[...] = jnp.dot(xt[...], s[...], preferred_element_type=F32)
-
-
-def gradient(transposed, slopes):
-    depth, tokens = transposed.shape
-    width = slopes.shape[1]
+    )(*inputs, grad_out, kernel)
+
+
+def gradient_kernel(*refs):
+    *given, grad, w = refs
+    for parity in range(2):
+
+        def body(s_in, xt_in, w_in):
+            grad[...] = jnp.dot(xt_in[...], s_in[...], preferred_element_type=F32)
+            w[...] = w_in[...]
+
+        only_if(lax.rem(lax.axis_index("blk"), 2) == parity, functools.partial(body, *given[3 * parity : 3 * parity + 3]))
+
+
+def gradient(even, odd):
+    (depth, tokens), width = even[1].shape, even[0].shape[1]
     return pl.pallas_call(
         gradient_kernel,
-        out_shape=jax.ShapeDtypeStruct((depth, width), F32),
-        compiler_params=pltpu.CompilerParams(vmem_limit_bytes=16 * MIB),
+        out_shape=(jax.ShapeDtypeStruct((depth, width), F32), jax.ShapeDtypeStruct((depth, width), BF16)),
+        compiler_params=pltpu.CompilerParams(vmem_limit_bytes=24 * MIB),
         cost_estimate=pl.CostEstimate(
             flops=2 * tokens * depth * width, bytes_accessed=4 * depth * width, transcendentals=0
         ),
         name="gradient",
-    )(transposed, slopes)
-
-
-def finish_kernel(shards, moments, grad, w, *refs):
-    given, refs = refs[:moments], refs[moments:]
-    home, back, refs = refs[0], refs[1], refs[2:]
-    last, (w_out, m_out, v_out, r_out, m, v, w_new, m_new, v_new, r, sem) = refs[:shards], refs[shards:]
+    )(*even, *odd)
+
+
+def finish_kernel(moments, grad, w, *refs):
+    given, (w_out, m_out, v_out, m, v, w_new, m_new, v_new, sem) = refs[:moments], refs[moments:]
     m_even, v_even, m_odd, v_odd, *m_detour = given
     bands = blocks(w.shape[0], 256)
-    n = len(bands)
     origin = sources()
     even, odd = lax.rem(origin, 2) == 0, lax.rem(origin, 2) == 1
     m_from, v_from = [(odd, m_odd)], [(even, v_even), (odd, v_odd)]
@@ -288,15 +279,7 @@
         ]
         for i, band in enumerate(bands)
     ]
-    total = last[0][...].astype(F32)
-    for piece in last[1:]:
-        total = total + piece[...].astype(F32)
-    r[...] = total.astype(BF16)
-    puts = [
-        pltpu.make_async_copy(one, r_out.at[i], sem.at[5 * n + i]) for i, one in enumerate((home, back, r))
-    ]
-    for put in puts:
-        put.start()
+    puts = []
     for i, band in enumerate(bands):
         for get in gets[i]:
             get.wait()
@@ -312,33 +295,52 @@
         put.wait()
 
 
-def finish(grad, kernel, moments, home, back, last):
+def finish(grad, kernel, moments):
     depth, width = kernel.shape
-    rows = home.shape
     n = len(blocks(depth, 256))
     return pl.pallas_call(
-        functools.partial(finish_kernel, len(last), len(moments)),
+        functools.partial(finish_kernel, len(moments)),
         out_shape=(
             jax.ShapeDtypeStruct((depth, width), BF16),
             jax.ShapeDtypeStruct((depth, width), F32),
             jax.ShapeDtypeStruct((depth, width), F32),
-            jax.ShapeDtypeStruct((HOPS,) + rows, BF16),
-        ),
-        in_specs=[WHOLE] * 2 + [ANY] * len(moments) + [WHOLE] * (2 + len(last)),
-        out_specs=(ANY,) * 4,
+        ),
+        in_specs=[WHOLE] * 2 + [ANY] * len(moments),
+        out_specs=(ANY,) * 3,
         scratch_shapes=[
             pltpu.VMEM((depth, width), BF16),
             pltpu.VMEM((depth, width), BF16),
             pltpu.VMEM((depth, width), BF16),
             pltpu.VMEM((depth, width), F32),
             pltpu.VMEM((depth, width), F32),
-            pltpu.VMEM(rows, BF16),
-            pltpu.SemaphoreType.DMA((5 * n + HOPS,)),
+            pltpu.SemaphoreType.DMA((5 * n,)),
         ],
         compiler_params=pltpu.CompilerParams(vmem_limit_bytes=24 * MIB),
         cost_estimate=pl.CostEstimate(flops=30 * depth * width, bytes_accessed=16 * depth * width, transcendentals=0),
         name="finish",
-    )(grad, kernel, *moments, home, back, *last)
+    )(grad, kernel, *moments)
+
+
+def collect_kernel(*refs):
+    *returned, out, sem = refs
+    puts = [pltpu.make_async_copy(one, out.at[i], sem.at[i]) for i, one in enumerate(returned)]
+    for put in puts:
+        put.start()
+    for put in puts:
+        put.wait()
+
+
+def collect(*returned):
+    return pl.pallas_call(
+        collect_kernel,
+        out_shape=jax.ShapeDtypeStruct((len(returned),) + returned[0].shape, BF16),
+        in_specs=[WHOLE] * len(returned),
+        out_specs=ANY,
+        scratch_shapes=[pltpu.SemaphoreType.DMA((len(returned),))],
+        compiler_params=pltpu.CompilerParams(vmem_limit_bytes=8 * MIB),
+        cost_estimate=pl.CostEstimate(flops=returned[0].size, bytes_accessed=12 * returned[0].size, transcendentals=0),
+        name="collect",
+    )(*returned)
 
 
 def shards(cut_acts, upstream, weights, moment_one, moment_two):
@@ -375,19 +377,27 @@
     if detour:
         moments += (routed(even_m, {i: (i + 2 + HOPS) % n for i in range(0, n, 4)}),)
 
-    def summed(slopes, kernel):
-        parts = [part(slopes, kernel, k) for k in range(1, m)]
-        parts = [passed_along(one, "shard", k + 1) for k, one in enumerate(parts)]
-        return part(slopes, kernel, 0, parts)
-
-    home = summed([slopes0], kernel)
-    back = summed([slopes_even, slopes_odd], kernel1)
+    def sent(cases, places):
+        routes = {k: [(i * m + s, i * m + (s + k) % m) for i in places for s in range(m)] for k in range(1, m)}
+        parts = {k: part(cases, k) for k in routes}
+        return [lax.ppermute(parts[k], ("blk", "shard"), route) for k, route in routes.items()]
+
+    case0 = {None: (slopes0, kernel)}
+    case1 = {0: (slopes_even, kernel1), 1: (slopes_odd, kernel1)}
+    arrived0, arrived1 = sent(case0, range(n)), sent(case1, range(n))
+    home = part({None: (*case0[None], *arrived0)}, 0)
+    back = part({parity: (*case, *arrived1) for parity, case in case1.items()}, 0)
     back = passed_along(back, "blk", 1)
 
-    slopes2, moved, transposed = forward(across, near_x, before_g, near_g, even_w, odd_w)
-    last = passed_along(summed([slopes2], moved), "blk", -1)
-    grad2 = gradient(transposed, slopes2)
-    kernel3, first3, second3, returned = finish(grad2, moved, moments, home, back, [last])
+    slopes_o, turned_o = forward([near_x], near_g, even_w, 1)
+    arrived_o = sent({1: (slopes_o, even_w)}, odds)
+    slopes_e, turned_e = forward(across, before_g, odd_w, 0)
+    arrived_e = sent({0: (slopes_e, odd_w)}, evens)
+    last = part({0: (slopes_e, odd_w, *arrived_e), 1: (slopes_o, even_w, *arrived_o)}, 0)
+    last = passed_along(last, "blk", -1)
+    grad2, moved = gradient((slopes_e, turned_e, odd_w), (slopes_o, turned_o, even_w))
+    kernel3, first3, second3 = finish(grad2, moved, moments)
+    returned = collect(home, back, last)
     return (kernel3[None], first3[None], second3[None], returned)
 
 

time: 120 us -> 119 us (level)
  waiting for transfers between devices: 70.5 us -> 60.4 us
  starting transfers between devices: 31.7 us -> 39.3 us
    ppermute x8 -> x5, waiting for transfers between devices: 64.3 us -> 23.1 us  [passed_along(): lax.ppermute(part, axis, [(i, (i + by) % devices) for i in range(devices)])]
    ppermute x0 -> x4, waiting for transfers between devices: none -> 16.1 us  [sent(): lax.ppermute(parts[k], ('blk', 'shard'), route)]
    ppermute x10, waiting for transfers between devices: 6.23 us -> 21.2 us  [routed(): lax.ppermute(one, 'blk', sorted(route.items()))]
    ppermute x0 -> x4, starting transfers between devices: none -> 7.22 us  [sent(): lax.ppermute(parts[k], ('blk', 'shard'), route)]
    pallas_call x9 -> x12, Pallas kernels: 8.37 us -> 9.41 us  [the longest x7 3.07 us: part(): pl.pallas_call(functools.partial(part_kernel, shift, n, tuple(cases)), ou...]
    ppermute x8 -> x5, starting transfers between devices: 7.33 us -> 7.63 us  [passed_along(): lax.ppermute(part, axis, [(i, (i + by) % devices) for i in range(devices)])]
  transfers between devices with their start and end apart: 18 -> 19, of which waited for: 6 -> 5; matrix products, arithmetic and copies ran while one was open for 0% -> 0% of each run, Pallas kernels for 10% -> 13%
where the time goes in v5:
time: 119 us; the launch traced here: 118 us
  waiting for transfers between devices  60.4 us (51%)
  starting transfers between devices  39.3 us (33%)
  Pallas kernels  17.6 us (15%)
    ppermute x10, starting transfers between devices, routed(): lax.ppermute(one, 'blk', sorted(route.items()))  24.5 us
    ppermute x5, waiting for transfers between devices, passed_along(): lax.ppermute(part, axis, [(i, (i + by) % devices) for i in range(devices)])  23.1 us
    ppermute x10, waiting for transfers between devices, routed(): lax.ppermute(one, 'blk', sorted(route.items()))  21.2 us
    ppermute x4, waiting for transfers between devices, sent(): lax.ppermute(parts[k], ('blk', 'shard'), route)  16.1 us
    ppermute x5, starting transfers between devices, passed_along(): lax.ppermute(part, axis, [(i, (i + by) % devices) for i in range(devices)])  7.63 us
    ppermute x4, starting transfers between devices, sent(): lax.ppermute(parts[k], ('blk', 'shard'), route)  7.22 us
    pallas_call x3, Pallas kernels, train(): pl.pallas_call(body, out_shape=(jax.ShapeDtypeStruct((depth, width), BF16...  6.96 us
    pallas_call x7, Pallas kernels, part(): pl.pallas_call(functools.partial(part_kernel, shift, n, tuple(cases)), ou...  3.07 us
  transfers between devices with their start and end apart: 19, of which 5 were waited for; matrix products, arithmetic and copies ran while one was open for 0% of the time, Pallas kernels for 13%

profile of v5, /device:TPU:0, one launch (start us, length us, event | category | flops | bytes accessed | tf_op | source)
XLA Modules:
  0.0 118.4 jit_solution(16627270468456978468)
XLA Ops:
  0.7 1.2 %cut.1 = bf16[512,512]{1,0:T(8,128)(2,1)S(1)} custom-call(bf16[512,1024]{1,0:T(8,128)(2,1)} %refs_0_.1), custom_call_target="tpu_custom_call" | custom-call | flops 4000000000 | bytes 2097152 | tf_op jit(solution)/shard_map/cut/pallas_call | solution.py:148
  1.9 5.5 %collective-permute-start = (bf16[512,512]{1,0:T(8,128)(2,1)S(1)}, bf16[512,512]{1,0:T(8,128)(2,1)S(1)}, u32[]{:S(2)}, u32[]{:S(2)}) collective-permute-start(bf16[512,512]{1,0:T(8,128)(2,1)S(1)} %cut.1), channel_id=1, source_target_pairs={{0,30},{2,4},{4,2},{6,8},{8,6},{10,12},{12,10},{14,16},{16,14},{18... | collective-permute-start | bytes 1572872 | tf_op jit(solution)/shard_map/ppermute | solution.py:25
  7.4 0.8 collective-permute-start.3
  8.2 6.2 %collective-permute-done.refs_0_ = bf16[512,512]{1,0:T(8,128)(2,1)S(1)} collective-permute-done((bf16[512,512]{1,0:T(8,128)(2,1)S(1)}, bf16[512,512]{1,0:T(8,128)(2,1)S(1)}, u32[]{:S(2)}, u32[]{:S(2)}) %collective-permute-start) | collective-permute-done | bytes 524320 | tf_op jit(solution)/shard_map/ppermute | solution.py:25
  14.4 1.9 %collective-permute-start.1 = (bf16[512,512]{1,0:T(8,128)(2,1)S(1)}, bf16[512,512]{1,0:T(8,128)(2,1)S(1)}, u32[]{:S(2)}, u32[]{:S(2)}) collective-permute-start(bf16[512,512]{1,0:T(8,128)(2,1)S(1)} %collective-permute-done.refs_0_), channel_id=1, source_target_pairs={{0,1},{1,0},{2,3},{3,2},{4,5},{5,4},{6,7},{7,6},{8,9},{9,8},{10,11... | collective-permute-start | bytes 1572872 | tf_op jit(solution)/shard_map/ppermute | solution.py:21
  16.3 7.3 %collective-permute-start.6 = (bf16[512,512]{1,0:T(8,128)(2,1)S(1)}, bf16[512,512]{1,0:T(8,128)(2,1)S(1)}, u32[]{:S(2)}, u32[]{:S(2)}) collective-permute-start(bf16[512,512]{1,0:T(8,128)(2,1)S(1)} %copy-done.3), channel_id=1, source_target_pairs={{0,2},{2,0},{4,6},{6,4},{8,10},{10,8},{12,14},{14,12},{16,18},{18,... | collective-permute-start | bytes 1572872 | tf_op jit(solution)/shard_map/ppermute | solution.py:25
  23.6 4.0 %shard_map.84 = (bf16[1024,512]{1,0:T(8,128)(2,1)S(1)}, f32[1024,512]{1,0:T(8,128)S(1)}, f32[1024,512]{1,0:T(8,128)S(1)}, bf16[512,512]{1,0:T(8,128)(2,1)S(1)}) custom-call(bf16[512,1024]{1,0:T(8,128)(2,1)} %refs_0_.1, bf16[512,512]{1,0:T(8,128)(2,1)S(1)} %copy-done.3, bf16[1024,512]{1,0:T(8,128)(2,1)S(1)} %bitcast.6, f32[1024,512]{1,0:T(8,128)S(1)} %bitcast.9, ...), custom_call_target="tpu_custom_call" | custom-call | flops 1073741824 | bytes 8388608 | tf_op jit(solution)/shard_map/pallas_call | solution.py:121
  27.7 5.9 %collective-permute-start.4 = (bf16[1024,512]{1,0:T(8,128)(2,1)S(1)}, bf16[1024,512]{1,0:T(8,128)(2,1)S(1)}, u32[]{:S(2)}, u32[]{:S(2)}) collective-permute-start(bf16[1024,512]{1,0:T(8,128)(2,1)S(1)} %get-tuple-element.28), channel_id=1, source_target_pairs={{0,2},{2,8},{4,6},{6,12},{8,10},{10,16},{12,14},{14,20},{16,18},{1... | collective-permute-start | bytes 3145736 | tf_op jit(solution)/shard_map/ppermute | solution.py:25
  33.6 2.9 %shard_map.87 = (bf16[1024,512]{1,0:T(8,128)(2,1)S(1)}, bf16[1024,512]{1,0:T(8,128)(2,1)S(1)}, bf16[1024,512]{1,0:T(8,128)(2,1)S(1)}, bf16[512,512]{1,0:T(8,128)(2,1)S(1)}) custom-call(bf16[512,1024]{1,0:T(8,128)(2,1)S(1)} %collective-permute-done.5.refs_0_, bf16[512,512]{1,0:T(8,128)(2,1)S(1)} %collective-permute-done.6.refs_1_, ...), custom_call_target="tpu_custom_call" | custom-call | flops 1073741824 | bytes 8388608 | tf_op jit(solution)/shard_map/pallas_call | solution.py:121
  36.6 0.5 collective-permute-start.2
  37.1 4.2 %collective-permute-start.8 = (bf16[1024,512]{1,0:T(8,128)(2,1)S(1)}, bf16[1024,512]{1,0:T(8,128)(2,1)S(1)}, u32[]{:S(2)}, u32[]{:S(2)}) collective-permute-start(bf16[1024,512]{1,0:T(8,128)(2,1)S(1)} %get-tuple-element.36), channel_id=1, source_target_pairs={{0,6},{2,2},{4,0},{6,4},{8,14},{10,10},{12,8},{14,12},{16,22},{18,... | collective-permute-start | bytes 3145736 | tf_op jit(solution)/shard_map/ppermute | solution.py:25
  41.3 0.5 part.9
  41.8 1.6 %collective-permute-start.14 = (bf16[256,1024]{1,0:T(8,128)(2,1)S(1)}, bf16[256,1024]{1,0:T(8,128)(2,1)S(1)}, u32[]{:S(2)}, u32[]{:S(2)}) collective-permute-start(bf16[256,1024]{1,0:T(8,128)(2,1)S(1)} %part.9), channel_id=1, source_target_pairs={{0,1},{1,0},{2,3},{3,2},{4,5},{5,4},{6,7},{7,6},{8,9},{9,8},{10,11... | collective-permute-start | bytes 1572872 | tf_op jit(solution)/shard_map/ppermute | solution.py:383
  43.3 23.1 %collective-permute-done.2.refs_2_ = bf16[512,512]{1,0:T(8,128)(2,1)S(1)} collective-permute-done((bf16[512,512]{1,0:T(8,128)(2,1)S(1)}, bf16[512,512]{1,0:T(8,128)(2,1)S(1)}, u32[]{:S(2)}, u32[]{:S(2)}) %collective-permute-start.2) | collective-permute-done | bytes 524320 | tf_op jit(solution)/shard_map/ppermute | solution.py:21
  66.5 1.3 %shard_map.86 = (bf16[512,512]{1,0:T(8,128)(2,1)S(1)}, bf16[1024,512]{1,0:T(8,128)(2,1)S(1)}) custom-call(bf16[512,512]{1,0:T(8,128)(2,1)S(1)} %collective-permute-done.refs_0_, bf16[512,512]{1,0:T(8,128)(2,1)S(1)} %collective-permute-done.1.refs_1_, bf16[512,512]{1,0:T(8,128)(2,1)S(1)} %collective-permute-done.2.refs_2_, ...), custom_call_target="tpu_custom_call" | custom-call | flops 536870912 | bytes 2097152 | tf_op jit(solution)/shard_map/pallas_call | solution.py:220
  67.8 0.5 part.11
  68.3 3.4 %collective-permute-start.16 = (bf16[256,1024]{1,0:T(8,128)(2,1)S(1)}, bf16[256,1024]{1,0:T(8,128)(2,1)S(1)}, u32[]{:S(2)}, u32[]{:S(2)}) collective-permute-start(bf16[256,1024]{1,0:T(8,128)(2,1)S(1)} %part.11), channel_id=1, source_target_pairs={{0,1},{1,0},{4,5},{5,4},{8,9},{9,8},{12,13},{13,12},{16,17},{17,16... | collective-permute-start | bytes 1572872 | tf_op jit(solution)/shard_map/ppermute | solution.py:383
  71.8 0.2 part.12
  72.0 0.7 collective-permute-start.17
  72.9 9.4 %collective-permute-done.16.refs_2_ = bf16[256,1024]{1,0:T(8,128)(2,1)S(1)} collective-permute-done((bf16[256,1024]{1,0:T(8,128)(2,1)S(1)}, bf16[256,1024]{1,0:T(8,128)(2,1)S(1)}, u32[]{:S(2)}, u32[]{:S(2)}) %collective-permute-start.16) | collective-permute-done | bytes 524320 | tf_op jit(solution)/shard_map/ppermute | solution.py:383
  82.3 1.3 %collective-permute-start.12 = (bf16[1024,512]{1,0:T(8,128)(2,1)S(1)}, bf16[1024,512]{1,0:T(8,128)(2,1)S(1)}, u32[]{:S(2)}, u32[]{:S(2)}) collective-permute-start(bf16[1024,512]{1,0:T(8,128)(2,1)S(1)} %collective-permute-done.8.refs_0_), channel_id=1, source_target_pairs={{0,10},{8,18},{16,26},{24,2},{1,11},{9,19},{17,27},{25,3}} | collective-permute-start | bytes 3145736 | tf_op jit(solution)/shard_map/ppermute | solution.py:25
  83.6 0.5 part.7
  84.1 1.6 %collective-permute-start.13 = (bf16[256,1024]{1,0:T(8,128)(2,1)S(1)}, bf16[256,1024]{1,0:T(8,128)(2,1)S(1)}, u32[]{:S(2)}, u32[]{:S(2)}) collective-permute-start(bf16[256,1024]{1,0:T(8,128)(2,1)S(1)} %part.7), channel_id=1, source_target_pairs={{0,1},{1,0},{2,3},{3,2},{4,5},{5,4},{6,7},{7,6},{8,9},{9,8},{10,11... | collective-permute-start | bytes 1572872 | tf_op jit(solution)/shard_map/ppermute | solution.py:383
  85.7 0.5 part.10
  86.2 0.5 part.13
  86.7 6.7 %collective-permute-done.13.refs_2_ = bf16[256,1024]{1,0:T(8,128)(2,1)S(1)} collective-permute-done((bf16[256,1024]{1,0:T(8,128)(2,1)S(1)}, bf16[256,1024]{1,0:T(8,128)(2,1)S(1)}, u32[]{:S(2)}, u32[]{:S(2)}) %collective-permute-start.13) | collective-permute-done | bytes 524320 | tf_op jit(solution)/shard_map/ppermute | solution.py:383
  93.4 4.4 %collective-permute-start.18 = (bf16[256,1024]{1,0:T(8,128)(2,1)S(1)}, bf16[256,1024]{1,0:T(8,128)(2,1)S(1)}, u32[]{:S(2)}, u32[]{:S(2)}) collective-permute-start(bf16[256,1024]{1,0:T(8,128)(2,1)S(1)} %part.13), channel_id=1, source_target_pairs={{0,30},{2,0},{4,2},{6,4},{8,6},{10,8},{12,10},{14,12},{16,14},{18,... | collective-permute-start | bytes 1572872 | tf_op jit(solution)/shard_map/ppermute | solution.py:21
  97.8 0.5 part.8.refs_0_
  98.3 0.7 gradient.1
  99.1 15.0 %collective-permute-done.11.refs_3_ = bf16[1024,512]{1,0:T(8,128)(2,1)S(1)} collective-permute-done((bf16[1024,512]{1,0:T(8,128)(2,1)S(1)}, bf16[1024,512]{1,0:T(8,128)(2,1)S(1)}, u32[]{:S(2)}, u32[]{:S(2)}) %collective-permute-start.11) | collective-permute-done | bytes 1048608 | tf_op jit(solution)/shard_map/ppermute | solution.py:25
  114.0 3.1 %finish.1 = (bf16[1024,512]{1,0:T(8,128)(2,1)}, f32[1024,512]{1,0:T(8,128)}, f32[1024,512]{1,0:T(8,128)}) custom-call(f32[1024,512]{1,0:T(8,128)S(1)} %get-tuple-element.34.grad, bf16[1024,512]{1,0:T(8,128)(2,1)S(1)} %get-tuple-element.35.w, bf16[1024,512]{1,0:T(8,128)(2,1)S(1)} %collective-permute-done.8.refs_0_, ...), custom_call_target="tpu_custom_call" | custom-call | flops 15728640 | bytes 8388608 | tf_op jit(solution)/shard_map/finish/pallas_call | solution.py:301
  117.1 1.2 collect.1
  (30 shorter events, 0.4 us)
Async XLA Ops:
  0.6 6.8 %copy-start.3 = (bf16[512,512]{1,0:T(8,128)(2,1)S(1)}, bf16[512,512]{1,0:T(8,128)(2,1)}, u32[]{:S(2)}) copy-start(bf16[512,512]{1,0:T(8,128)(2,1)} %refs_1_.1) | copy-start | bytes 1572868
  0.6 23.0 %copy-start.2 = (f32[1,1024,512]{2,1,0:T(8,128)S(1)}, f32[1,1024,512]{2,1,0:T(8,128)}, u32[]{:S(2)}) copy-start(f32[1,1024,512]{2,1,0:T(8,128)} %param.9) | copy-start | bytes 6291460
  0.7 23.0 %copy-start.1 = (f32[1,1024,512]{2,1,0:T(8,128)S(1)}, f32[1,1024,512]{2,1,0:T(8,128)}, u32[]{:S(2)}) copy-start(f32[1,1024,512]{2,1,0:T(8,128)} %param.8) | copy-start | bytes 6291460
  0.7 23.0 %copy-start = (bf16[1,1024,512]{2,1,0:T(8,128)(2,1)S(1)}, bf16[1,1024,512]{2,1,0:T(8,128)(2,1)}, u32[]{:S(2)}) copy-start(bf16[1,1024,512]{2,1,0:T(8,128)(2,1)} %param.7) | copy-start | bytes 3145732
  1.9 12.5 %collective-permute-start = (bf16[512,512]{1,0:T(8,128)(2,1)S(1)}, bf16[512,512]{1,0:T(8,128)(2,1)S(1)}, u32[]{:S(2)}, u32[]{:S(2)}) collective-permute-start(bf16[512,512]{1,0:T(8,128)(2,1)S(1)} %cut.1), channel_id=1, source_target_pairs={{0,30},{2,4},{4,2},{6,8},{8,6},{10,12},{12,10},{14,16},{16,14},{18... | collective-permute-start | bytes 1572872 | tf_op jit(solution)/shard_map/ppermute | solution.py:25
  7.4 26.1 %collective-permute-start.5 = (bf16[512,1024]{1,0:T(8,128)(2,1)}, bf16[512,1024]{1,0:T(8,128)(2,1)S(1)}, u32[]{:S(2)}, u32[]{:S(2)}) collective-permute-start(bf16[512,1024]{1,0:T(8,128)(2,1)} %refs_0_.1), channel_id=1, source_target_pairs={{0,2},{2,0},{4,6},{6,4},{8,10},{10,8},{12,14},{14,12},{16,18},{18,... | collective-permute-start | bytes 3145736 | tf_op jit(solution)/shard_map/ppermute | solution.py:25
  7.4 20.2 %collective-permute-start.3 = (bf16[512,512]{1,0:T(8,128)(2,1)S(1)}, bf16[512,512]{1,0:T(8,128)(2,1)S(1)}, u32[]{:S(2)}, u32[]{:S(2)}) collective-permute-start(bf16[512,512]{1,0:T(8,128)(2,1)S(1)} %copy-done.3), channel_id=1, source_target_pairs={{0,30},{2,0},{4,2},{6,4},{8,6},{10,8},{12,10},{14,12},{16,14},{18,... | collective-permute-start | bytes 1572872 | tf_op jit(solution)/shard_map/ppermute | solution.py:21
  14.4 13.2 %collective-permute-start.1 = (bf16[512,512]{1,0:T(8,128)(2,1)S(1)}, bf16[512,512]{1,0:T(8,128)(2,1)S(1)}, u32[]{:S(2)}, u32[]{:S(2)}) collective-permute-start(bf16[512,512]{1,0:T(8,128)(2,1)S(1)} %collective-permute-done.refs_0_), channel_id=1, source_target_pairs={{0,1},{1,0},{2,3},{3,2},{4,5},{5,4},{6,7},{7,6},{8,9},{9,8},{10,11... | collective-permute-start | bytes 1572872 | tf_op jit(solution)/shard_map/ppermute | solution.py:21
  16.3 17.2 %collective-permute-start.6 = (bf16[512,512]{1,0:T(8,128)(2,1)S(1)}, bf16[512,512]{1,0:T(8,128)(2,1)S(1)}, u32[]{:S(2)}, u32[]{:S(2)}) collective-permute-start(bf16[512,512]{1,0:T(8,128)(2,1)S(1)} %copy-done.3), channel_id=1, source_target_pairs={{0,2},{2,0},{4,6},{6,4},{8,10},{10,8},{12,14},{14,12},{16,18},{18,... | collective-permute-start | bytes 1572872 | tf_op jit(solution)/shard_map/ppermute | solution.py:25
  27.7 38.8 %collective-permute-start.4 = (bf16[1024,512]{1,0:T(8,128)(2,1)S(1)}, bf16[1024,512]{1,0:T(8,128)(2,1)S(1)}, u32[]{:S(2)}, u32[]{:S(2)}) collective-permute-start(bf16[1024,512]{1,0:T(8,128)(2,1)S(1)} %get-tuple-element.28), channel_id=1, source_target_pairs={{0,2},{2,8},{4,6},{6,12},{8,10},{10,16},{12,14},{14,20},{16,18},{1... | collective-permute-start | bytes 3145736 | tf_op jit(solution)/shard_map/ppermute | solution.py:25
  36.5 35.2 %collective-permute-start.7 = (bf16[1024,512]{1,0:T(8,128)(2,1)S(1)}, bf16[1024,512]{1,0:T(8,128)(2,1)S(1)}, u32[]{:S(2)}, u32[]{:S(2)}) collective-permute-start(bf16[1024,512]{1,0:T(8,128)(2,1)S(1)} %get-tuple-element.31), channel_id=1, source_target_pairs={{0,6},{2,0},{4,10},{6,4},{8,14},{10,8},{12,18},{14,12},{16,22},{18... | collective-permute-start | bytes 3145736 | tf_op jit(solution)/shard_map/ppermute | solution.py:25
  36.6 29.9 %collective-permute-start.2 = (bf16[512,512]{1,0:T(8,128)(2,1)S(1)}, bf16[512,512]{1,0:T(8,128)(2,1)S(1)}, u32[]{:S(2)}, u32[]{:S(2)}) collective-permute-start(bf16[512,512]{1,0:T(8,128)(2,1)S(1)} %copy-done.3), channel_id=1, source_target_pairs={{0,2},{2,4},{4,6},{6,8},{8,10},{10,12},{12,14},{14,16},{16,18},{18... | collective-permute-start | bytes 1572872 | tf_op jit(solution)/shard_map/ppermute | solution.py:21
  37.1 35.8 %collective-permute-start.8 = (bf16[1024,512]{1,0:T(8,128)(2,1)S(1)}, bf16[1024,512]{1,0:T(8,128)(2,1)S(1)}, u32[]{:S(2)}, u32[]{:S(2)}) collective-permute-start(bf16[1024,512]{1,0:T(8,128)(2,1)S(1)} %get-tuple-element.36), channel_id=1, source_target_pairs={{0,6},{2,2},{4,0},{6,4},{8,14},{10,10},{12,8},{14,12},{16,22},{18,... | collective-permute-start | bytes 3145736 | tf_op jit(solution)/shard_map/ppermute | solution.py:25
  41.8 31.0 %collective-permute-start.14 = (bf16[256,1024]{1,0:T(8,128)(2,1)S(1)}, bf16[256,1024]{1,0:T(8,128)(2,1)S(1)}, u32[]{:S(2)}, u32[]{:S(2)}) collective-permute-start(bf16[256,1024]{1,0:T(8,128)(2,1)S(1)} %part.9), channel_id=1, source_target_pairs={{0,1},{1,0},{2,3},{3,2},{4,5},{5,4},{6,7},{7,6},{8,9},{9,8},{10,11... | collective-permute-start | bytes 1572872 | tf_op jit(solution)/shard_map/ppermute | solution.py:383
  68.3 14.0 %collective-permute-start.16 = (bf16[256,1024]{1,0:T(8,128)(2,1)S(1)}, bf16[256,1024]{1,0:T(8,128)(2,1)S(1)}, u32[]{:S(2)}, u32[]{:S(2)}) collective-permute-start(bf16[256,1024]{1,0:T(8,128)(2,1)S(1)} %part.11), channel_id=1, source_target_pairs={{0,1},{1,0},{4,5},{5,4},{8,9},{9,8},{12,13},{13,12},{16,17},{17,16... | collective-permute-start | bytes 1572872 | tf_op jit(solution)/shard_map/ppermute | solution.py:383
  72.0 12.1 %collective-permute-start.17 = (bf16[256,1024]{1,0:T(8,128)(2,1)S(1)}, bf16[256,1024]{1,0:T(8,128)(2,1)S(1)}, u32[]{:S(2)}, u32[]{:S(2)}) collective-permute-start(bf16[256,1024]{1,0:T(8,128)(2,1)S(1)} %part.12), channel_id=1, source_target_pairs={{2,3},{3,2},{6,7},{7,6},{10,11},{11,10},{14,15},{15,14},{18,19},{1... | collective-permute-start | bytes 1572872 | tf_op jit(solution)/shard_map/ppermute | solution.py:383
  72.7 20.7 %collective-permute-start.10 = (bf16[1024,512]{1,0:T(8,128)(2,1)S(1)}, bf16[1024,512]{1,0:T(8,128)(2,1)S(1)}, u32[]{:S(2)}, u32[]{:S(2)}) collective-permute-start(bf16[1024,512]{1,0:T(8,128)(2,1)S(1)} %get-tuple-element.38), channel_id=1, source_target_pairs={{0,2},{2,8},{4,6},{6,12},{8,10},{10,16},{12,14},{14,20},{16,18},{1... | collective-permute-start | bytes 3145736 | tf_op jit(solution)/shard_map/ppermute | solution.py:25
  72.8 41.3 %collective-permute-start.11 = (bf16[1024,512]{1,0:T(8,128)(2,1)S(1)}, bf16[1024,512]{1,0:T(8,128)(2,1)S(1)}, u32[]{:S(2)}, u32[]{:S(2)}) collective-permute-start(bf16[1024,512]{1,0:T(8,128)(2,1)S(1)} %get-tuple-element.39), channel_id=1, source_target_pairs={{0,2},{2,8},{4,6},{6,12},{8,10},{10,16},{12,14},{14,20},{16,18},{1... | collective-permute-start | bytes 3145736 | tf_op jit(solution)/shard_map/ppermute | solution.py:25
  72.8 41.2 %collective-permute-start.9 = (bf16[1024,512]{1,0:T(8,128)(2,1)S(1)}, bf16[1024,512]{1,0:T(8,128)(2,1)S(1)}, u32[]{:S(2)}, u32[]{:S(2)}) collective-permute-start(bf16[1024,512]{1,0:T(8,128)(2,1)S(1)} %get-tuple-element.37), channel_id=1, source_target_pairs={{0,6},{2,0},{4,10},{6,4},{8,14},{10,8},{12,18},{14,12},{16,22},{18... | collective-permute-start | bytes 3145736 | tf_op jit(solution)/shard_map/ppermute | solution.py:25
  82.3 31.7 %collective-permute-start.12 = (bf16[1024,512]{1,0:T(8,128)(2,1)S(1)}, bf16[1024,512]{1,0:T(8,128)(2,1)S(1)}, u32[]{:S(2)}, u32[]{:S(2)}) collective-permute-start(bf16[1024,512]{1,0:T(8,128)(2,1)S(1)} %collective-permute-done.8.refs_0_), channel_id=1, source_target_pairs={{0,10},{8,18},{16,26},{24,2},{1,11},{9,19},{17,27},{25,3}} | collective-permute-start | bytes 3145736 | tf_op jit(solution)/shard_map/ppermute | solution.py:25
  84.1 9.2 %collective-permute-start.13 = (bf16[256,1024]{1,0:T(8,128)(2,1)S(1)}, bf16[256,1024]{1,0:T(8,128)(2,1)S(1)}, u32[]{:S(2)}, u32[]{:S(2)}) collective-permute-start(bf16[256,1024]{1,0:T(8,128)(2,1)S(1)} %part.7), channel_id=1, source_target_pairs={{0,1},{1,0},{2,3},{3,2},{4,5},{5,4},{6,7},{7,6},{8,9},{9,8},{10,11... | collective-permute-start | bytes 1572872 | tf_op jit(solution)/shard_map/ppermute | solution.py:383
  93.4 23.7 %collective-permute-start.15 = (bf16[256,1024]{1,0:T(8,128)(2,1)S(1)}, bf16[256,1024]{1,0:T(8,128)(2,1)S(1)}, u32[]{:S(2)}, u32[]{:S(2)}) collective-permute-start(bf16[256,1024]{1,0:T(8,128)(2,1)S(1)} %part.10), channel_id=1, source_target_pairs={{0,2},{2,4},{4,6},{6,8},{8,10},{10,12},{12,14},{14,16},{16,18},{18... | collective-permute-start | bytes 1572872 | tf_op jit(solution)/shard_map/ppermute | solution.py:21
  93.4 23.7 %collective-permute-start.18 = (bf16[256,1024]{1,0:T(8,128)(2,1)S(1)}, bf16[256,1024]{1,0:T(8,128)(2,1)S(1)}, u32[]{:S(2)}, u32[]{:S(2)}) collective-permute-start(bf16[256,1024]{1,0:T(8,128)(2,1)S(1)} %part.13), channel_id=1, source_target_pairs={{0,30},{2,0},{4,2},{6,4},{8,6},{10,8},{12,10},{14,12},{16,14},{18,... | collective-permute-start | bytes 1572872 | tf_op jit(solution)/shard_map/ppermute | solution.py:21
